TPU v7x, 32 devices: a whole 2x2x4 slice. The times are simulated.
32 devices in a mesh: dp: 4 (over z), seq: 4 (over x, core), tensor: 2 (over y).
Axes of the slice: x: 2, y: 2, z: 4, core: 2. Of those that a mesh axis runs over, the one named last changes fastest.
Arguments:
- latent_embed: bfloat16 [20480, 2, 1024], P(('dp', 'seq'), None, 'tensor'), may hold values from -6 to 6
- adapter: bfloat16 [2, 1024, 1024], P(None, 'tensor'), may hold values from -0.125 to 0.125
- first_gain: float32 [1024], replicated, may hold values from 0.5 to 1.5
- query_weight: bfloat16 [1024, 1024], P(None, 'tensor'), may hold values from -0.1875 to 0.1875
- key_weight: bfloat16 [1024, 1024], P(None, 'tensor'), may hold values from -0.1875 to 0.1875
- value_weight: bfloat16 [1024, 1024], P(None, 'tensor'), may hold values from -0.1875 to 0.1875
- output_weight: bfloat16 [1024, 1024], P('tensor'), may hold values from -0.1875 to 0.1875
- second_gain: float32 [1024], replicated, may hold values from 0.5 to 1.5
- third_gain: float32 [1024], replicated, may hold values from 0.5 to 1.5
- gate_weight: bfloat16 [1024, 2816], P(None, 'tensor'), may hold values from -0.1875 to 0.1875
- up_weight: bfloat16 [1024, 2816], P(None, 'tensor'), may hold values from -0.1875 to 0.1875
- down_weight: bfloat16 [2816, 1024], P('tensor'), may hold values from -0.109375 to 0.109375
- fourth_gain: float32 [1024], replicated, may hold values from 0.5 to 1.5
- parents: int32 [4, 20], P('dp'), may hold values from -1 to 19, as said below
- positions: int32 [20480], P(('dp', 'seq')), may hold values from 0 to 2559, as said below
- cotangent: bfloat16 [20480, 1024], P(('dp', 'seq')), may hold values from -6 to 6
Outputs:
- layer_out: float32 [20480, 1024], P(('dp', 'seq'))
- latent_gradient: float32 [20480, 2, 1024], P(('dp', 'seq'), None, 'tensor')
- adapter_gradient: float32 [2, 1024, 1024], P(None, 'tensor')
- first_gain_gradient: float32 [1024], replicated
- query_gradient: float32 [1024, 1024], P(None, 'tensor')
- key_gradient: float32 [1024, 1024], P(None, 'tensor')
- value_gradient: float32 [1024, 1024], P(None, 'tensor')
- output_gradient: float32 [1024, 1024], P('tensor')
- second_gain_gradient: float32 [1024], replicated
- third_gain_gradient: float32 [1024], replicated
- gate_gradient: float32 [1024, 2816], P(None, 'tensor')
- up_gradient: float32 [1024, 2816], P(None, 'tensor')
- down_gradient: float32 [2816, 1024], P('tensor')
- fourth_gain_gradient: float32 [1024], replicated
Inputs may be any that keep to these rules, and one draw needn't show every extreme that they name: `parents`: each tree's segments form a trunk of 8 chained segments from the root, 4 branches whose parent is the trunk's last segment and 2 leaves under each branch; which segment number plays which role is drawn. `positions`: a token's position is 256 times the number of its segment's ancestors plus its place inside its segment.
All inputs are finite; a program needn't handle non-finite values.
Results may differ from a plain program's by a relative error of at most 0.025.
Values may be sent and summed in bfloat16 or wider, within the bound.
A program may use at most 896 MiB of HBM per device.

v0:
```python
import jax
import jax.numpy as jnp
from jax import lax
from jax.sharding import PartitionSpec as P

DH = 64
SEG = 256


EPSILON = 1e-06
THETA = 50000.0


def normalize(values, gain):
    scale = lax.rsqrt(jnp.mean(values * values, axis=-1, keepdims=True) + EPSILON)
    normed = values * scale
    return (normed * gain, normed, scale)


def normalize_back(upstream, gain, normed, scale):
    scaled = upstream * gain
    inward = scale * (scaled - normed * jnp.mean(scaled * normed, axis=-1, keepdims=True))
    return (inward, jnp.sum(upstream * normed, axis=0))


def angles(positions, width):
    half = width // 2
    freq = THETA ** (-jnp.arange(half, dtype=jnp.float32) * 2.0 / width)
    angle = positions.astype(jnp.float32)[:, None] * freq[None, :]
    return (jnp.cos(angle)[:, None, :], jnp.sin(angle)[:, None, :])


def rotate(values, cosine, sine, sign):
    half = values.shape[-1] // 2
    first = values[..., :half]
    second = values[..., half:]
    return jnp.concatenate(
        [first * cosine - sign * second * sine, second * cosine + sign * first * sine], axis=-1
    )


def ancestry(parent_row):
    labels = jnp.arange(parent_row.shape[0], dtype=jnp.int32)

    def extend(index, state):
        current, total = state
        total = total | (current[:, None] == labels[None, :])
        current = jnp.where(current >= 0, jnp.take(parent_row, jnp.maximum(current, 0)), -1)
        return (current, total)

    start = (parent_row, jnp.zeros((parent_row.shape[0], parent_row.shape[0]), jnp.bool_))
    current, total = lax.fori_loop(0, parent_row.shape[0], extend, start)
    return total


def path_mask(parent_row, query_ids, key_ids):
    table = ancestry(parent_row)
    query_seg = query_ids // SEG
    key_seg = key_ids // SEG
    far = jnp.take(jnp.take(table, query_seg, axis=0), key_seg, axis=1)
    near = (query_seg[:, None] == key_seg[None, :]) & (key_ids[None, :] <= query_ids[:, None])
    return far | near


def on_device(
    latent_embed,
    adapter,
    first_gain,
    query_weight,
    key_weight,
    value_weight,
    output_weight,
    second_gain,
    third_gain,
    gate_weight,
    up_weight,
    down_weight,
    fourth_gain,
    parents,
    positions,
    cotangent,
):
    rows = latent_embed.shape[0]
    local_heads = query_weight.shape[1] // DH
    scale = DH ** (-0.5)
    adapted = lax.psum(
        jnp.einsum("rcd,cde->re", latent_embed, adapter, preferred_element_type=jnp.float32),
        "tensor",
    )
    first_out, first_normed, first_scale = normalize(adapted, first_gain)
    first_low = first_out.astype(jnp.bfloat16)
    cosine, sine = angles(positions, DH)
    query_raw = jnp.dot(first_low, query_weight, preferred_element_type=jnp.float32).reshape(
        rows, local_heads, DH
    )
    queries = rotate(query_raw, cosine, sine, 1.0).astype(jnp.bfloat16)
    key_raw = jnp.dot(first_low, key_weight, preferred_element_type=jnp.float32).reshape(
        rows, local_heads, DH
    )
    keys_local = rotate(key_raw, cosine, sine, 1.0).astype(jnp.bfloat16)
    values_local = (
        jnp.dot(first_low, value_weight, preferred_element_type=jnp.float32)
        .astype(jnp.bfloat16)
        .reshape(rows, local_heads, DH)
    )
    keys_all, values_all = (
        lax.all_gather(keys_local, "seq", axis=0, tiled=True),
        lax.all_gather(values_local, "seq", axis=0, tiled=True),
    )
    tree_rows = keys_all.shape[0]
    query_ids = lax.axis_index("seq") * rows + jnp.arange(rows, dtype=jnp.int32)
    key_ids = jnp.arange(tree_rows, dtype=jnp.int32)
    allowed = path_mask(parents[0], query_ids, key_ids)[None]

    def score_block(keys):
        raw = jnp.einsum("qhd,khd->hqk", queries, keys, preferred_element_type=jnp.float32) * scale
        return jnp.where(allowed, raw, -1e30)

    scores = score_block(keys_all)
    top = jnp.max(scores, axis=-1, keepdims=True)
    weights = jnp.exp(scores - top)
    total = jnp.sum(weights, axis=-1, keepdims=True)
    probs = weights / total
    logsum = top + jnp.log(total)
    attended = jnp.einsum(
        "hqk,khd->qhd", probs.astype(jnp.bfloat16), values_all, preferred_element_type=jnp.float32
    )
    attended = attended.reshape(rows, local_heads * DH).astype(jnp.bfloat16)
    attention = lax.psum(
        jnp.dot(attended, output_weight, preferred_element_type=jnp.float32).astype(jnp.bfloat16),
        "tensor",
    ).astype(jnp.float32)
    second_out, second_normed, second_scale = normalize(attention, second_gain)
    middle = adapted + second_out
    third_out, third_normed, third_scale = normalize(middle, third_gain)
    third_low = third_out.astype(jnp.bfloat16)
    gate = jnp.dot(third_low, gate_weight, preferred_element_type=jnp.float32)
    upward = jnp.dot(third_low, up_weight, preferred_element_type=jnp.float32)
    hidden = (jax.nn.silu(gate) * upward).astype(jnp.bfloat16)
    mixed = lax.psum(
        jnp.dot(hidden, down_weight, preferred_element_type=jnp.float32).astype(jnp.bfloat16),
        "tensor",
    ).astype(jnp.float32)
    fourth_out, fourth_normed, fourth_scale = normalize(mixed, fourth_gain)
    layer_out = middle + fourth_out
    upstream = cotangent.astype(jnp.float32)
    mixed_back, fourth_gain_part = normalize_back(
        upstream, fourth_gain, fourth_normed, fourth_scale
    )
    mixed_low = mixed_back.astype(jnp.bfloat16)
    down_part = jnp.einsum("rf,rd->fd", hidden, mixed_low, preferred_element_type=jnp.float32)
    hidden_back = (
        jnp.einsum("rd,fd->rf", mixed_low, down_weight, preferred_element_type=jnp.float32)
        .astype(jnp.bfloat16)
        .astype(jnp.float32)
    )
    swiglu_value, product_back = jax.vjp(
        lambda left, right: jax.nn.silu(left) * right, gate, upward
    )
    gate_back, up_back = product_back(hidden_back)
    gate_low = gate_back.astype(jnp.bfloat16)
    up_low = up_back.astype(jnp.bfloat16)
    gate_part = jnp.einsum("rd,rf->df", third_low, gate_low, preferred_element_type=jnp.float32)
    up_part = jnp.einsum("rd,rf->df", third_low, up_low, preferred_element_type=jnp.float32)
    third_term = jnp.einsum(
        "rf,df->rd", gate_low, gate_weight, preferred_element_type=jnp.float32
    ) + jnp.einsum("rf,df->rd", up_low, up_weight, preferred_element_type=jnp.float32)
    third_back = lax.psum(third_term.astype(jnp.bfloat16), "tensor").astype(jnp.float32)
    middle_part, third_gain_part = normalize_back(third_back, third_gain, third_normed, third_scale)
    middle_back = upstream + middle_part
    attention_back, second_gain_part = normalize_back(
        middle_back, second_gain, second_normed, second_scale
    )
    attention_low = attention_back.astype(jnp.bfloat16)
    output_part = jnp.einsum(
        "re,rd->ed", attended, attention_low, preferred_element_type=jnp.float32
    )
    attended_back = (
        jnp.einsum("rd,ed->re", attention_low, output_weight, preferred_element_type=jnp.float32)
        .astype(jnp.bfloat16)
        .reshape(rows, local_heads, DH)
    )
    keys_back, values_back = (
        lax.all_gather(keys_local, "seq", axis=0, tiled=True),
        lax.all_gather(values_local, "seq", axis=0, tiled=True),
    )
    probs_back = jnp.exp(score_block(keys_back) - logsum)
    prob_grad = jnp.einsum(
        "qhd,khd->hqk", attended_back, values_back, preferred_element_type=jnp.float32
    )
    score_grad = (
        probs_back * (prob_grad - jnp.sum(prob_grad * probs_back, axis=-1, keepdims=True))
    ).astype(jnp.bfloat16)
    query_rot = (
        jnp.einsum("hqk,khd->qhd", score_grad, keys_back, preferred_element_type=jnp.float32)
        * scale
    )
    key_rot_all = (
        jnp.einsum("hqk,qhd->khd", score_grad, queries, preferred_element_type=jnp.float32) * scale
    )
    value_back_all = jnp.einsum(
        "hqk,qhd->khd",
        probs_back.astype(jnp.bfloat16),
        attended_back,
        preferred_element_type=jnp.float32,
    )
    key_rot, value_back = (
        lax.psum_scatter(
            key_rot_all.astype(jnp.bfloat16), "seq", scatter_dimension=0, tiled=True
        ).astype(jnp.float32),
        lax.psum_scatter(
            value_back_all.astype(jnp.bfloat16), "seq", scatter_dimension=0, tiled=True
        ).astype(jnp.float32),
    )
    query_low = (
        rotate(query_rot, cosine, sine, -1.0).astype(jnp.bfloat16).reshape(rows, local_heads * DH)
    )
    key_low = (
        rotate(key_rot, cosine, sine, -1.0).astype(jnp.bfloat16).reshape(rows, local_heads * DH)
    )
    value_low = value_back.astype(jnp.bfloat16).reshape(rows, local_heads * DH)
    query_part = jnp.einsum("rd,re->de", first_low, query_low, preferred_element_type=jnp.float32)
    key_part = jnp.einsum("rd,re->de", first_low, key_low, preferred_element_type=jnp.float32)
    value_part = jnp.einsum("rd,re->de", first_low, value_low, preferred_element_type=jnp.float32)
    first_term = jnp.einsum(
        "re,de->rd", query_low, query_weight, preferred_element_type=jnp.float32
    )
    first_term = first_term + jnp.einsum(
        "re,de->rd", key_low, key_weight, preferred_element_type=jnp.float32
    )
    first_term = first_term + jnp.einsum(
        "re,de->rd", value_low, value_weight, preferred_element_type=jnp.float32
    )
    first_back = lax.psum(first_term.astype(jnp.bfloat16), "tensor").astype(jnp.float32)
    adapted_part, first_gain_part = normalize_back(
        first_back, first_gain, first_normed, first_scale
    )
    adapted_low = (middle_back + adapted_part).astype(jnp.bfloat16)
    latent_gradient = jnp.einsum(
        "re,cde->rcd", adapted_low, adapter, preferred_element_type=jnp.float32
    )
    adapter_part = jnp.einsum(
        "rcd,re->cde", latent_embed, adapted_low, preferred_element_type=jnp.float32
    )
    summed = (
        lax.psum(gate_part.astype(jnp.bfloat16), ("dp", "seq")).astype(jnp.float32),
        lax.psum(up_part.astype(jnp.bfloat16), ("dp", "seq")).astype(jnp.float32),
        lax.psum(down_part.astype(jnp.bfloat16), ("dp", "seq")).astype(jnp.float32),
        lax.psum(third_gain_part.astype(jnp.bfloat16), ("dp", "seq")).astype(jnp.float32),
        lax.psum(fourth_gain_part.astype(jnp.bfloat16), ("dp", "seq")).astype(jnp.float32),
        lax.psum(query_part.astype(jnp.bfloat16), ("dp", "seq")).astype(jnp.float32),
        lax.psum(key_part.astype(jnp.bfloat16), ("dp", "seq")).astype(jnp.float32),
        lax.psum(value_part.astype(jnp.bfloat16), ("dp", "seq")).astype(jnp.float32),
        lax.psum(output_part.astype(jnp.bfloat16), ("dp", "seq")).astype(jnp.float32),
        lax.psum(first_gain_part.astype(jnp.bfloat16), ("dp", "seq")).astype(jnp.float32),
        lax.psum(second_gain_part.astype(jnp.bfloat16), ("dp", "seq")).astype(jnp.float32),
        lax.psum(adapter_part.astype(jnp.bfloat16), ("dp", "seq")).astype(jnp.float32),
    )
    gate_total, up_total, down_total, third_total, fourth_total = (
        summed[0],
        summed[1],
        summed[2],
        summed[3],
        summed[4],
    )
    query_total, key_total, value_total, output_total, first_total, second_total = (
        summed[5],
        summed[6],
        summed[7],
        summed[8],
        summed[9],
        summed[10],
    )
    adapter_total = summed[11]
    return (
        layer_out,
        latent_gradient,
        adapter_total,
        first_total,
        query_total,
        key_total,
        value_total,
        output_total,
        second_total,
        third_total,
        gate_total,
        up_total,
        down_total,
        fourth_total,
    )


def solution(mesh):
    in_specs = (
        P(("dp", "seq"), None, "tensor"),
        P(None, "tensor", None),
        P(),
        P(None, "tensor"),
        P(None, "tensor"),
        P(None, "tensor"),
        P("tensor", None),
        P(),
        P(),
        P(None, "tensor"),
        P(None, "tensor"),
        P("tensor", None),
        P(),
        P("dp", None),
        P(("dp", "seq")),
        P(("dp", "seq"), None),
    )
    out_specs = (
        P(("dp", "seq"), None),
        P(("dp", "seq"), None, "tensor"),
        P(None, "tensor", None),
        P(),
        P(None, "tensor"),
        P(None, "tensor"),
        P(None, "tensor"),
        P("tensor", None),
        P(),
        P(),
        P(None, "tensor"),
        P(None, "tensor"),
        P("tensor", None),
        P(),
    )
    return jax.shard_map(
        on_device, mesh=mesh, in_specs=in_specs, out_specs=out_specs, check_vma=False
    )
```

profile of v0, /device:TPU:0, one launch (start us, length us, event | category | flops | bytes accessed | tf_op | source)
XLA Modules:
  0.0 1609.5 jit_solution(6540593411886035098)
XLA Ops:
  17.1 131.4 %all-reduce.9.cloned.1.call-done = f32[1280,1024]{1,0:T(8,128)} async-done(((f32[1280,1024]{1,0:T(8,128)}), f32[1280,1024]{1,0:T(8,128)}) %all-reduce.9.cloned.1.call-update) | async-done | bytes 5242896 | tf_op jit(solution)/shard_map/psum | solution.py:86
  160.6 16.5 %while.13 = (s32[]{:T(128)}, s32[20]{0:T(128)S(1)}, pred[20,20]{1,0:T(8,128)(4,1)S(1)}, s32[20]{0:T(128)S(1)}, s32[]{:T(128)}, /*index=5*/s32[]{:T(128)}) while((s32[]{:T(128)}, s32[20]{0:T(128)S(1)}, pred[20,20]{1,0:T(8,128)(4,1)S(1)}, s32[20]{0:T(128)S(1)}, s32[]{:T(128)}, /*index=5*/s32[]{:T(128)}) %tuple.77), condition=%wide.region_3.0_spmd.clone, body=%wide.region_2.3_spmd.clone.sunk | while | flops 2347 | bytes 5775 | solution.py:52
  180.3 22.2 %gather_fusion.2 = pred[5120,1280]{1,0:T(8,128)(4,1)} fusion(pred[1280,20]{0,1:T(8,128)(4,1)S(1)} %copy.38, s32[5120]{0:T(1024)S(1)} %broadcast_clamp_fusion), kind=kCustom, calls=%fused_computation.2 | custom fusion | bytes 13127680 | tf_op jit(solution)/shard_map/jit(_take)/gather | solution.py:60
  202.5 11.1 fusion.10
  213.6 16.6 %copy.39 = pred[1280,5120]{1,0:T(8,128)(4,1)} copy(pred[1280,5120]{0,1:T(8,128)(4,1)} %fusion.10) | data formatting | bytes 13107200 | tf_op jit(solution)/shard_map/or | solution.py:62
  235.0 74.7 %fusion.76 = (f32[8,1280]{1,0:T(8,128)}, f32[8,1280,5120]{2,1,0:T(8,128)}) fusion(bf16[5120,8,64]{0,2,1:T(8,128)(2,1)} %all-gather.5.cloned.1.call-done, bf16[1280,8,32]{0,2,1:T(8,128)(2,1)} %get-tuple-element.126, bf16[1280,8,32]{0,2,1:T(8,128)(2,1)S(1)} %copy-done.20, pred[1280,5120]{1,0:T(8,128)(4,1)} %copy.39), kind=kOutput, calls=%fused_computation.170 | convolution fusion | flops 6870784000 | bytes 222863360 | tf_op jit(solution)/shard_map/qhd,khd->hqk/dot_general | solution.py:116
  309.7 63.5 %fusion.3 = f32[8,1280]{1,0:T(8,128)S(1)} fusion(f32[8,1280,5120]{2,1,0:T(8,128)} %get-tuple-element.137, f32[8,1280]{1,0:T(8,128)} %get-tuple-element.136), kind=kLoop, calls=%fused_computation.16 | loop fusion | flops 104847360 | bytes 209797120 | tf_op jit(solution)/shard_map/reduce_sum | solution.py:122
  373.2 68.2 %fusion.56 = bf16[8,64,1280]{2,1,0:T(8,128)(2,1)} fusion(bf16[5120,8,64]{0,2,1:T(8,128)(2,1)} %all-gather.3.cloned.1.call-done, f32[8,1280,5120]{2,1,0:T(8,128)} %get-tuple-element.137, f32[8,1280]{1,0:T(8,128)S(1)} %fusion.3, f32[8,1280]{1,0:T(8,128)S(1)} %copy-done.43), kind=kOutput, calls=%fused_computation.97 | convolution fusion | flops 6868828160 | bytes 216350720 | tf_op jit(solution)/shard_map/hqk,khd->qhd/dot_general | solution.py:125
  446.4 74.6 %all-reduce.11.cloned.1.call-done = bf16[1280,1024]{1,0:T(8,128)(2,1)} async-done(((bf16[1280,1024]{1,0:T(8,128)(2,1)}), bf16[1280,1024]{1,0:T(8,128)(2,1)}) %all-reduce.11.cloned.1.call-update) | async-done | bytes 2621456 | tf_op jit(solution)/shard_map/psum | solution.py:129
  549.9 74.0 %all-reduce.13.cloned.1.call-done = bf16[1280,1024]{1,0:T(8,128)(2,1)} async-done(((bf16[1280,1024]{1,0:T(8,128)(2,1)}), bf16[1280,1024]{1,0:T(8,128)(2,1)}) %all-reduce.13.cloned.1.call-update) | async-done | bytes 2621456 | tf_op jit(solution)/shard_map/psum | solution.py:140
  630.7 11.4 fusion.14
  652.2 8.8 convolution_convert_fusion.3
  667.1 59.6 %all-reduce.15.cloned.1.call-done = bf16[1280,1024]{1,0:T(8,128)(2,1)} async-done(((bf16[1280,1024]{1,0:T(8,128)(2,1)}), bf16[1280,1024]{1,0:T(8,128)(2,1)}) %all-reduce.15.cloned.1.call-update) | async-done | bytes 2621456 | tf_op jit(solution)/shard_map/psum | solution.py:168
  732.2 8.5 fusion.47
  744.7 138.2 %multiply_reduce_fusion = (f32[8,1280]{1,0:T(8,128)S(1)}, f32[8,1280,5120]{2,1,0:T(8,128)}) fusion(f32[8,1280,5120]{2,1,0:T(8,128)} %get-tuple-element.137, f32[8,1280]{1,0:T(8,128)S(1)} %log_add_fusion, bf16[1280,8,64]{0,2,1:T(8,128)(2,1)S(1)} %bitcast.82, bf16[5120,8,64]{0,2,1:T(8,128)(2,1)} %all-gather.3.cloned.1.call-done), kind=kOutput, calls=%fused_computation.11 | convolution fusion | flops 6868162560 | bytes 426065920 | tf_op jit(solution)/shard_map/qhd,khd->hqk/dot_general | solution.py:188
  882.9 160.8 %multiply_convert_fusion = bf16[8,1280,5120]{2,1,0:T(8,128)(2,1)} fusion(f32[8,1280,5120]{2,1,0:T(8,128)} %get-tuple-element.141, f32[8,1280,5120]{2,1,0:T(8,128)} %get-tuple-element.137, f32[8,1280]{1,0:T(8,128)S(1)} %get-tuple-element.140, f32[8,1280]{1,0:T(8,128)S(1)} %log_add_fusion), kind=kLoop, calls=%fused_computation.10 | loop fusion | flops 209715200 | bytes 524369920 | tf_op jit(solution)/shard_map/convert_element_type | solution.py:193
  1043.7 37.6 %fusion.55 = bf16[5120,8,64]{0,2,1:T(8,128)(2,1)} fusion(bf16[8,1280,5120]{2,1,0:T(8,128)(2,1)} %multiply_convert_fusion, bf16[1280,8,32]{0,2,1:T(8,128)(2,1)S(1)} %copy-done.22, bf16[1280,8,32]{0,2,1:T(8,128)(2,1)S(1)} %copy-done.21), kind=kOutput, calls=%fused_computation.82 | convolution fusion | flops 6718750720 | bytes 111411200 | tf_op jit(solution)/shard_map/hqk,qhd->khd/dot_general | solution.py:199
  1082.6 71.0 %fusion.19 = bf16[5120,8,64]{0,2,1:T(8,128)(2,1)} fusion(bf16[1280,8,64]{0,2,1:T(8,128)(2,1)S(1)} %bitcast.83, f32[8,1280,5120]{2,1,0:T(8,128)} %get-tuple-element.137, f32[8,1280]{1,0:T(8,128)S(1)} %log_add_fusion), kind=kOutput, calls=%fused_computation.40 | convolution fusion | flops 6818365440 | bytes 216309760 | tf_op jit(solution)/shard_map/hqk,qhd->khd/dot_general | solution.py:201
  1153.6 44.4 %multiply_bitcast_fusion = f32[1280,8,64]{0,2,1:T(8,128)S(1)} fusion(bf16[5120,8,64]{0,2,1:T(8,128)(2,1)} %all-gather.5.cloned.1.call-done, bf16[8,1280,5120]{2,1,0:T(8,128)(2,1)} %multiply_convert_fusion), kind=kOutput, calls=%fused_computation.99 | convolution fusion | flops 6711541760 | bytes 112721920 | tf_op jit(solution)/shard_map/hqk,khd->qhd/dot_general | solution.py:195
  1218.0 8.0 convolution_convert_fusion.4
  1236.2 56.2 %all-reduce.17.cloned.1.call-done = bf16[1280,1024]{1,0:T(8,128)(2,1)} async-done(((bf16[1280,1024]{1,0:T(8,128)(2,1)}), bf16[1280,1024]{1,0:T(8,128)(2,1)}) %all-reduce.17.cloned.1.call-update) | async-done | bytes 2621456 | tf_op jit(solution)/shard_map/psum | solution.py:234
  1308.8 36.3 %all-reduce = (bf16[1024]{0:T(1024)(128)(2,1)S(1)}, bf16[1024]{0:T(1024)(128)(2,1)S(1)}, bf16[1024]{0:T(1024)(128)(2,1)S(1)}, bf16[1024]{0:T(1024)(128)(2,1)S(1)}) all-reduce(bf16[1024]{0:T(1024)(128)(2,1)S(1)} %get-tuple-element.91, bf16[1024]{0:T(1024)(128)(2,1)S(1)} %copy-done.52, ...), channel_id=1, replica_groups=mesh['dp'=4,'seq'=4,'tensor'=2] {'dp','seq'}, use_global_device_ids=true, to_apply=%region_22.23 | all-reduce | flops 4096 | bytes 16384 | tf_op jit(solution)/shard_map/psum | solution.py:255
  1352.0 10.7 copy.42
  1362.7 219.9 %all-reduce.19.cloned.1.call-done = (bf16[2,512,1024]{1,2,0:T(8,128)(2,1)}, bf16[1024,512]{1,0:T(8,128)(2,1)}, bf16[1024,512]{1,0:T(8,128)(2,1)}, bf16[1024,512]...) async-done(((bf16[2,512,1024]{1,2,0:T(8,128)(2,1)}, ...) | async-done | bytes 14942224 | tf_op jit(solution)/shard_map/psum | solution.py:257
  (341 shorter events, 186.5 us)
Async XLA Ops:
  7.2 536.7 %copy-start = (bf16[1408,1024]{1,0:T(8,128)(2,1)S(1)}, bf16[1408,1024]{1,0:T(8,128)(2,1)}, u32[]{:S(2)}) copy-start(bf16[1408,1024]{1,0:T(8,128)(2,1)} %param.29) | copy-start | bytes 8650756
  7.2 141.2 %all-reduce.9.cloned.1.call-start = ((), (), s32[]{:S(2)}) async-start(), calls=%async_computation.2 | async-start | bytes 10485760 | tf_op jit(solution)/shard_map/psum | solution.py:86
  15.0 136.5 %copy-start.48 = (f32[1024]{0:T(1024)S(1)}, f32[1024]{0:T(1024)}, u32[]{:S(2)}) copy-start(f32[1024]{0:T(1024)} %param.20) | copy-start | bytes 12292
  15.1 219.9 %all-gather.5.cloned.1.call-start = ((), (), s32[]{:S(2)}) async-start(), calls=%async_computation.4 | async-start | bytes 6553600 | tf_op jit(solution)/shard_map/all_gather | solution.py:107
  17.1 140.3 %copy-start.31 = (f32[1280,32]{0,1:T(8,128)}, f32[1280,32]{0,1:T(8,128)S(1)}, u32[]{:S(2)}) copy-start(f32[1280,32]{0,1:T(8,128)S(1)} %get-tuple-element.135) | copy-start | bytes 491524
  160.4 212.8 %all-gather.3.cloned.1.call-start = ((), (), s32[]{:S(2)}) async-start(), calls=%async_computation.3 | async-start | bytes 6553600 | tf_op jit(solution)/shard_map/all_gather | solution.py:108
  234.9 286.1 %all-reduce.11.cloned.1.call-start = ((), (), s32[]{:S(2)}) async-start(), calls=%async_computation.5 | async-start | bytes 5242880 | tf_op jit(solution)/shard_map/psum | solution.py:129
  309.7 63.5 %copy-start.43 = (f32[8,1280]{1,0:T(8,128)S(1)}, f32[8,1280]{1,0:T(8,128)}, u32[]{:S(2)}) copy-start(f32[8,1280]{1,0:T(8,128)} %get-tuple-element.136) | copy-start | bytes 122884
  446.1 77.4 %copy-start.47 = (f32[1024]{0:T(1024)S(1)}, f32[1024]{0:T(1024)}, u32[]{:S(2)}) copy-start(f32[1024]{0:T(1024)} %param.25) | copy-start | bytes 12292
  446.1 177.8 %all-reduce.13.cloned.1.call-start = ((), (), s32[]{:S(2)}) async-start(), calls=%async_computation.6 | async-start | bytes 5242880 | tf_op jit(solution)/shard_map/psum | solution.py:140
  549.4 77.0 %copy-start.50 = (f32[1024]{0:T(1024)S(1)}, f32[1024]{0:T(1024)}, u32[]{:S(2)}) copy-start(f32[1024]{0:T(1024)} %param.30) | copy-start | bytes 12292
  549.4 177.2 %all-reduce.15.cloned.1.call-start = ((), (), s32[]{:S(2)}) async-start(), calls=%async_computation.7 | async-start | bytes 5242880 | tf_op jit(solution)/shard_map/psum | solution.py:168
  630.7 11.4 copy-start.56
  652.1 545.9 %reduce-scatter.3.cloned.1.call-start = ((), (), s32[]{:S(2)}) async-start(), calls=%async_computation.8 | async-start | bytes 6553600 | tf_op jit(solution)/shard_map/reduce_scatter | solution.py:208
  667.1 65.2 %copy-start.9 = (bf16[1280,1024]{1,0:T(8,128)(2,1)S(1)}, bf16[1280,1024]{1,0:T(8,128)(2,1)}, u32[]{:S(2)}) copy-start(bf16[1280,1024]{1,0:T(8,128)(2,1)} %all-reduce.11.cloned.1.call-done) | copy-start | bytes 7864324
  744.7 138.2 %copy-start.3 = (bf16[1280,512]{0,1:T(8,128)(2,1)}, bf16[1280,512]{0,1:T(8,128)(2,1)S(1)}, u32[]{:S(2)}) copy-start(bf16[1280,512]{0,1:T(8,128)(2,1)S(1)} %convolution_convert_fusion.6) | copy-start | bytes 3932164
  882.9 160.8 %copy-start.21 = (bf16[1280,8,32]{0,2,1:T(8,128)(2,1)S(1)}, bf16[1280,8,32]{0,2,1:T(8,128)(2,1)}, u32[]{:S(2)}) copy-start(bf16[1280,8,32]{0,2,1:T(8,128)(2,1)} %get-tuple-element.125) | copy-start | bytes 1966084
  882.9 160.8 %copy-start.22 = (bf16[1280,8,32]{0,2,1:T(8,128)(2,1)S(1)}, bf16[1280,8,32]{0,2,1:T(8,128)(2,1)}, u32[]{:S(2)}) copy-start(bf16[1280,8,32]{0,2,1:T(8,128)(2,1)} %get-tuple-element.126) | copy-start | bytes 1966084
  1081.3 128.7 %reduce-scatter.5.cloned.1.call-start = ((), (), s32[]{:S(2)}) async-start(), calls=%async_computation.9 | async-start | bytes 6553600 | tf_op jit(solution)/shard_map/reduce_scatter | solution.py:211
  1153.5 138.9 %all-reduce.17.cloned.1.call-start = ((), (), s32[]{:S(2)}) async-start(), calls=%async_computation.10 | async-start | bytes 5242880 | tf_op jit(solution)/shard_map/psum | solution.py:234
  1217.9 364.7 %all-reduce.19.cloned.1.call-start = ((), (), s32[]{:S(2)}) async-start(), calls=%async_computation.11 | async-start | bytes 29884416 | tf_op jit(solution)/shard_map/psum | solution.py:257
  1233.7 58.8 %copy-start.45 = (f32[1280]{0:T(1024)S(1)}, f32[1280]{0:T(1024)}, u32[]{:S(2)}) copy-start(f32[1280]{0:T(1024)} %copy-done.44) | copy-start | bytes 15364
  1233.7 58.8 %copy-start.49 = (f32[1024]{0:T(1024)S(1)}, f32[1024]{0:T(1024)}, u32[]{:S(2)}) copy-start(f32[1024]{0:T(1024)} %param.20) | copy-start | bytes 12292
  1308.1 39.4 %copy-start.24 = (bf16[1280,1024,1]{1,0,2:T(8,128)(2,1)S(1)}, bf16[1280,1024,1]{1,0,2:T(8,128)(2,1)}, u32[]{:S(2)}) copy-start(bf16[1280,1024,1]{1,0,2:T(8,128)(2,1)} %copy-done.23) | copy-start | bytes 7864324
  (57 other events, 207.3 us)
Sparse Core Ops, SparseCore 0:
  15.2 133.2 all-reduce.8
  160.5 40.4 all-gather.4
  235.0 40.4 all-gather.2
  446.3 74.6 all-reduce.10
  549.5 74.3 all-reduce.12
  652.3 74.3 all-reduce.14
  1081.4 51.3 reduce-scatter.2
  1153.7 51.3 reduce-scatter.4
  1218.1 74.3 all-reduce.16
  1308.2 274.3 all-reduce.18
where the time goes:
time: 1620 us; the launch traced here: 1610 us
  waiting for transfers between devices  616 us (38%)
  matrix products  551 us (34%)
  other arithmetic  305 us (19%)
  local copies, waits for them, and re-layouts  84.2 us (5%)
  blocking collectives  36.3 us (2%)
    psum x1, waiting for transfers between devices, on_device(): lax.psum(adapter_part.astype(jnp.bfloat16), ('dp', 'seq'))  220 us
    convert_element_type x1, other arithmetic, on_device(): score_grad = (probs_back * (prob_grad - jnp.sum(prob_grad * probs_back, a...  161 us
    dot_general x1, matrix products, on_device(): jnp.einsum('qhd,khd->hqk', attended_back, values_back, preferred_element_...  138 us
    psum x1, waiting for transfers between devices, on_device(): lax.psum(jnp.einsum('rcd,cde->re', latent_embed, adapter, preferred_eleme...  131 us
    dot_general x1, matrix products, score_block(): jnp.einsum('qhd,khd->hqk', queries, keys, preferred_element_type=jnp.floa...  74.7 us
    psum x1, waiting for transfers between devices, on_device(): lax.psum(jnp.dot(attended, output_weight, preferred_element_type=jnp.floa...  74.6 us
    psum x1, waiting for transfers between devices, on_device(): lax.psum(jnp.dot(hidden, down_weight, preferred_element_type=jnp.float32)...  74 us
    dot_general x1, matrix products, on_device(): jnp.einsum('hqk,qhd->khd', probs_back.astype(jnp.bfloat16), attended_back...  71 us
  transfers between devices with their start and end apart: 10, of which 6 were waited for; matrix products, arithmetic and copies ran while one was open for 24% of the time, Pallas kernels for 0%

commit v1 on v0

--- a/solution.py
+++ b/solution.py
@@ -1,6 +1,11 @@
+import functools
+
 import jax
 import jax.numpy as jnp
 from jax import lax
+from jax.experimental import pallas as pl
+from jax.experimental.pallas import tpu as pltpu
+from jax.sharding import Mesh
 from jax.sharding import PartitionSpec as P
 
 DH = 64
@@ -290,41 +295,963 @@
     )
 
 
-def solution(mesh):
+TRUNK = 8
+BRANCH = 4
+LEAVES = 2
+SEGS = TRUNK + BRANCH + BRANCH * LEAVES
+WIDE = 2 * DH
+NEG = -1e30
+F32 = jnp.float32
+BF16 = jnp.bfloat16
+KEYS = 512
+HIDDEN = 256
+VMEM_BYTES = 60 << 20
+
+
+def nt(left, right):
+    return lax.dot_general(left, right, (((1,), (1,)), ((), ())), preferred_element_type=F32)
+
+
+def nn(left, right):
+    return lax.dot_general(left, right, (((1,), (0,)), ((), ())), preferred_element_type=F32)
+
+
+def segment(index, size=SEG):
+    return pl.ds(pl.multiple_of(index * SEG, SEG), size)
+
+
+def find_roles(parents, child, count, role):
+    for s in range(SEGS):
+        count[s] = 0
+    role[0] = 0
+    for s in range(SEGS):
+        parent = parents[0, s]
+
+        @pl.when(parent < 0)
+        def _():
+            role[0] = s
+
+        @pl.when(parent >= 0)
+        def _():
+            seen = count[parent]
+            child[parent * BRANCH + seen] = s
+            count[parent] = seen + 1
+
+    for i in range(TRUNK - 1):
+        role[i + 1] = child[role[i] * BRANCH]
+    for b in range(BRANCH):
+        role[TRUNK + b] = child[role[TRUNK - 1] * BRANCH + b]
+    for b in range(BRANCH):
+        for leaf in range(LEAVES):
+            role[TRUNK + BRANCH + b * LEAVES + leaf] = child[role[TRUNK + b] * BRANCH + leaf]
+
+
+def token_parts(refs):
+    owners = refs[0].shape[0]
+    rows = sum(ref.shape[1] for ref in refs)
+    base = 0
+    for ref in refs:
+        for owner in range(owners):
+            for at in range(0, ref.shape[1], SEG):
+                yield ref, owner, at, (owner * rows + base + at) // SEG
+        base += ref.shape[1]
+
+
+def heads_apart(values, first):
+    zero = jnp.zeros_like(values)
+    return jnp.concatenate(
+        [jnp.where(first, values, zero), jnp.where(first, zero, values)], axis=0
+    )
+
+
+def attention_kernel(n_parts, *refs):
+    parents = refs[0]
+    parts = refs[1 : 1 + n_parts]
+    out, logsum, qr, kr, v0, v1, kept, acc, top, total, child, count, role, place = refs[
+        1 + n_parts :
+    ]
+    find_roles(parents, child, count, role)
+    for i in range(SEGS):
+        place[role[i]] = i
+    first = lax.broadcasted_iota(jnp.int32, (SEG, WIDE), 1) < DH
+    for ref, owner, at, seg in token_parts(parts):
+        here = segment(place[seg])
+        block = slice(at, at + SEG)
+        qr[here, :] = ref[owner, block, 0:WIDE] * jnp.asarray(DH**-0.5, BF16)
+        kr[here, :] = ref[owner, block, WIDE : 2 * WIDE]
+        value = ref[owner, block, 2 * WIDE : 3 * WIDE]
+        zero = jnp.zeros_like(value)
+        v0[here, :] = jnp.where(first, value, zero)
+        v1[here, :] = jnp.where(first, zero, value)
+    row = lax.broadcasted_iota(jnp.int32, (2 * SEG, SEG), 0)
+    col = lax.broadcasted_iota(jnp.int32, (2 * SEG, SEG), 1)
+    causal = col <= jnp.where(row >= SEG, row - SEG, row)
+
+    def fold(values, op):
+        result = values[:, 0:128]
+        for at in range(128, values.shape[1], 128):
+            result = op(result, values[:, at : at + 128])
+        return result
+
+    def query(index, count_big, big, extra):
+        queries = heads_apart(qr[segment(index), :], first)
+        own = jnp.where(causal, nt(queries, kr[segment(index), :]), NEG)
+        top[...] = fold(own, jnp.maximum)
+        others = []
+        for other in extra:
+            scores = nt(queries, kr[segment(other), :])
+            top[...] = jnp.maximum(top[...], fold(scores, jnp.maximum))
+            others.append(scores)
+
+        def find(c, _):
+            scores = nt(queries, kr[pl.ds(pl.multiple_of(c * big, big), big), :])
+            kept[c, :, 0:big] = scores
+            top[...] = jnp.maximum(top[...], fold(scores, jnp.maximum))
+            return 0
+
+        lax.fori_loop(0, count_big, find, 0)
+        most = jnp.max(top[...], axis=1, keepdims=True)
+
+        def add(scores, keys, fresh=False):
+            weights = jnp.exp(scores - most)
+            summed = fold(weights, jnp.add)
+            low = weights.astype(BF16)
+            product = nn(low[:SEG], v0[keys, :]) + nn(low[SEG:], v1[keys, :])
+            total[...] = summed if fresh else total[...] + summed
+            acc[...] = product if fresh else acc[...] + product
+
+        add(own, segment(index), True)
+        for other, scores in zip(extra, others):
+            add(scores, segment(other))
+
+        def use(c, _):
+            add(kept[c, :, 0:big], pl.ds(pl.multiple_of(c * big, big), big))
+            return 0
+
+        lax.fori_loop(0, count_big, use, 0)
+        whole = jnp.sum(total[...], axis=1, keepdims=True)
+        inverse = 1.0 / whole
+        log = most + jnp.log(whole)
+        here = segment(role[index])
+        out[here, :] = (acc[...] * jnp.where(first, inverse[:SEG], inverse[SEG:])).astype(BF16)
+        logsum[here, :] = jnp.where(first, log[:SEG], log[SEG:])
+
+    def trunk(i, _):
+        query(i, i, SEG, [])
+        return 0
+
+    def branch(i, _):
+        query(TRUNK + i, TRUNK * SEG // KEYS, KEYS, [])
+        return 0
+
+    def leaf(i, _):
+        query(TRUNK + BRANCH + i, TRUNK * SEG // KEYS, KEYS, [TRUNK + i // LEAVES])
+        return 0
+
+    lax.fori_loop(0, TRUNK, trunk, 0)
+    lax.fori_loop(0, BRANCH, branch, 0)
+    lax.fori_loop(0, BRANCH * LEAVES, leaf, 0)
+
+
+def attention_forward(parents, parts):
+    tokens = SEGS * SEG
+    vmem = pl.BlockSpec(memory_space=pltpu.VMEM)
+    return pl.pallas_call(
+        functools.partial(attention_kernel, len(parts)),
+        out_shape=(
+            jax.ShapeDtypeStruct((tokens, WIDE), BF16),
+            jax.ShapeDtypeStruct((tokens, WIDE), F32),
+        ),
+        in_specs=[pl.BlockSpec(memory_space=pltpu.SMEM)] + [vmem] * len(parts),
+        out_specs=(vmem, vmem),
+        scratch_shapes=[pltpu.VMEM((tokens, WIDE), BF16)] * 4
+        + [
+            pltpu.VMEM((TRUNK, 2 * SEG, KEYS), F32),
+            pltpu.VMEM((SEG, WIDE), F32),
+            pltpu.VMEM((2 * SEG, 128), F32),
+            pltpu.VMEM((2 * SEG, 128), F32),
+            pltpu.SMEM((SEGS * BRANCH,), jnp.int32),
+            pltpu.SMEM((SEGS,), jnp.int32),
+            pltpu.SMEM((SEGS,), jnp.int32),
+            pltpu.SMEM((SEGS,), jnp.int32),
+        ],
+        compiler_params=pltpu.CompilerParams(vmem_limit_bytes=VMEM_BYTES),
+        cost_estimate=pl.CostEstimate(
+            flops=152 * 2 * 4 * SEG * SEG * 128,
+            bytes_accessed=tokens * WIDE * 12,
+            transcendentals=152 * 2 * SEG * SEG,
+        ),
+        name="attention_forward",
+    )(parents, *parts)
+
+
+def swap_halves(values, low):
+    return jnp.where(
+        low, pltpu.roll(values, WIDE - DH // 2, 1), pltpu.roll(values, DH // 2, 1)
+    )
+
+
+def attention_back_kernel(n_parts, *refs):
+    parents = refs[0]
+    parts = refs[1 : 1 + n_parts]
+    (
+        upstream,
+        attended,
+        logsum,
+        cosine,
+        sine,
+        out,
+        qr,
+        kr,
+        vr,
+        kt,
+        dk,
+        dv,
+        dqt,
+        child,
+        count,
+        role,
+        place,
+    ) = refs[1 + n_parts :]
+    find_roles(parents, child, count, role)
+    for i in range(SEGS):
+        place[role[i]] = i
+    lane = lax.broadcasted_iota(jnp.int32, (SEG, WIDE), 1)
+    first = lane < DH
+    low = (lane % DH) < (DH // 2)
+    for ref, owner, at, seg in token_parts(parts):
+        here = segment(place[seg])
+        block = slice(at, at + SEG)
+        qr[here, :] = ref[owner, block, 0:WIDE] * jnp.asarray(DH**-0.5, BF16)
+        key = ref[owner, block, WIDE : 2 * WIDE]
+        kr[here, :] = key
+        kt[:, here] = key.T
+        vr[here, :] = ref[owner, block, 2 * WIDE : 3 * WIDE]
+    dk[...] = jnp.zeros_like(dk)
+    dv[...] = jnp.zeros_like(dv)
+    key_at = lax.broadcasted_iota(jnp.int32, (SEG, 2 * SEG), 0)
+    query_at = lax.broadcasted_iota(jnp.int32, (SEG, 2 * SEG), 1)
+    causal = key_at <= jnp.where(query_at >= SEG, query_at - SEG, query_at)
+
+    def rope_back(values, depth):
+        at = segment(depth)
+        return values * cosine[at, :] - swap_halves(values, low) * sine[at, :]
+
+    def query(index, depth, count_big, big, extra):
+        here = segment(role[index])
+        queries = heads_apart(qr[segment(index), :], first)
+        up = upstream[here, :]
+        ups = heads_apart(up, first)
+        turned = logsum[here, :].T
+        log = jnp.concatenate([turned[0:1, :], turned[DH : DH + 1, :]], axis=1)
+        product = (up.astype(F32) * attended[here, :].astype(F32)).T
+        inner = jnp.concatenate(
+            [
+                jnp.sum(product[:DH], axis=0, keepdims=True),
+                jnp.sum(product[DH:], axis=0, keepdims=True),
+            ],
+            axis=1,
+        )
+        dqt[...] = jnp.zeros_like(dqt)
+
+        def add(keys, mask=None):
+            weights = jnp.exp(nt(kr[keys, :], queries) - log)
+            if mask is not None:
+                weights = jnp.where(mask, weights, 0.0)
+            back = (weights * (nt(vr[keys, :], ups) - inner)).astype(BF16)
+            dv[keys, :] += nn(weights.astype(BF16), ups)
+            dk[keys, :] += nn(back, queries)
+            dqt[...] += nn(kt[:, keys], back)
+
+        add(segment(index), causal)
+        for other in extra:
+            add(segment(other))
+
+        def use(c, _):
+            add(pl.ds(pl.multiple_of(c * big, big), big))
+            return 0
+
+        lax.fori_loop(0, count_big, use, 0)
+        both = jnp.concatenate([dqt[:DH, :SEG], dqt[DH:, SEG:]], axis=0) * (DH**-0.5)
+        out[here, 0:WIDE] = rope_back(both.T, depth).astype(BF16)
+
+    def leaf(i, _):
+        query(TRUNK + BRANCH + i, TRUNK + 1, TRUNK * SEG // KEYS, KEYS, [TRUNK + i // LEAVES])
+        return 0
+
+    def branch(i, _):
+        query(TRUNK + i, TRUNK, TRUNK * SEG // KEYS, KEYS, [])
+        return 0
+
+    def trunk(i, _):
+        query(i, i, i, SEG, [])
+        return 0
+
+    lax.fori_loop(0, BRANCH * LEAVES, leaf, 0)
+    lax.fori_loop(0, BRANCH, branch, 0)
+    lax.fori_loop(0, TRUNK, trunk, 0)
+
+    def finish(i, _):
+        here = segment(role[i])
+        depth = jnp.where(i < TRUNK + BRANCH, jnp.minimum(i, TRUNK), TRUNK + 1)
+        out[here, WIDE : 2 * WIDE] = rope_back(dk[segment(i), :], depth).astype(BF16)
+        out[here, 2 * WIDE : 3 * WIDE] = dv[segment(i), :].astype(BF16)
+        return 0
+
+    lax.fori_loop(0, SEGS, finish, 0)
+
+
+def attention_backward(parents, parts, upstream, attended, logsum, cosine, sine):
+    tokens = SEGS * SEG
+    vmem = pl.BlockSpec(memory_space=pltpu.VMEM)
+    return pl.pallas_call(
+        functools.partial(attention_back_kernel, len(parts)),
+        out_shape=jax.ShapeDtypeStruct((tokens, 3 * WIDE), BF16),
+        in_specs=[pl.BlockSpec(memory_space=pltpu.SMEM)] + [vmem] * (len(parts) + 5),
+        out_specs=vmem,
+        scratch_shapes=[pltpu.VMEM((tokens, WIDE), BF16)] * 3
+        + [pltpu.VMEM((WIDE, tokens), BF16)]
+        + [pltpu.VMEM((tokens, WIDE), F32)] * 2
+        + [
+            pltpu.VMEM((WIDE, 2 * SEG), F32),
+            pltpu.SMEM((SEGS * BRANCH,), jnp.int32),
+            pltpu.SMEM((SEGS,), jnp.int32),
+            pltpu.SMEM((SEGS,), jnp.int32),
+            pltpu.SMEM((SEGS,), jnp.int32),
+        ],
+        compiler_params=pltpu.CompilerParams(vmem_limit_bytes=VMEM_BYTES),
+        cost_estimate=pl.CostEstimate(
+            flops=152 * 2 * 10 * SEG * SEG * 128,
+            bytes_accessed=tokens * WIDE * 24,
+            transcendentals=152 * 2 * SEG * SEG,
+        ),
+        name="attention_backward",
+    )(parents, *parts, upstream, attended, logsum, cosine, sine)
+
+
+def angle_tables(positions):
+    lane = jnp.arange(WIDE)
+    freq = THETA ** (-(lane % (DH // 2)).astype(F32) * 2.0 / DH)
+    angle = positions.astype(F32)[:, None] * freq[None, :]
+    sign = jnp.where((lane % DH) < DH // 2, -1.0, 1.0)
+    return jnp.cos(angle), jnp.sin(angle) * sign[None, :]
+
+
+def project_kernel(mine, theirs, gain, query_w, key_w, value_w, cosine, sine, out, low_out):
+    total = mine[...].astype(F32) + theirs[...].astype(F32)
+    scale = lax.rsqrt(jnp.mean(total * total, axis=-1, keepdims=True) + EPSILON)
+    rounded = (total * scale * gain[...]).astype(BF16)
+    low_out[...] = rounded
+    low = (lax.broadcasted_iota(jnp.int32, (total.shape[0], WIDE), 1) % DH) < (DH // 2)
+    for at, weight in enumerate((query_w, key_w, value_w)):
+        raw = nn(rounded, weight[...])
+        for peer in range(out.shape[0]):
+            part = raw[:, peer * WIDE : (peer + 1) * WIDE]
+            if at < 2:
+                part = part * cosine[...] + swap_halves(part, low) * sine[...]
+            out[peer, :, at * WIDE : (at + 1) * WIDE] = part.astype(BF16)
+
+
+def project(mine, theirs, gain, query_w, key_w, value_w, cosine, sine):
+    rows, width = mine.shape
+    block = SEG
+    inner = query_w.shape[1]
+    peers = inner // WIDE
+    by_row = pl.BlockSpec((block, width), lambda i: (i, 0))
+    weight = pl.BlockSpec((width, inner), lambda i: (0, 0))
+    table = pl.BlockSpec((block, WIDE), lambda i: (i, 0))
+    return pl.pallas_call(
+        project_kernel,
+        grid=(rows // block,),
+        out_shape=(
+            jax.ShapeDtypeStruct((peers, rows, 3 * WIDE), BF16),
+            jax.ShapeDtypeStruct((rows, width), BF16),
+        ),
+        in_specs=[
+            by_row,
+            by_row,
+            pl.BlockSpec((1, width), lambda i: (0, 0)),
+            weight,
+            weight,
+            weight,
+            table,
+            table,
+        ],
+        out_specs=(pl.BlockSpec((peers, block, 3 * WIDE), lambda i: (0, i, 0)), by_row),
+        compiler_params=pltpu.CompilerParams(vmem_limit_bytes=VMEM_BYTES),
+        cost_estimate=pl.CostEstimate(
+            flops=2 * rows * width * 3 * inner,
+            bytes_accessed=rows * width * 6 + 6 * width * inner + rows * inner * 6,
+            transcendentals=rows,
+        ),
+        name="project",
+    )(mine, theirs, gain, query_w, key_w, value_w, cosine, sine)
+
+
+def middle_kernel(
+    meta,
+    adapted,
+    heads,
+    cotangent,
+    second_gain,
+    third_gain,
+    fourth_gain,
+    wo_own,
+    wo_all,
+    wg_own,
+    wg_all,
+    wu_own,
+    wu_all,
+    wd_own,
+    wd_all,
+    layer_out,
+    middle_out,
+    attended_out,
+    attention_out,
+    third_out,
+    mixed_out,
+    hidden_out,
+    gate_out,
+    up_out,
+    heads_back,
+    gains_out,
+    wo,
+    wg,
+    wu,
+    wd,
+    gate_s,
+    up_s,
+    sums,
+    sem,
+):
+    step = pl.program_id(0)
+    tensor = meta[0]
+    copies = []
+    for weight, own, all_of, by_lane in (
+        (wo, wo_own, wo_all, False),
+        (wg, wg_own, wg_all, True),
+        (wu, wu_own, wu_all, True),
+        (wd, wd_own, wd_all, False),
+    ):
+        rows, lanes = own.shape
+        other = all_of.at[pl.ds(pl.multiple_of((1 - tensor) * rows, 128), rows)]
+        for src, row, lane in (
+            (own, 0, 0),
+            (other, 0 if by_lane else rows, lanes if by_lane else 0),
+        ):
+            dst = weight.at[pl.ds(row, rows), pl.ds(lane, lanes)]
+            copies.append(pltpu.make_async_copy(src, dst, sem.at[len(copies)]))
+
+    @pl.when(step == 0)
+    def _():
+        for copy in copies:
+            copy.start()
+        gains_out[...] = jnp.zeros_like(gains_out)
+        for copy in copies[:2]:
+            copy.wait()
+
+    groups = heads.shape[0] // 2
+    for side in range(2):
+        for group in range(groups):
+            at = (side * groups + group) * WIDE
+            source = group * 2 + (tensor if side == 0 else 1 - tensor)
+            attended_out[:, at : at + WIDE] = heads[source]
+    attention = nn(attended_out[...], wo[...])
+
+    def scaling(values):
+        return lax.rsqrt(jnp.mean(values * values, axis=-1, keepdims=True) + EPSILON)
+
+    def inward(upstream, gain, normed, scale):
+        scaled = upstream * gain
+        return scale * (scaled - normed * jnp.mean(scaled * normed, axis=-1, keepdims=True))
+
+    second_scale = scaling(attention)
+    second_normed = attention * second_scale
+    middle = adapted[...] + second_normed * second_gain[...]
+    third_scale = scaling(middle)
+    third_normed = middle * third_scale
+    third_out[...] = (third_normed * third_gain[...]).astype(BF16)
+
+    @pl.when(step == 0)
+    def _():
+        for copy in copies[2:]:
+            copy.wait()
+
+    sums[...] = jnp.zeros_like(sums)
+
+    def forward(c, _):
+        cut = pl.ds(pl.multiple_of(c * HIDDEN, HIDDEN), HIDDEN)
+        gate = nn(third_out[...], wg[:, cut])
+        upward = nn(third_out[...], wu[:, cut])
+        gate_s[c] = gate
+        up_s[c] = upward
+        hidden = (gate / (1.0 + jnp.exp(-gate)) * upward).astype(BF16)
+        hidden_out[:, cut] = hidden
+        sums[...] += nn(hidden, wd[cut, :])
+        return 0
+
+    lax.fori_loop(0, gate_s.shape[0], forward, 0)
+    mixed = sums[...]
+    fourth_scale = scaling(mixed)
+    fourth_normed = mixed * fourth_scale
+    layer_out[...] = (middle + fourth_normed * fourth_gain[...]).astype(BF16)
+    upstream = cotangent[...].astype(F32)
+    gains_out[2:3, :] += jnp.sum(upstream * fourth_normed, axis=0, keepdims=True)
+    mixed_out[...] = inward(upstream, fourth_gain[...], fourth_normed, fourth_scale).astype(BF16)
+    sums[...] = jnp.zeros_like(sums)
+
+    def backward(c, _):
+        cut = pl.ds(pl.multiple_of(c * HIDDEN, HIDDEN), HIDDEN)
+        back = nt(mixed_out[...], wd[cut, :]).astype(BF16).astype(F32)
+        gate = gate_s[c]
+        sigmoid = 1.0 / (1.0 + jnp.exp(-gate))
+        silu = gate * sigmoid
+        gate_back = (back * up_s[c] * (sigmoid + silu * (1.0 - sigmoid))).astype(BF16)
+        up_back = (back * silu).astype(BF16)
+        gate_out[:, cut] = gate_back
+        up_out[:, cut] = up_back
+        sums[...] += nt(gate_back, wg[:, cut]) + nt(up_back, wu[:, cut])
+        return 0
+
+    lax.fori_loop(0, gate_s.shape[0], backward, 0)
+    third_back = sums[...]
+    gains_out[1:2, :] += jnp.sum(third_back * third_normed, axis=0, keepdims=True)
+    middle_back = upstream + inward(third_back, third_gain[...], third_normed, third_scale)
+    middle_out[...] = middle_back
+    gains_out[0:1, :] += jnp.sum(middle_back * second_normed, axis=0, keepdims=True)
+    attention_out[...] = inward(
+        middle_back, second_gain[...], second_normed, second_scale
+    ).astype(BF16)
+    heads_low = nt(attention_out[...], wo[...]).astype(BF16)
+    for side in range(2):
+        for group in range(groups):
+            at = (side * groups + group) * WIDE
+            target = group * 2 + (tensor if side == 0 else 1 - tensor)
+            heads_back[target] = heads_low[:, at : at + WIDE]
+
+
+def middle_section(meta, adapted, heads, cotangent, gains, weights):
+    rows, width = adapted.shape
+    sources = heads.shape[0]
+    inner = sources * WIDE
+    hidden = 2 * weights[2].shape[1]
+    block = rows // 2
+    steps = rows // block
+    row = pl.BlockSpec((block, width), lambda i, meta: (i, 0))
+    wide = pl.BlockSpec((block, hidden), lambda i, meta: (i, 0))
+    head = pl.BlockSpec((sources, block, WIDE), lambda i, meta: (0, i, 0))
+    gain = pl.BlockSpec((1, width), lambda i, meta: (0, 0))
+    hbm = pl.BlockSpec(memory_space=pl.ANY)
+    return pl.pallas_call(
+        middle_kernel,
+        grid_spec=pltpu.PrefetchScalarGridSpec(
+            num_scalar_prefetch=1,
+            grid=(steps,),
+            in_specs=[
+                row,
+                head,
+                pl.BlockSpec((block, width), lambda i, meta: (meta[0] * steps + i, 0)),
+                gain,
+                gain,
+                gain,
+            ]
+            + [hbm] * 8,
+            out_specs=(
+                row,
+                row,
+                pl.BlockSpec((block, inner), lambda i, meta: (i, 0)),
+                row,
+                row,
+                row,
+                wide,
+                wide,
+                wide,
+                head,
+                pl.BlockSpec((8, width), lambda i, meta: (0, 0)),
+            ),
+            scratch_shapes=[
+                pltpu.VMEM((inner, width), BF16),
+                pltpu.VMEM((width, hidden), BF16),
+                pltpu.VMEM((width, hidden), BF16),
+                pltpu.VMEM((hidden, width), BF16),
+                pltpu.VMEM((hidden // HIDDEN, block, HIDDEN), F32),
+                pltpu.VMEM((hidden // HIDDEN, block, HIDDEN), F32),
+                pltpu.VMEM((block, width), F32),
+                pltpu.SemaphoreType.DMA((8,)),
+            ],
+        ),
+        out_shape=(
+            jax.ShapeDtypeStruct((rows, width), BF16),
+            jax.ShapeDtypeStruct((rows, width), F32),
+            jax.ShapeDtypeStruct((rows, inner), BF16),
+            jax.ShapeDtypeStruct((rows, width), BF16),
+            jax.ShapeDtypeStruct((rows, width), BF16),
+            jax.ShapeDtypeStruct((rows, width), BF16),
+            jax.ShapeDtypeStruct((rows, hidden), BF16),
+            jax.ShapeDtypeStruct((rows, hidden), BF16),
+            jax.ShapeDtypeStruct((rows, hidden), BF16),
+            jax.ShapeDtypeStruct((sources, rows, WIDE), BF16),
+            jax.ShapeDtypeStruct((8, width), F32),
+        ),
+        compiler_params=pltpu.CompilerParams(vmem_limit_bytes=VMEM_BYTES),
+        cost_estimate=pl.CostEstimate(
+            flops=rows * width * (4 * inner + 12 * hidden),
+            bytes_accessed=6 * width * hidden + 2 * width * inner + rows * (hidden * 6 + width * 20),
+            transcendentals=rows * hidden * 2,
+        ),
+        name="middle_section",
+    )(meta, adapted, heads, cotangent, *gains, *weights)
+
+
+def input_back_kernel(meta, parts, query_w, key_w, value_w, out, joined):
+    inner = query_w.shape[1]
+    for at in range(3):
+        for group in range(parts.shape[0]):
+            to = at * inner + group * WIDE
+            joined[:, to : to + WIDE] = parts[group, :, at * WIDE : (at + 1) * WIDE]
+    total = nt(joined[:, 0:inner], query_w[...])
+    total += nt(joined[:, inner : 2 * inner], key_w[...])
+    total += nt(joined[:, 2 * inner : 3 * inner], value_w[...])
+    out[...] = total.astype(out.dtype)
+
+
+def input_back(meta, parts, query_w, key_w, value_w, dtype):
+    groups, rows, lanes = parts.shape
+    rows = rows // 2
+    width, inner = query_w.shape
+    block = rows // 2
+    steps = 2
+    weight = pl.BlockSpec((width, inner), lambda i, meta: (0, 0))
+    return pl.pallas_call(
+        input_back_kernel,
+        grid_spec=pltpu.PrefetchScalarGridSpec(
+            num_scalar_prefetch=1,
+            grid=(steps,),
+            in_specs=[
+                pl.BlockSpec((groups, block, lanes), lambda i, meta: (0, meta[0] * steps + i, 0)),
+                weight,
+                weight,
+                weight,
+            ],
+            out_specs=(
+                pl.BlockSpec((block, width), lambda i, meta: (i, 0)),
+                pl.BlockSpec((block, 3 * inner), lambda i, meta: (i, 0)),
+            ),
+        ),
+        out_shape=(
+            jax.ShapeDtypeStruct((rows, width), dtype),
+            jax.ShapeDtypeStruct((rows, 3 * inner), BF16),
+        ),
+        compiler_params=pltpu.CompilerParams(vmem_limit_bytes=VMEM_BYTES),
+        cost_estimate=pl.CostEstimate(
+            flops=2 * rows * width * 3 * inner,
+            bytes_accessed=rows * inner * 12 + 6 * width * inner + rows * width * 4,
+            transcendentals=0,
+        ),
+        name="input_back",
+    )(meta, parts, query_w, key_w, value_w)
+
+
+def swap(value, axis):
+    return lax.ppermute(value, axis, [(0, 1), (1, 0)])
+
+
+def together(*values):
+    return lax.optimization_barrier(values)
+
+
+def cut(value, index, rows):
+    return lax.dynamic_slice_in_dim(value, index * rows, rows, 0)
+
+
+def add_low(left, right):
+    return (left.astype(F32) + right.astype(F32)).astype(BF16)
+
+
+def fold(value, index, axis):
+    half = value.shape[0] // 2
+    return add_low(cut(value, index, half), swap(cut(value, 1 - index, half), axis))
+
+
+def unfold(value, index, axis):
+    other = swap(value, axis)
+    return jnp.concatenate(
+        [jnp.where(index == 0, value, other), jnp.where(index == 0, other, value)], axis=0
+    )
+
+
+def sum_small(value):
+    for axis in ("tensor", "core", "x"):
+        value = value + swap(value, axis)
+    for pairs in ([(0, 1), (1, 0), (2, 3), (3, 2)], [(0, 2), (2, 0), (1, 3), (3, 1)]):
+        value = value + lax.ppermute(value, "dp", pairs)
+    return value
+
+
+def tn(left, right):
+    return lax.dot_general(
+        left, right, (((0,), (0,)), ((), ())), preferred_element_type=F32
+    ).astype(BF16)
+
+
+def on_device_paired(
+    latent_embed,
+    adapter,
+    first_gain,
+    query_weight,
+    key_weight,
+    value_weight,
+    output_weight,
+    second_gain,
+    third_gain,
+    gate_weight,
+    up_weight,
+    down_weight,
+    fourth_gain,
+    parents,
+    positions,
+    cotangent,
+):
+    rows = latent_embed.shape[0]
+    width = adapter.shape[2]
+    half_rows = rows // 2
+    tensor = lax.axis_index("tensor")
+    core = lax.axis_index("core")
+    x = lax.axis_index("x")
+    everyone = ("x", "core", "tensor")
+    meta = jnp.stack([tensor, core]).astype(jnp.int32)
+    meta_other = jnp.stack([1 - tensor, core]).astype(jnp.int32)
+    one_row = lambda gain: gain.reshape(1, -1)
+
+    cosine, sine = angle_tables(positions)
+    cuts = [0, 2 * SEG, 4 * SEG, rows]
+    adapted_parts, low_parts, head_parts = [], [], []
+    mine = [
+        jnp.einsum(
+            "rcd,cde->re", latent_embed[start:stop], adapter, preferred_element_type=F32
+        ).astype(BF16)
+        for start, stop in zip(cuts[:-1], cuts[1:])
+    ]
+    theirs = []
+    for i in range(len(mine)):
+        if i > 0:
+            mine[i], theirs[i - 1] = together(mine[i], theirs[i - 1])
+        theirs.append(swap(mine[i], "tensor"))
+    own_weights = (output_weight, gate_weight, up_weight, down_weight)
+    pieces = [cut(weight, 2 * x + core, weight.shape[0] // 4) for weight in own_weights]
+    *pieces, theirs[-1] = together(*pieces, theirs[-1])
+    weights = []
+    for weight, piece in zip(own_weights, pieces):
+        weights.append(weight)
+        weights.append(lax.all_gather(piece, ("tensor", "x", "core"), axis=0, tiled=True))
+    for i in range(len(mine)):
+        start, stop = cuts[i], cuts[i + 1]
+        sent, low = project(
+            mine[i],
+            theirs[i],
+            one_row(first_gain),
+            query_weight,
+            key_weight,
+            value_weight,
+            cosine[start:stop],
+            sine[start:stop],
+        )
+        head_parts.append(lax.all_to_all(sent, ("x", "core"), 0, 0, tiled=False))
+        low_parts.append(low)
+        adapted_parts.append(mine[i].astype(F32) + theirs[i].astype(F32))
+    adapted = cut(jnp.concatenate(adapted_parts, axis=0), tensor, half_rows)
+    first_low = jnp.concatenate(low_parts, axis=0)
+
+    attended, logsum = attention_forward(parents, head_parts)
+    heads = lax.all_to_all(
+        attended.reshape(8, half_rows, WIDE), everyone, 0, 0, tiled=False
+    )
+    (
+        layer_half,
+        middle_back,
+        attended_all,
+        attention_low,
+        third_low,
+        mixed_low,
+        hidden,
+        gate_low,
+        up_low,
+        heads_back,
+        gain_parts,
+    ) = middle_section(
+        meta,
+        adapted,
+        heads,
+        cotangent,
+        (one_row(second_gain), one_row(third_gain), one_row(fourth_gain)),
+        weights,
+    )
+    upstream = lax.all_to_all(heads_back, everyone, 0, 0, tiled=False).reshape(-1, WIDE)
+    layer_other = swap(layer_half, "tensor")
+    layer_out = jnp.concatenate(
+        [
+            jnp.where(tensor == 0, layer_half, layer_other),
+            jnp.where(tensor == 0, layer_other, layer_half),
+        ],
+        axis=0,
+    ).astype(F32)
+
+    split = gate_weight.shape[1]
+    inner = output_weight.shape[0]
+    own, other = slice(None, split), slice(split, None)
+    gate_sides = [fold(tn(third_low, gate_low[:, side]), core, "core") for side in (own, other)]
+    up_sides = [fold(tn(third_low, up_low[:, side]), core, "core") for side in (own, other)]
+    down_sides = [fold(tn(hidden[:, side], mixed_low), core, "core") for side in (own, other)]
+    output_sides = [
+        fold(tn(attended_all[:, side], attention_low), core, "core")
+        for side in (slice(None, inner), slice(inner, None))
+    ]
+    upstream, *sides = together(
+        upstream, *gate_sides, *up_sides, *down_sides, *output_sides
+    )
+    gate_sides, up_sides, down_sides, output_sides = (
+        sides[0:2],
+        sides[2:4],
+        sides[4:6],
+        sides[6:8],
+    )
+    gate_sides = [fold(side, x, "x") for side in gate_sides]
+    up_sides = [fold(side, x, "x") for side in up_sides]
+    down_kept = add_low(down_sides[0], swap(down_sides[1], "tensor"))
+    output_kept = add_low(output_sides[0], swap(output_sides[1], "tensor"))
+
+    table_cosine, table_sine = angle_tables(jnp.arange((TRUNK + 2) * SEG))
+    sent = attention_backward(
+        parents, head_parts, upstream, attended, logsum, table_cosine, table_sine
+    )
+    parts = lax.all_to_all(
+        sent.reshape(4, rows, 3 * WIDE), ("x", "core"), 0, 0, tiled=False
+    )
+
+    def finish(value):
+        return unfold(unfold(value, x, "x"), core, "core").astype(F32)
+
+    gate_kept = add_low(gate_sides[0], swap(gate_sides[1], "tensor"))
+    up_kept = add_low(up_sides[0], swap(up_sides[1], "tensor"))
+    gate_sum, up_sum = lax.psum((gate_kept, up_kept), "dp")
+    parts, down_kept, output_kept = together(parts, down_kept, output_kept)
+    down_kept = fold(down_kept, x, "x")
+    output_kept = fold(output_kept, x, "x")
+    down_kept, output_kept, gate_sum, up_sum = together(down_kept, output_kept, gate_sum, up_sum)
+    down_sum, output_sum = lax.psum((down_kept, output_kept), "dp")
+
+    away, joined_away = input_back(
+        meta_other, parts, query_weight, key_weight, value_weight, BF16
+    )
+    home, joined_home = input_back(meta, parts, query_weight, key_weight, value_weight, F32)
+    away = swap(away, "tensor")
+    first_low_home = cut(first_low, tensor, half_rows)
+    first_low_away = cut(first_low, 1 - tensor, half_rows)
+    input_part = (
+        lax.dot_general(
+            first_low_home, joined_home, (((0,), (0,)), ((), ())), preferred_element_type=F32
+        )
+        + lax.dot_general(
+            first_low_away, joined_away, (((0,), (0,)), ((), ())), preferred_element_type=F32
+        )
+    ).astype(BF16)
+    input_kept = fold(fold(input_part, core, "core"), x, "x")
+    input_kept, down_sum, output_sum = together(input_kept, down_sum, output_sum)
+    input_sum = lax.psum(input_kept, "dp")
+    first_back = home + away.astype(F32)
+    first_out, first_normed, first_scale = normalize(adapted, first_gain)
+    adapted_part, first_gain_part = normalize_back(
+        first_back, first_gain, first_normed, first_scale
+    )
+    adapted_home = (middle_back + adapted_part).astype(BF16)
+    adapted_away = swap(adapted_home, "tensor")
+    adapted_low = jnp.concatenate(
+        [
+            jnp.where(tensor == 0, adapted_home, adapted_away),
+            jnp.where(tensor == 0, adapted_away, adapted_home),
+        ],
+        axis=0,
+    )
+    adapter_part = jnp.einsum(
+        "rcd,re->cde", latent_embed, adapted_low, preferred_element_type=F32
+    ).astype(BF16)
+    adapter_kept = fold(fold(adapter_part.reshape(-1, width), core, "core"), x, "x")
+    adapter_kept, input_sum = together(adapter_kept, input_sum)
+    adapter_sum = lax.psum(adapter_kept, "dp")
+    latent_gradient = jnp.einsum("re,cde->rcd", adapted_low, adapter, preferred_element_type=F32)
+    gains = sum_small(jnp.concatenate([gain_parts[:3], first_gain_part[None]], axis=0))
+    gate_total, up_total = finish(gate_sum), finish(up_sum)
+    down_total, output_total = finish(down_sum), finish(output_sum)
+    input_total = finish(input_sum)
+    adapter_total = finish(adapter_sum).reshape(adapter.shape)
+    return (
+        layer_out,
+        latent_gradient,
+        adapter_total,
+        gains[3],
+        input_total[:, :inner],
+        input_total[:, inner : 2 * inner],
+        input_total[:, 2 * inner :],
+        output_total,
+        gains[0],
+        gains[1],
+        gate_total,
+        up_total,
+        down_total,
+        gains[2],
+    )
+
+
+def specs(rows):
+    split = P(None, "tensor")
     in_specs = (
-        P(("dp", "seq"), None, "tensor"),
+        P(rows, None, "tensor"),
         P(None, "tensor", None),
         P(),
-        P(None, "tensor"),
-        P(None, "tensor"),
-        P(None, "tensor"),
+        split,
+        split,
+        split,
         P("tensor", None),
         P(),
         P(),
-        P(None, "tensor"),
-        P(None, "tensor"),
+        split,
+        split,
         P("tensor", None),
         P(),
         P("dp", None),
-        P(("dp", "seq")),
-        P(("dp", "seq"), None),
+        P(rows),
+        P(rows, None),
     )
     out_specs = (
-        P(("dp", "seq"), None),
-        P(("dp", "seq"), None, "tensor"),
+        P(rows, None),
+        P(rows, None, "tensor"),
         P(None, "tensor", None),
         P(),
-        P(None, "tensor"),
-        P(None, "tensor"),
-        P(None, "tensor"),
+        split,
+        split,
+        split,
         P("tensor", None),
         P(),
         P(),
-        P(None, "tensor"),
-        P(None, "tensor"),
+        split,
+        split,
         P("tensor", None),
         P(),
     )
+    return in_specs, out_specs
+
+
+def solution(mesh):
+    sizes = dict(mesh.shape)
+    if sizes["seq"] == 4 and sizes["tensor"] == 2:
+        fine = Mesh(
+            mesh.devices.reshape(sizes["dp"], 2, 2, 2), ("dp", "x", "core", "tensor")
+        )
+        in_specs, out_specs = specs(("dp", "x", "core"))
+        return jax.shard_map(
+            on_device_paired, mesh=fine, in_specs=in_specs, out_specs=out_specs, check_vma=False
+        )
+    in_specs, out_specs = specs(("dp", "seq"))
     return jax.shard_map(
         on_device, mesh=mesh, in_specs=in_specs, out_specs=out_specs, check_vma=False
     )

time: 1620 us -> 859 us (0.53)
  matrix products: 551 us -> 39.8 us
  waiting for transfers between devices: 616 us -> 340 us
  Pallas kernels: 0 us -> 231 us
  other arithmetic: 305 us -> 98.7 us
  starting transfers between devices: 1.2 us -> 65.6 us
  blocking collectives: 36.3 us -> 0 us
  local copies, waits for them, and re-layouts: 84.2 us -> 59.2 us
    psum x6 -> x4, waiting for transfers between devices: 616 us -> 43.3 us  [the longest x1 30.3 us: on_device_paired(): adapter_sum = lax.psum(adapter_kept, 'dp')]
    dot_general x30 -> x15, matrix products: 551 us -> 39.8 us  [the longest x8 21.6 us: tn(): lax.dot_general(left, right, (((0,), (0,)), ((), ())), preferred_element_...]
    pallas_call x0 -> x8, Pallas kernels: none -> 231 us  [the longest x1 78.2 us: attention_backward(): pl.pallas_call(functools.partial(attention_back_kernel, len(parts)), out_...]
    ppermute x0 -> x45, waiting for transfers between devices: none -> 215 us  [the longest x43 213 us: swap(): return lax.ppermute(value, axis, [(0, 1), (1, 0)])]
    convert_element_type x18 -> x30, other arithmetic: 188 us -> 53.7 us  [the longest x20 30.1 us: add_low(): return (left.astype(F32) + right.astype(F32)).astype(BF16)]
    all_to_all x0 -> x6, waiting for transfers between devices: none -> 73.8 us  [the longest x3 53.8 us: on_device_paired(): head_parts.append(lax.all_to_all(sent, ('x', 'core'), 0, 0, tiled=False))]
    reduce_sum x1 -> x0, other arithmetic: 63.5 us -> none  [on_device(): total = jnp.sum(weights, axis=-1, keepdims=True)]
    ppermute x0 -> x45, starting transfers between devices: none -> 39.4 us  [the longest x43 35.7 us: swap(): return lax.ppermute(value, axis, [(0, 1), (1, 0)])]
  transfers between devices with their start and end apart: 10 -> 59, of which waited for: 6 -> 25; matrix products, arithmetic and copies ran while one was open for 24% -> 19% of each run, Pallas kernels for 0% -> 20%
where the time goes in v1:
time: 859 us; the launch traced here: 850 us
  waiting for transfers between devices  340 us (40%)
  Pallas kernels  231 us (27%)
  other arithmetic  98.7 us (11%)
  starting transfers between devices  65.6 us (8%)
  local copies, waits for them, and re-layouts  59.2 us (7%)
  matrix products  39.8 us (5%)
  between operations  15.7 us (2%)
    ppermute x43, waiting for transfers between devices, swap(): return lax.ppermute(value, axis, [(0, 1), (1, 0)])  213 us
    pallas_call x1, Pallas kernels, attention_backward(): pl.pallas_call(functools.partial(attention_back_kernel, len(parts)), out_...  78.2 us
    pallas_call x1, Pallas kernels, attention_forward(): pl.pallas_call(functools.partial(attention_kernel, len(parts)), out_shape...  63 us
    pallas_call x1, Pallas kernels, middle_section(): pl.pallas_call(middle_kernel, grid_spec=pltpu.PrefetchScalarGridSpec(num_...  60.6 us
    all_to_all x3, waiting for transfers between devices, on_device_paired(): head_parts.append(lax.all_to_all(sent, ('x', 'core'), 0, 0, tiled=False))  53.8 us
    ppermute x43, starting transfers between devices, swap(): return lax.ppermute(value, axis, [(0, 1), (1, 0)])  35.7 us
    psum x1, waiting for transfers between devices, on_device_paired(): adapter_sum = lax.psum(adapter_kept, 'dp')  30.3 us
    convert_element_type x20, other arithmetic, add_low(): return (left.astype(F32) + right.astype(F32)).astype(BF16)  30.1 us
  transfers between devices with their start and end apart: 59, of which 25 were waited for; matrix products, arithmetic and copies ran while one was open for 19% of the time, Pallas kernels for 20%

profile of v1, /device:TPU:0, one launch (start us, length us, event | category | flops | bytes accessed | tf_op | source)
XLA Modules:
  0.0 849.6 jit_solution(15932501451649819598)
XLA Ops:
  16.6 20.9 %collective-permute-done.theirs = bf16[512,1024]{1,0:T(8,128)(2,1)S(1)} collective-permute-done((bf16[512,1024]{1,0:T(8,128)(2,1)S(1)}, bf16[512,1024]{1,0:T(8,128)(2,1)S(1)}, u32[]{:S(2)}, u32[]{:S(2)}) %collective-permute-start) | collective-permute-done | bytes 1048608 | tf_op jit(solution)/shard_map/ppermute | solution.py:956
  41.0 22.2 %collective-permute-done.1.theirs = bf16[512,1024]{1,0:T(8,128)(2,1)} collective-permute-done((bf16[512,1024]{1,0:T(8,128)(2,1)}, bf16[512,1024]{1,0:T(8,128)(2,1)}, u32[]{:S(2)}, u32[]{:S(2)}) %collective-permute-start.1) | collective-permute-done | bytes 1048608 | tf_op jit(solution)/shard_map/ppermute | solution.py:956
  97.9 19.8 %all-to-all-done.refs_1_ = bf16[4,512,384]{2,1,0:T(8,128)(2,1)} async-done(((bf16[4,512,384]{2,1,0:T(8,128)(2,1)}), bf16[4,512,384]{2,1,0:T(8,128)(2,1)}, u32[]{:S(2)}, u32[]{:S(2)}) %all-to-all-start) | async-done | bytes 1572896 | tf_op jit(solution)/shard_map/all_to_all | solution.py:1059
  128.4 9.9 %all-to-all-done.2.refs_3_ = bf16[4,256,384]{2,1,0:T(8,128)(2,1)S(1)} async-done(((bf16[4,256,384]{2,1,0:T(8,128)(2,1)}), bf16[4,256,384]{2,1,0:T(8,128)(2,1)S(1)}, u32[]{:S(2)}, u32[]{:S(2)}) %all-to-all-start.2) | async-done | bytes 786464 | tf_op jit(solution)/shard_map/all_to_all | solution.py:1059
  142.9 6.3 fusion.14
  151.9 24.1 %all-to-all-done.1.refs_2_ = bf16[4,512,384]{2,1,0:T(8,128)(2,1)} async-done(((bf16[4,512,384]{2,1,0:T(8,128)(2,1)}), bf16[4,512,384]{2,1,0:T(8,128)(2,1)}, u32[]{:S(2)}, u32[]{:S(2)}) %all-to-all-start.1) | async-done | bytes 1572896 | tf_op jit(solution)/shard_map/all_to_all | solution.py:1059
  176.0 63.0 %attention_forward.1 = (bf16[5120,128]{1,0:T(8,128)(2,1)}, f32[5120,128]{1,0:T(8,128)}) custom-call(s32[1,20]{1,0:T(1,128)} %refs_0_.3, bf16[4,512,384]{2,1,0:T(8,128)(2,1)} %all-to-all-done.refs_1_, bf16[4,512,384]{2,1,0:T(8,128)(2,1)} %all-to-all-done.1.refs_2_, bf16[4,256,384]{2,1,0:T(8,128)(2,1)} %copy-done.46), custom_call_target="tpu_custom_call" | custom-call | flops 10200547328 | bytes 7864320 | tf_op jit(solution)/shard_map/attention_forward/pallas_call | solution.py:459
  251.7 20.0 %all-to-all-done.3.heads = bf16[8,640,128]{2,1,0:T(8,128)(2,1)S(1)} async-done(((bf16[8,640,128]{2,1,0:T(8,128)(2,1)}), bf16[8,640,128]{2,1,0:T(8,128)(2,1)S(1)}, u32[]{:S(2)}, u32[]{:S(2)}) %all-to-all-start.3) | async-done | bytes 1310752 | tf_op jit(solution)/shard_map/all_to_all | solution.py:1066
  277.1 60.6 %middle_section.1 = (bf16[640,1024]{1,0:T(8,128)(2,1)}, f32[640,1024]{1,0:T(8,128)}, bf16[640,1024]{1,0:T(8,128)(2,1)}, bf16[640,1024]{1,0:T(8,128)(2,1)}, bf16[...) custom-call(s32[2]{0:T(128)} %pad_add_fusion.meta, ...), custom_call_target="tpu_custom_call" | custom-call | flops 24830279680 | bytes 43319296 | tf_op jit(solution)/shard_map/middle_section/pallas_call | solution.py:845
  383.9 22.1 %collective-permute-done.3 = bf16[640,1024]{1,0:T(8,128)(2,1)} collective-permute-done((bf16[640,1024]{1,0:T(8,128)(2,1)}, bf16[640,1024]{1,0:T(8,128)(2,1)}, u32[]{:S(2)}, u32[]{:S(2)}) %collective-permute-start.3) | collective-permute-done | bytes 1310752 | tf_op jit(solution)/shard_map/ppermute | solution.py:956
  429.1 78.2 %attention_backward.1 = bf16[5120,384]{1,0:T(8,128)(2,1)} custom-call(s32[1,20]{1,0:T(1,128)} %refs_0_.3, bf16[4,512,384]{2,1,0:T(8,128)(2,1)} %all-to-all-done.refs_1_, bf16[4,512,384]{2,1,0:T(8,128)(2,1)} %all-to-all-done.1.refs_2_, bf16[4,256,384]{2,1,0:T(8,128)(2,1)} %copy-done.46, bf16[5120,128]{1,0:T(8,128)(2,1)} %bitcast.10.refs_4_, ...), custom_call_target="tpu_custom_call" | custom-call | flops 25501368320 | bytes 15728640 | tf_op jit(solution)/shard_map/attention_backward/pallas_call | solution.py:607
  520.4 52.9 %collective-permute-done.23 = bf16[256,1408]{1,0:T(8,128)(2,1)S(1)} collective-permute-done((bf16[256,1408]{1,0:T(8,128)(2,1)S(1)}, bf16[256,1408]{1,0:T(8,128)(2,1)S(1)}, u32[]{:S(2)}, u32[]{:S(2)}) %collective-permute-start.23) | collective-permute-done | bytes 720928 | tf_op jit(solution)/shard_map/ppermute | solution.py:956
  576.6 15.8 %collective-permute-done.27 = bf16[256,1408]{1,0:T(8,128)(2,1)S(1)} collective-permute-done((bf16[256,1408]{1,0:T(8,128)(2,1)S(1)}, bf16[256,1408]{1,0:T(8,128)(2,1)S(1)}, u32[]{:S(2)}, u32[]{:S(2)}) %collective-permute-start.27) | collective-permute-done | bytes 720928 | tf_op jit(solution)/shard_map/ppermute | solution.py:956
  594.6 11.3 %collective-permute-done.24 = bf16[256,1408]{1,0:T(8,128)(2,1)S(1)} collective-permute-done((bf16[256,1408]{1,0:T(8,128)(2,1)S(1)}, bf16[256,1408]{1,0:T(8,128)(2,1)S(1)}, u32[]{:S(2)}, u32[]{:S(2)}) %collective-permute-start.24) | collective-permute-done | bytes 720928 | tf_op jit(solution)/shard_map/ppermute | solution.py:956
  615.4 6.2 input_back.3
  622.8 6.4 input_back.2
  637.2 12.9 %collective-permute-done.14 = bf16[640,1024]{1,0:T(8,128)(2,1)S(1)} collective-permute-done((bf16[640,1024]{1,0:T(8,128)(2,1)}, bf16[640,1024]{1,0:T(8,128)(2,1)S(1)}, u32[]{:S(2)}, u32[]{:S(2)}) %collective-permute-start.14) | collective-permute-done | bytes 1310752 | tf_op jit(solution)/shard_map/ppermute | solution.py:956
  660.6 11.1 %all-reduce.13.cloned.1.call-done = (bf16[256,1408]{1,0:T(8,128)(2,1)}, bf16[256,1408]{1,0:T(8,128)(2,1)}) async-done(((bf16[256,1408]{1,0:T(8,128)(2,1)}, bf16[256,1408]{1,0:T(8,128)(2,1)}), (bf16[256,1408]{1,0:T(8,128)(2,1)}, bf16[256,1408]{1,0:T(8,128)(2,1)})) %all-reduce.13.cloned.1.call-update) | async-done | bytes 1441808 | tf_op jit(solution)/shard_map/psum | solution.py:1136
  697.0 9.5 %collective-permute-done.39 = bf16[256,1408]{1,0:T(8,128)(2,1)} collective-permute-done((bf16[256,1408]{1,0:T(8,128)(2,1)}, bf16[256,1408]{1,0:T(8,128)(2,1)}, u32[]{:S(2)}, u32[]{:S(2)}) %collective-permute-start.39) | collective-permute-done | bytes 720928 | tf_op jit(solution)/shard_map/ppermute | solution.py:956
  708.9 12.9 %collective-permute-done.19 = bf16[256,1536]{1,0:T(8,128)(2,1)S(1)} collective-permute-done((bf16[256,1536]{1,0:T(8,128)(2,1)S(1)}, bf16[256,1536]{1,0:T(8,128)(2,1)S(1)}, u32[]{:S(2)}, u32[]{:S(2)}) %collective-permute-start.19) | collective-permute-done | bytes 786464 | tf_op jit(solution)/shard_map/ppermute | solution.py:956
  745.8 10.9 %copy.34 = f32[1280,2,512]{2,1,0:T(2,128)} copy(f32[1280,2,512]{2,0,1:T(8,128)S(1)} %fusion.13) | data formatting | bytes 10485760
  766.6 6.9 collective-permute-done.17
  782.9 30.3 %all-reduce.9.cloned.1.call-done = bf16[256,1024]{1,0:T(8,128)(2,1)} async-done(((bf16[256,1024]{1,0:T(8,128)(2,1)}), bf16[256,1024]{1,0:T(8,128)(2,1)}) %all-reduce.9.cloned.1.call-update) | async-done | bytes 524304 | tf_op jit(solution)/shard_map/psum | solution.py:1180
  816.4 9.7 %collective-permute-done.28 = bf16[256,1024]{1,0:T(8,128)(2,1)S(1)} collective-permute-done((bf16[256,1024]{1,0:T(8,128)(2,1)}, bf16[256,1024]{1,0:T(8,128)(2,1)S(1)}, u32[]{:S(2)}, u32[]{:S(2)}) %collective-permute-start.28) | collective-permute-done | bytes 524320 | tf_op jit(solution)/shard_map/ppermute | solution.py:956
  (357 shorter events, 289.8 us)
Async XLA Ops:
  7.2 264.5 %all-gather.5.cloned.1.call-start = ((), (), s32[]{:S(2)}) async-start(), calls=%async_computation.6 | async-start | bytes 2359296 | tf_op jit(solution)/shard_map/all_gather | solution.py:1046
  75.4 196.3 %all-gather.11.cloned.1.call-start = ((), (), s32[]{:S(2)}) async-start(), calls=%async_computation.9 | async-start | bytes 6488064 | tf_op jit(solution)/shard_map/all_gather | solution.py:1046
  76.1 195.5 %all-gather.7.cloned.1.call-start = ((), (), s32[]{:S(2)}) async-start(), calls=%async_computation.7 | async-start | bytes 6488064 | tf_op jit(solution)/shard_map/all_gather | solution.py:1046
  76.9 200.2 %all-gather.9.cloned.1.call-start = ((), (), s32[]{:S(2)}) async-start(), calls=%async_computation.8 | async-start | bytes 6488064 | tf_op jit(solution)/shard_map/all_gather | solution.py:1046
  365.3 49.1 %collective-permute-start.9 = (bf16[704,1024]{1,0:T(8,128)(2,1)}, bf16[704,1024]{1,0:T(8,128)(2,1)S(1)}, u32[]{:S(2)}, u32[]{:S(2)}) collective-permute-start(bf16[704,1024]{1,0:T(8,128)(2,1)} %constant_dynamic-slice_fusion.12), channel_id=1, source_target_pairs={{0,2},{2,0},{1,3},{3,1},{4,6},{6,4},{5,7},{7,5},{8,10},{10,8},{9,1... | collective-permute-start | bytes 4325384 | tf_op jit(solution)/shard_map/ppermute | solution.py:956
  366.8 44.1 %collective-permute-start.7 = (bf16[512,1408]{1,0:T(8,128)(2,1)}, bf16[512,1408]{1,0:T(8,128)(2,1)}, u32[]{:S(2)}, u32[]{:S(2)}) collective-permute-start(bf16[512,1408]{1,0:T(8,128)(2,1)} %constant_dynamic-slice_fusion.14), channel_id=1, source_target_pairs={{0,2},{2,0},{1,3},{3,1},{4,6},{6,4},{5,7},{7,5},{8,10},{10,8},{9,1... | collective-permute-start | bytes 4325384 | tf_op jit(solution)/shard_map/ppermute | solution.py:956
  372.0 51.0 %all-to-all-start.4 = ((bf16[8,640,128]{2,1,0:T(8,128)(2,1)}), bf16[8,640,128]{2,1,0:T(8,128)(2,1)}, u32[]{:S(2)}, u32[]{:S(2)}) async-start(bf16[8,640,128]{2,1,0:T(8,128)(2,1)} %get-tuple-element.82), calls=%async_computation.4 | async-start | bytes 2621440 | tf_op jit(solution)/shard_map/all_to_all | solution.py:1089
  425.0 93.3 %collective-permute-start.26 = (bf16[256,1408]{1,0:T(8,128)(2,1)}, bf16[256,1408]{1,0:T(8,128)(2,1)}, u32[]{:S(2)}, u32[]{:S(2)}) collective-permute-start(bf16[256,1408]{1,0:T(8,128)(2,1)} %constant_dynamic-slice_fusion), channel_id=1, source_target_pairs={{0,4},{4,0},{1,5},{5,1},{2,6},{6,2},{3,7},{7,3},{8,12},{12,8},{9,1... | collective-permute-start | bytes 2162696 | tf_op jit(solution)/shard_map/ppermute | solution.py:956
  428.5 148.1 %collective-permute-start.25 = (bf16[256,1408]{1,0:T(8,128)(2,1)}, bf16[256,1408]{1,0:T(8,128)(2,1)}, u32[]{:S(2)}, u32[]{:S(2)}) collective-permute-start(bf16[256,1408]{1,0:T(8,128)(2,1)} %constant_dynamic-slice_fusion.1), channel_id=1, source_target_pairs={{0,4},{4,0},{1,5},{5,1},{2,6},{6,2},{3,7},{7,3},{8,12},{12,8},{9,1... | collective-permute-start | bytes 2162696 | tf_op jit(solution)/shard_map/ppermute | solution.py:956
  507.2 103.0 %all-to-all-start.5 = ((bf16[4,1280,384]{2,1,0:T(8,128)(2,1)}), bf16[4,1280,384]{2,1,0:T(8,128)(2,1)}, u32[]{:S(2)}, u32[]{:S(2)}) async-start(bf16[4,1280,384]{2,1,0:T(8,128)(2,1)} %bitcast.47), calls=%async_computation.5 | async-start | bytes 7864320 | tf_op jit(solution)/shard_map/all_to_all | solution.py:1127
  512.0 159.7 %all-reduce.13.cloned.1.call-start = ((), (), s32[]{:S(2)}) async-start(), calls=%async_computation.13 | async-start | bytes 2883584 | tf_op jit(solution)/shard_map/psum | solution.py:1136
  513.6 59.7 %collective-permute-start.23 = (bf16[256,1408]{1,0:T(8,128)(2,1)S(1)}, bf16[256,1408]{1,0:T(8,128)(2,1)S(1)}, u32[]{:S(2)}, u32[]{:S(2)}) collective-permute-start(bf16[256,1408]{1,0:T(8,128)(2,1)S(1)} %constant_dynamic-slice_fusion.2), channel_id=1, source_target_pairs={{0,4},{4,0},{1,5},{5,1},{2,6},{6,2},{3,7},{7,3},{8,12},{12,8},{9,1... | collective-permute-start | bytes 2162696 | tf_op jit(solution)/shard_map/ppermute | solution.py:956
  516.8 77.8 %collective-permute-start.22 = (bf16[256,1408]{1,0:T(8,128)(2,1)S(1)}, bf16[256,1408]{1,0:T(8,128)(2,1)S(1)}, u32[]{:S(2)}, u32[]{:S(2)}) collective-permute-start(bf16[256,1408]{1,0:T(8,128)(2,1)S(1)} %constant_dynamic-slice_fusion.3), channel_id=1, source_target_pairs={{0,4},{4,0},{1,5},{5,1},{2,6},{6,2},{3,7},{7,3},{8,12},{12,8},{9,1... | collective-permute-start | bytes 2162696 | tf_op jit(solution)/shard_map/ppermute | solution.py:956
  517.0 57.8 %collective-permute-start.13 = (bf16[256,1024]{1,0:T(8,128)(2,1)S(1)}, bf16[256,1024]{1,0:T(8,128)(2,1)S(1)}, u32[]{:S(2)}, u32[]{:S(2)}) collective-permute-start(bf16[256,1024]{1,0:T(8,128)(2,1)S(1)} %copy-done.51), channel_id=1, source_target_pairs={{0,1},{1,0},{2,3},{3,2},{4,5},{5,4},{6,7},{7,6},{8,9},{9,8},{10,11... | collective-permute-start | bytes 1572872 | tf_op jit(solution)/shard_map/ppermute | solution.py:956
  518.3 88.8 %collective-permute-start.12 = (bf16[704,1024]{1,0:T(8,128)(2,1)}, bf16[704,1024]{1,0:T(8,128)(2,1)}, u32[]{:S(2)}, u32[]{:S(2)}) collective-permute-start(bf16[704,1024]{1,0:T(8,128)(2,1)} %add_convert_fusion.3), channel_id=1, source_target_pairs={{0,1},{1,0},{2,3},{3,2},{4,5},{5,4},{6,7},{7,6},{8,9},{9,8},{10,11... | collective-permute-start | bytes 4325384 | tf_op jit(solution)/shard_map/ppermute | solution.py:956
  607.1 117.7 %all-reduce.11.cloned.1.call-start = ((), (), s32[]{:S(2)}) async-start(), calls=%async_computation.12 | async-start | bytes 1966080 | tf_op jit(solution)/shard_map/psum | solution.py:1141
  614.0 44.3 %collective-permute-start.20 = (bf16[352,1024]{1,0:T(8,128)(2,1)}, bf16[352,1024]{1,0:T(8,128)(2,1)}, u32[]{:S(2)}, u32[]{:S(2)}) collective-permute-start(bf16[352,1024]{1,0:T(8,128)(2,1)} %constant_dynamic-slice_fusion.5), channel_id=1, source_target_pairs={{0,4},{4,0},{1,5},{5,1},{2,6},{6,2},{3,7},{7,3},{8,12},{12,8},{9,1... | collective-permute-start | bytes 2162696 | tf_op jit(solution)/shard_map/ppermute | solution.py:956
  673.8 100.7 %all-reduce.7.cloned.1.call-start = ((), (), s32[]{:S(2)}) async-start(), calls=%async_computation.10 | async-start | bytes 1572864 | tf_op jit(solution)/shard_map/psum | solution.py:1160
  685.3 51.6 %collective-permute-start.15 = (bf16[640,1024]{1,0:T(8,128)(2,1)}, bf16[640,1024]{1,0:T(8,128)(2,1)}, u32[]{:S(2)}, u32[]{:S(2)}) collective-permute-start(bf16[640,1024]{1,0:T(8,128)(2,1)} %add_convert_fusion.9), channel_id=1, source_target_pairs={{0,1},{1,0},{2,3},{3,2},{4,5},{5,4},{6,7},{7,6},{8,9},{9,8},{10,11... | collective-permute-start | bytes 3932168 | tf_op jit(solution)/shard_map/ppermute | solution.py:956
  697.0 59.7 %collective-permute-start.42 = (bf16[512,1408]{1,0:T(8,128)(2,1)}, bf16[512,1408]{1,0:T(8,128)(2,1)}, u32[]{:S(2)}, u32[]{:S(2)}) collective-permute-start(bf16[512,1408]{1,0:T(8,128)(2,1)} %pad_maximum_fusion.3), channel_id=1, source_target_pairs={{0,2},{2,0},{1,3},{3,1},{4,6},{6,4},{5,7},{7,5},{8,10},{10,8},{9,1... | collective-permute-start | bytes 4325384 | tf_op jit(solution)/shard_map/ppermute | solution.py:956
  728.8 51.4 %collective-permute-start.43 = (bf16[352,1024]{1,0:T(8,128)(2,1)}, bf16[352,1024]{1,0:T(8,128)(2,1)}, u32[]{:S(2)}, u32[]{:S(2)}) collective-permute-start(bf16[352,1024]{1,0:T(8,128)(2,1)} %get-tuple-element.119), channel_id=1, source_target_pairs={{0,4},{4,0},{1,5},{5,1},{2,6},{6,2},{3,7},{7,3},{8,12},{12,8},{9,1... | collective-permute-start | bytes 2162696 | tf_op jit(solution)/shard_map/ppermute | solution.py:956
  729.4 83.8 %all-reduce.9.cloned.1.call-start = ((), (), s32[]{:S(2)}) async-start(), calls=%async_computation.11 | async-start | bytes 1048576 | tf_op jit(solution)/shard_map/psum | solution.py:1180
  736.9 89.5 %collective-permute-start.38 = (bf16[256,1024]{1,0:T(8,128)(2,1)}, bf16[256,1024]{1,0:T(8,128)(2,1)}, u32[]{:S(2)}, u32[]{:S(2)}) collective-permute-start(bf16[256,1024]{1,0:T(8,128)(2,1)} %pad_maximum_fusion.6), channel_id=1, source_target_pairs={{0,2},{2,0},{1,3},{3,1},{4,6},{6,4},{5,7},{7,5},{8,10},{10,8},{9,1... | collective-permute-start | bytes 1572872 | tf_op jit(solution)/shard_map/ppermute | solution.py:956
  782.9 46.3 %collective-permute-start.44 = (bf16[704,1024]{1,0:T(8,128)(2,1)}, bf16[704,1024]{1,0:T(8,128)(2,1)}, u32[]{:S(2)}, u32[]{:S(2)}) collective-permute-start(bf16[704,1024]{1,0:T(8,128)(2,1)} %pad_maximum_fusion.4), channel_id=1, source_target_pairs={{0,2},{2,0},{1,3},{3,1},{4,6},{6,4},{5,7},{7,5},{8,10},{10,8},{9,1... | collective-permute-start | bytes 4325384 | tf_op jit(solution)/shard_map/ppermute | solution.py:956
  (100 other events, 1474.9 us)
Sparse Core Ops, SparseCore 0:
  75.5 34.3 all-gather.4
  111.8 61.8 all-gather.10
  176.2 43.6 all-gather.6
  222.2 54.8 all-gather.8
  607.3 64.4 all-reduce.12
  674.6 50.1 all-reduce.10
  729.5 42.9 all-reduce.6
  776.1 37.0 all-reduce.8

commit v2 on v1

--- a/solution.py
+++ b/solution.py
@@ -346,17 +346,6 @@
             role[TRUNK + BRANCH + b * LEAVES + leaf] = child[role[TRUNK + b] * BRANCH + leaf]
 
 
-def token_parts(refs):
-    owners = refs[0].shape[0]
-    rows = sum(ref.shape[1] for ref in refs)
-    base = 0
-    for ref in refs:
-        for owner in range(owners):
-            for at in range(0, ref.shape[1], SEG):
-                yield ref, owner, at, (owner * rows + base + at) // SEG
-        base += ref.shape[1]
-
-
 def heads_apart(values, first):
     zero = jnp.zeros_like(values)
     return jnp.concatenate(
@@ -364,25 +353,23 @@
     )
 
 
-def attention_kernel(n_parts, *refs):
-    parents = refs[0]
-    parts = refs[1 : 1 + n_parts]
-    out, logsum, qr, kr, v0, v1, kept, acc, top, total, child, count, role, place = refs[
-        1 + n_parts :
-    ]
+def attention_kernel(
+    parents, parts, out, logsum, qr, kr, v0, v1, kept, acc, top, total, child, count, role
+):
     find_roles(parents, child, count, role)
-    for i in range(SEGS):
-        place[role[i]] = i
     first = lax.broadcasted_iota(jnp.int32, (SEG, WIDE), 1) < DH
-    for ref, owner, at, seg in token_parts(parts):
-        here = segment(place[seg])
-        block = slice(at, at + SEG)
-        qr[here, :] = ref[owner, block, 0:WIDE] * jnp.asarray(DH**-0.5, BF16)
-        kr[here, :] = ref[owner, block, WIDE : 2 * WIDE]
-        value = ref[owner, block, 2 * WIDE : 3 * WIDE]
+
+    def sort(i, _):
+        here, source = segment(i), segment(role[i])
+        qr[here, :] = parts[source, 0:WIDE] * jnp.asarray(DH**-0.5, BF16)
+        kr[here, :] = parts[source, WIDE : 2 * WIDE]
+        value = parts[source, 2 * WIDE : 3 * WIDE]
         zero = jnp.zeros_like(value)
         v0[here, :] = jnp.where(first, value, zero)
         v1[here, :] = jnp.where(first, zero, value)
+        return 0
+
+    lax.fori_loop(0, SEGS, sort, 0)
     row = lax.broadcasted_iota(jnp.int32, (2 * SEG, SEG), 0)
     col = lax.broadcasted_iota(jnp.int32, (2 * SEG, SEG), 1)
     causal = col <= jnp.where(row >= SEG, row - SEG, row)
@@ -457,12 +444,12 @@
     tokens = SEGS * SEG
     vmem = pl.BlockSpec(memory_space=pltpu.VMEM)
     return pl.pallas_call(
-        functools.partial(attention_kernel, len(parts)),
+        attention_kernel,
         out_shape=(
             jax.ShapeDtypeStruct((tokens, WIDE), BF16),
             jax.ShapeDtypeStruct((tokens, WIDE), F32),
         ),
-        in_specs=[pl.BlockSpec(memory_space=pltpu.SMEM)] + [vmem] * len(parts),
+        in_specs=[pl.BlockSpec(memory_space=pltpu.SMEM), vmem],
         out_specs=(vmem, vmem),
         scratch_shapes=[pltpu.VMEM((tokens, WIDE), BF16)] * 4
         + [
@@ -473,7 +460,6 @@
             pltpu.SMEM((SEGS * BRANCH,), jnp.int32),
             pltpu.SMEM((SEGS,), jnp.int32),
             pltpu.SMEM((SEGS,), jnp.int32),
-            pltpu.SMEM((SEGS,), jnp.int32),
         ],
         compiler_params=pltpu.CompilerParams(vmem_limit_bytes=VMEM_BYTES),
         cost_estimate=pl.CostEstimate(
@@ -482,7 +468,7 @@
             transcendentals=152 * 2 * SEG * SEG,
         ),
         name="attention_forward",
-    )(parents, *parts)
+    )(parents, parts.reshape(tokens, 3 * WIDE))
 
 
 def swap_halves(values, low):
@@ -491,42 +477,41 @@
     )
 
 
-def attention_back_kernel(n_parts, *refs):
-    parents = refs[0]
-    parts = refs[1 : 1 + n_parts]
-    (
-        upstream,
-        attended,
-        logsum,
-        cosine,
-        sine,
-        out,
-        qr,
-        kr,
-        vr,
-        kt,
-        dk,
-        dv,
-        dqt,
-        child,
-        count,
-        role,
-        place,
-    ) = refs[1 + n_parts :]
+def attention_back_kernel(
+    parents,
+    parts,
+    upstream,
+    attended,
+    logsum,
+    cosine,
+    sine,
+    out,
+    qr,
+    kr,
+    vr,
+    kt,
+    dk,
+    dv,
+    dqt,
+    child,
+    count,
+    role,
+):
     find_roles(parents, child, count, role)
-    for i in range(SEGS):
-        place[role[i]] = i
     lane = lax.broadcasted_iota(jnp.int32, (SEG, WIDE), 1)
     first = lane < DH
     low = (lane % DH) < (DH // 2)
-    for ref, owner, at, seg in token_parts(parts):
-        here = segment(place[seg])
-        block = slice(at, at + SEG)
-        qr[here, :] = ref[owner, block, 0:WIDE] * jnp.asarray(DH**-0.5, BF16)
-        key = ref[owner, block, WIDE : 2 * WIDE]
+
+    def sort(i, _):
+        here, source = segment(i), segment(role[i])
+        qr[here, :] = parts[source, 0:WIDE] * jnp.asarray(DH**-0.5, BF16)
+        key = parts[source, WIDE : 2 * WIDE]
         kr[here, :] = key
         kt[:, here] = key.T
-        vr[here, :] = ref[owner, block, 2 * WIDE : 3 * WIDE]
+        vr[here, :] = parts[source, 2 * WIDE : 3 * WIDE]
+        return 0
+
+    lax.fori_loop(0, SEGS, sort, 0)
     dk[...] = jnp.zeros_like(dk)
     dv[...] = jnp.zeros_like(dv)
     key_at = lax.broadcasted_iota(jnp.int32, (SEG, 2 * SEG), 0)
@@ -605,9 +590,9 @@
     tokens = SEGS * SEG
     vmem = pl.BlockSpec(memory_space=pltpu.VMEM)
     return pl.pallas_call(
-        functools.partial(attention_back_kernel, len(parts)),
+        attention_back_kernel,
         out_shape=jax.ShapeDtypeStruct((tokens, 3 * WIDE), BF16),
-        in_specs=[pl.BlockSpec(memory_space=pltpu.SMEM)] + [vmem] * (len(parts) + 5),
+        in_specs=[pl.BlockSpec(memory_space=pltpu.SMEM)] + [vmem] * 6,
         out_specs=vmem,
         scratch_shapes=[pltpu.VMEM((tokens, WIDE), BF16)] * 3
         + [pltpu.VMEM((WIDE, tokens), BF16)]
@@ -615,7 +600,6 @@
         + [
             pltpu.VMEM((WIDE, 2 * SEG), F32),
             pltpu.SMEM((SEGS * BRANCH,), jnp.int32),
-            pltpu.SMEM((SEGS,), jnp.int32),
             pltpu.SMEM((SEGS,), jnp.int32),
             pltpu.SMEM((SEGS,), jnp.int32),
         ],
@@ -626,7 +610,7 @@
             transcendentals=152 * 2 * SEG * SEG,
         ),
         name="attention_backward",
-    )(parents, *parts, upstream, attended, logsum, cosine, sine)
+    )(parents, parts.reshape(tokens, 3 * WIDE), upstream, attended, logsum, cosine, sine)
 
 
 def angle_tables(positions):
@@ -637,55 +621,135 @@
     return jnp.cos(angle), jnp.sin(angle) * sign[None, :]
 
 
-def project_kernel(mine, theirs, gain, query_w, key_w, value_w, cosine, sine, out, low_out):
-    total = mine[...].astype(F32) + theirs[...].astype(F32)
-    scale = lax.rsqrt(jnp.mean(total * total, axis=-1, keepdims=True) + EPSILON)
-    rounded = (total * scale * gain[...]).astype(BF16)
-    low_out[...] = rounded
-    low = (lax.broadcasted_iota(jnp.int32, (total.shape[0], WIDE), 1) % DH) < (DH // 2)
-    for at, weight in enumerate((query_w, key_w, value_w)):
-        raw = nn(rounded, weight[...])
-        for peer in range(out.shape[0]):
-            part = raw[:, peer * WIDE : (peer + 1) * WIDE]
-            if at < 2:
-                part = part * cosine[...] + swap_halves(part, low) * sine[...]
-            out[peer, :, at * WIDE : (at + 1) * WIDE] = part.astype(BF16)
-
-
-def project(mine, theirs, gain, query_w, key_w, value_w, cosine, sine):
+MESH = pl.DeviceIdType.MESH
+
+
+def neighbours():
+    x, core = lax.axis_index("x"), lax.axis_index("core")
+    others = []
+    for step in (1, 2, 3):
+        to_x = lax.rem(x + step // 2, 2)
+        to_core = lax.rem(core + step % 2, 2)
+        others.append((2 * to_x + to_core, {"x": to_x, "core": to_core}))
+    return 2 * x + core, others
+
+
+def greet(tensor_peer, others):
+    barrier = pltpu.get_barrier_semaphore()
+    for target in [tensor_peer] + [where for _, where in others]:
+        pl.semaphore_signal(barrier, inc=1, device_id=target, device_id_type=MESH)
+    pl.semaphore_wait(barrier, 1 + len(others))
+
+
+def enter_kernel(
+    mine,
+    gain,
+    query_w,
+    key_w,
+    value_w,
+    cosine,
+    sine,
+    parts,
+    low_out,
+    theirs,
+    ready,
+    swap_send,
+    swap_recv,
+    part_send,
+    part_recv,
+):
+    me, others = neighbours()
+    tensor_peer = {"tensor": 1 - lax.axis_index("tensor")}
+    greet(tensor_peer, others)
+    steps = mine.shape[0] // SEG
+
+    def exchange(i):
+        return pltpu.make_async_remote_copy(
+            src_ref=mine.at[segment(i)],
+            dst_ref=theirs.at[segment(i)],
+            send_sem=swap_send.at[i],
+            recv_sem=swap_recv.at[i],
+            device_id=tensor_peer,
+            device_id_type=MESH,
+        )
+
+    def scatter(i, at):
+        place, where = others[at]
+        return pltpu.make_async_remote_copy(
+            src_ref=ready.at[place, segment(i)],
+            dst_ref=parts.at[me, segment(i)],
+            send_sem=part_send.at[i, at],
+            recv_sem=part_recv.at[i, at],
+            device_id=where,
+            device_id_type=MESH,
+        )
+
+    for i in range(steps):
+        exchange(i).start()
+    low = (lax.broadcasted_iota(jnp.int32, (SEG, WIDE), 1) % DH) < (DH // 2)
+
+    def step(i, _):
+        here = segment(i)
+        exchange(i).wait_recv()
+        total = mine[here, :].astype(F32) + theirs[here, :].astype(F32)
+        scale = lax.rsqrt(jnp.mean(total * total, axis=-1, keepdims=True) + EPSILON)
+        rounded = (total * scale * gain[...]).astype(BF16)
+        low_out[here, :] = rounded
+        for at, weight in enumerate((query_w, key_w, value_w)):
+            raw = nn(rounded, weight[...])
+            for peer in range(ready.shape[0]):
+                part = raw[:, peer * WIDE : (peer + 1) * WIDE]
+                if at < 2:
+                    part = part * cosine[here, :] + swap_halves(part, low) * sine[here, :]
+                ready[peer, here, at * WIDE : (at + 1) * WIDE] = part.astype(BF16)
+        for at in range(len(others)):
+            scatter(i, at).start()
+        parts[me, here, :] = ready[me, here, :]
+        return 0
+
+    lax.fori_loop(0, steps, step, 0)
+
+    def finish(i, _):
+        exchange(i).wait_send()
+        for at in range(len(others)):
+            scatter(i, at).wait()
+        return 0
+
+    lax.fori_loop(0, steps, finish, 0)
+
+
+def enter(mine, gain, query_w, key_w, value_w, cosine, sine):
     rows, width = mine.shape
-    block = SEG
     inner = query_w.shape[1]
     peers = inner // WIDE
-    by_row = pl.BlockSpec((block, width), lambda i: (i, 0))
-    weight = pl.BlockSpec((width, inner), lambda i: (0, 0))
-    table = pl.BlockSpec((block, WIDE), lambda i: (i, 0))
+    steps = rows // SEG
+    vmem = pl.BlockSpec(memory_space=pltpu.VMEM)
     return pl.pallas_call(
-        project_kernel,
-        grid=(rows // block,),
+        enter_kernel,
         out_shape=(
             jax.ShapeDtypeStruct((peers, rows, 3 * WIDE), BF16),
             jax.ShapeDtypeStruct((rows, width), BF16),
+            jax.ShapeDtypeStruct((rows, width), BF16),
         ),
-        in_specs=[
-            by_row,
-            by_row,
-            pl.BlockSpec((1, width), lambda i: (0, 0)),
-            weight,
-            weight,
-            weight,
-            table,
-            table,
+        in_specs=[vmem] * 7,
+        out_specs=(vmem,) * 3,
+        scratch_shapes=[
+            pltpu.VMEM((peers, rows, 3 * WIDE), BF16),
+            pltpu.SemaphoreType.DMA((steps,)),
+            pltpu.SemaphoreType.DMA((steps,)),
+            pltpu.SemaphoreType.DMA((steps, 3)),
+            pltpu.SemaphoreType.DMA((steps, 3)),
         ],
-        out_specs=(pl.BlockSpec((peers, block, 3 * WIDE), lambda i: (0, i, 0)), by_row),
-        compiler_params=pltpu.CompilerParams(vmem_limit_bytes=VMEM_BYTES),
+        compiler_params=pltpu.CompilerParams(
+            vmem_limit_bytes=VMEM_BYTES, collective_id=0, has_side_effects=True
+        ),
         cost_estimate=pl.CostEstimate(
             flops=2 * rows * width * 3 * inner,
-            bytes_accessed=rows * width * 6 + 6 * width * inner + rows * inner * 6,
+            bytes_accessed=200 << 20,
             transcendentals=rows,
         ),
-        name="project",
-    )(mine, theirs, gain, query_w, key_w, value_w, cosine, sine)
+        name="enter",
+    )(mine, gain, query_w, key_w, value_w, cosine, sine)
 
 
 def middle_kernel(
@@ -697,13 +761,11 @@
     third_gain,
     fourth_gain,
     wo_own,
-    wo_all,
     wg_own,
-    wg_all,
     wu_own,
-    wu_all,
     wd_own,
-    wd_all,
+    pair_all,
+    stack_all,
     layer_out,
     middle_out,
     attended_out,
@@ -711,8 +773,7 @@
     third_out,
     mixed_out,
     hidden_out,
-    gate_out,
-    up_out,
+    pair_out,
     heads_back,
     gains_out,
     wo,
@@ -727,27 +788,33 @@
     step = pl.program_id(0)
     tensor = meta[0]
     copies = []
-    for weight, own, all_of, by_lane in (
-        (wo, wo_own, wo_all, False),
-        (wg, wg_own, wg_all, True),
-        (wu, wu_own, wu_all, True),
-        (wd, wd_own, wd_all, False),
-    ):
-        rows, lanes = own.shape
-        other = all_of.at[pl.ds(pl.multiple_of((1 - tensor) * rows, 128), rows)]
-        for src, row, lane in (
-            (own, 0, 0),
-            (other, 0 if by_lane else rows, lanes if by_lane else 0),
-        ):
-            dst = weight.at[pl.ds(row, rows), pl.ds(lane, lanes)]
-            copies.append(pltpu.make_async_copy(src, dst, sem.at[len(copies)]))
+
+    def copy(src, weight, row, lane):
+        rows, lanes = src.shape
+        dst = weight.at[pl.ds(row, rows), pl.ds(lane, lanes)]
+        copies.append(pltpu.make_async_copy(src, dst, sem.at[len(copies)]))
+
+    quarters = stack_all.shape[0] // 2
+    first_other = (1 - tensor) * quarters
+    inner, split = wo_own.shape[0], wg_own.shape[1]
+    width = wg_own.shape[0]
+    for weight, own, start in ((wo, wo_own, 0), (wd, wd_own, inner // quarters)):
+        rows = own.shape[0]
+        copy(own, weight, 0, 0)
+        for i in range(quarters):
+            piece = stack_all.at[first_other + i, pl.ds(start, rows // quarters)]
+            copy(piece, weight, rows + i * (rows // quarters), 0)
+    others = pl.ds(pl.multiple_of((1 - tensor) * width, width), width)
+    for weight, own, lane in ((wg, wg_own, 0), (wu, wu_own, split)):
+        copy(own, weight, 0, 0)
+        copy(pair_all.at[others, pl.ds(lane, split)], weight, 0, split)
 
     @pl.when(step == 0)
     def _():
         for copy in copies:
             copy.start()
         gains_out[...] = jnp.zeros_like(gains_out)
-        for copy in copies[:2]:
+        for copy in copies[: 1 + quarters]:
             copy.wait()
 
     groups = heads.shape[0] // 2
@@ -774,7 +841,7 @@
 
     @pl.when(step == 0)
     def _():
-        for copy in copies[2:]:
+        for copy in copies[1 + quarters :]:
             copy.wait()
 
     sums[...] = jnp.zeros_like(sums)
@@ -799,6 +866,7 @@
     gains_out[2:3, :] += jnp.sum(upstream * fourth_normed, axis=0, keepdims=True)
     mixed_out[...] = inward(upstream, fourth_gain[...], fourth_normed, fourth_scale).astype(BF16)
     sums[...] = jnp.zeros_like(sums)
+    side_units = wg_own.shape[1] // 128
 
     def backward(c, _):
         cut = pl.ds(pl.multiple_of(c * HIDDEN, HIDDEN), HIDDEN)
@@ -808,8 +876,13 @@
         silu = gate * sigmoid
         gate_back = (back * up_s[c] * (sigmoid + silu * (1.0 - sigmoid))).astype(BF16)
         up_back = (back * silu).astype(BF16)
-        gate_out[:, cut] = gate_back
-        up_out[:, cut] = up_back
+        for piece in range(HIDDEN // 128):
+            unit = c * (HIDDEN // 128) + piece
+            unit = jnp.where(unit < side_units, unit, unit + side_units)
+            lanes = slice(piece * 128, (piece + 1) * 128)
+            pair_out[:, pl.ds(pl.multiple_of(unit * 128, 128), 128)] = gate_back[:, lanes]
+            unit += side_units
+            pair_out[:, pl.ds(pl.multiple_of(unit * 128, 128), 128)] = up_back[:, lanes]
         sums[...] += nt(gate_back, wg[:, cut]) + nt(up_back, wu[:, cut])
         return 0
 
@@ -834,7 +907,7 @@
     rows, width = adapted.shape
     sources = heads.shape[0]
     inner = sources * WIDE
-    hidden = 2 * weights[2].shape[1]
+    hidden = 2 * weights[1].shape[1]
     block = rows // 2
     steps = rows // block
     row = pl.BlockSpec((block, width), lambda i, meta: (i, 0))
@@ -855,7 +928,7 @@
                 gain,
                 gain,
             ]
-            + [hbm] * 8,
+            + [hbm] * 6,
             out_specs=(
                 row,
                 row,
@@ -864,8 +937,7 @@
                 row,
                 row,
                 wide,
-                wide,
-                wide,
+                pl.BlockSpec((block, 2 * hidden), lambda i, meta: (i, 0)),
                 head,
                 pl.BlockSpec((8, width), lambda i, meta: (0, 0)),
             ),
@@ -877,7 +949,7 @@
                 pltpu.VMEM((hidden // HIDDEN, block, HIDDEN), F32),
                 pltpu.VMEM((hidden // HIDDEN, block, HIDDEN), F32),
                 pltpu.VMEM((block, width), F32),
-                pltpu.SemaphoreType.DMA((8,)),
+                pltpu.SemaphoreType.DMA((14,)),
             ],
         ),
         out_shape=(
@@ -888,8 +960,7 @@
             jax.ShapeDtypeStruct((rows, width), BF16),
             jax.ShapeDtypeStruct((rows, width), BF16),
             jax.ShapeDtypeStruct((rows, hidden), BF16),
-            jax.ShapeDtypeStruct((rows, hidden), BF16),
-            jax.ShapeDtypeStruct((rows, hidden), BF16),
+            jax.ShapeDtypeStruct((rows, 2 * hidden), BF16),
             jax.ShapeDtypeStruct((sources, rows, WIDE), BF16),
             jax.ShapeDtypeStruct((8, width), F32),
         ),
@@ -903,53 +974,511 @@
     )(meta, adapted, heads, cotangent, *gains, *weights)
 
 
-def input_back_kernel(meta, parts, query_w, key_w, value_w, out, joined):
+LEAVE = 128
+
+
+def leave_kernel(
+    sent,
+    adapted,
+    middle_back,
+    gain,
+    query_w,
+    key_w,
+    value_w,
+    joined,
+    adapted_low,
+    gain_out,
+    landed,
+    away,
+    away_landed,
+    part_send,
+    part_recv,
+    away_send,
+    away_recv,
+    low_send,
+    low_recv,
+):
+    me, others = neighbours()
+    tensor = lax.axis_index("tensor")
+    tensor_peer = {"tensor": 1 - tensor}
+    greet(tensor_peer, others)
+    half = adapted.shape[0]
     inner = query_w.shape[1]
-    for at in range(3):
-        for group in range(parts.shape[0]):
-            to = at * inner + group * WIDE
-            joined[:, to : to + WIDE] = parts[group, :, at * WIDE : (at + 1) * WIDE]
-    total = nt(joined[:, 0:inner], query_w[...])
-    total += nt(joined[:, inner : 2 * inner], key_w[...])
-    total += nt(joined[:, 2 * inner : 3 * inner], value_w[...])
-    out[...] = total.astype(out.dtype)
-
-
-def input_back(meta, parts, query_w, key_w, value_w, dtype):
-    groups, rows, lanes = parts.shape
-    rows = rows // 2
-    width, inner = query_w.shape
-    block = rows // 2
-    steps = 2
-    weight = pl.BlockSpec((width, inner), lambda i, meta: (0, 0))
+    steps = half // LEAVE
+
+    def block(start, i):
+        return pl.ds(pl.multiple_of(start + i * LEAVE, LEAVE), LEAVE)
+
+    def gather(side, i, at):
+        here = block((tensor if side else 1 - tensor) * half, i)
+        place, where = others[at]
+        return pltpu.make_async_remote_copy(
+            src_ref=sent.at[place, here],
+            dst_ref=landed.at[me, here],
+            send_sem=part_send.at[side, i, at],
+            recv_sem=part_recv.at[side, i, at],
+            device_id=where,
+            device_id_type=MESH,
+        )
+
+    def hand_over(i):
+        return pltpu.make_async_remote_copy(
+            src_ref=away.at[block(0, i)],
+            dst_ref=away_landed.at[block(0, i)],
+            send_sem=away_send.at[i],
+            recv_sem=away_recv.at[i],
+            device_id=tensor_peer,
+            device_id_type=MESH,
+        )
+
+    def share(i):
+        here = block(tensor * half, i)
+        return pltpu.make_async_remote_copy(
+            src_ref=adapted_low.at[here],
+            dst_ref=adapted_low.at[here],
+            send_sem=low_send.at[i],
+            recv_sem=low_recv.at[i],
+            device_id=tensor_peer,
+            device_id_type=MESH,
+        )
+
+    for side in range(2):
+
+        def begin(i, _):
+            for at in range(len(others)):
+                gather(side, i, at).start()
+            return 0
+
+        lax.fori_loop(0, steps, begin, 0)
+    landed[me] = sent[me]
+    gain_out[...] = jnp.zeros_like(gain_out)
+
+    def input_grad(side, i):
+        for at in range(len(others)):
+            gather(side, i, at).wait_recv()
+        here = block((tensor if side else 1 - tensor) * half, i)
+        for at in range(3):
+            for group in range(landed.shape[0]):
+                to = at * inner + group * WIDE
+                joined[here, to : to + WIDE] = landed[group, here, at * WIDE : (at + 1) * WIDE]
+        total = nt(joined[here, 0:inner], query_w[...])
+        total += nt(joined[here, inner : 2 * inner], key_w[...])
+        total += nt(joined[here, 2 * inner : 3 * inner], value_w[...])
+        return total
+
+    def away_step(i, _):
+        away[block(0, i), :] = input_grad(0, i).astype(BF16)
+        hand_over(i).start()
+        return 0
+
+    lax.fori_loop(0, steps, away_step, 0)
+
+    def home_step(i, _):
+        total = input_grad(1, i)
+        hand_over(i).wait_recv()
+        rows = block(0, i)
+        upstream = total + away_landed[rows, :].astype(F32)
+        values = adapted[rows, :]
+        scale = lax.rsqrt(jnp.mean(values * values, axis=-1, keepdims=True) + EPSILON)
+        normed = values * scale
+        scaled = upstream * gain[...]
+        inward = scale * (scaled - normed * jnp.mean(scaled * normed, axis=-1, keepdims=True))
+        gain_out[0:1, :] += jnp.sum(upstream * normed, axis=0, keepdims=True)
+        adapted_low[block(tensor * half, i), :] = (middle_back[rows, :] + inward).astype(BF16)
+        share(i).start()
+        return 0
+
+    lax.fori_loop(0, steps, home_step, 0)
+
+    def finish(i, _):
+        for side in range(2):
+            for at in range(len(others)):
+                gather(side, i, at).wait_send()
+        hand_over(i).wait_send()
+        share(i).wait()
+        return 0
+
+    lax.fori_loop(0, steps, finish, 0)
+
+
+def leave(sent, adapted, middle_back, gain, query_w, key_w, value_w):
+    peers, rows, lanes = sent.shape
+    half, width = adapted.shape
+    inner = query_w.shape[1]
+    steps = half // LEAVE
+    vmem = pl.BlockSpec(memory_space=pltpu.VMEM)
     return pl.pallas_call(
-        input_back_kernel,
-        grid_spec=pltpu.PrefetchScalarGridSpec(
-            num_scalar_prefetch=1,
-            grid=(steps,),
-            in_specs=[
-                pl.BlockSpec((groups, block, lanes), lambda i, meta: (0, meta[0] * steps + i, 0)),
-                weight,
-                weight,
-                weight,
-            ],
-            out_specs=(
-                pl.BlockSpec((block, width), lambda i, meta: (i, 0)),
-                pl.BlockSpec((block, 3 * inner), lambda i, meta: (i, 0)),
-            ),
+        leave_kernel,
+        out_shape=(
+            jax.ShapeDtypeStruct((rows, 3 * inner), BF16),
+            jax.ShapeDtypeStruct((rows, width), BF16),
+            jax.ShapeDtypeStruct((8, width), F32),
         ),
-        out_shape=(
-            jax.ShapeDtypeStruct((rows, width), dtype),
-            jax.ShapeDtypeStruct((rows, 3 * inner), BF16),
+        in_specs=[vmem] * 7,
+        out_specs=(vmem,) * 3,
+        scratch_shapes=[
+            pltpu.VMEM((peers, rows, lanes), BF16),
+            pltpu.VMEM((half, width), BF16),
+            pltpu.VMEM((half, width), BF16),
+            pltpu.SemaphoreType.DMA((2, steps, 3)),
+            pltpu.SemaphoreType.DMA((2, steps, 3)),
+        ]
+        + [pltpu.SemaphoreType.DMA((steps,))] * 4,
+        compiler_params=pltpu.CompilerParams(
+            vmem_limit_bytes=VMEM_BYTES, collective_id=1, has_side_effects=True
         ),
-        compiler_params=pltpu.CompilerParams(vmem_limit_bytes=VMEM_BYTES),
         cost_estimate=pl.CostEstimate(
-            flops=2 * rows * width * 3 * inner,
-            bytes_accessed=rows * inner * 12 + 6 * width * inner + rows * width * 4,
-            transcendentals=0,
+            flops=2 * rows * width * 3 * inner, bytes_accessed=200 << 20, transcendentals=rows
         ),
-        name="input_back",
-    )(meta, parts, query_w, key_w, value_w)
+        name="leave",
+    )(sent, adapted, middle_back, gain, query_w, key_w, value_w)
+
+
+class Reduction:
+    def __init__(self, shape, by_lane, halved):
+        self.rows, self.lanes = shape
+        self.by_lane = by_lane
+        self.halved = halved
+
+    def scratch(self, dp):
+        rows, lanes = self.rows, self.lanes
+        quarter = (rows // 4, lanes)
+        chunk = (rows // 4, lanes // dp) if self.by_lane else (rows // 4 // dp, lanes)
+        refs = [
+            pltpu.VMEM(quarter, BF16),
+            pltpu.VMEM(quarter, BF16),
+            pltpu.VMEM((dp + 1,) + chunk, BF16),
+            pltpu.VMEM(quarter, BF16),
+            pltpu.VMEM((3,) + quarter, BF16),
+            pltpu.VMEM(quarter, F32),
+            pltpu.SemaphoreType.DMA((5,)),
+            pltpu.SemaphoreType.DMA((5,)),
+            pltpu.SemaphoreType.DMA((dp,)),
+            pltpu.SemaphoreType.DMA((dp + 1,)),
+            pltpu.SemaphoreType.DMA((2, dp)),
+            pltpu.SemaphoreType.DMA((dp,)),
+            pltpu.SemaphoreType.DMA((4,)),
+        ]
+        if not self.halved:
+            refs += [pltpu.VMEM((rows // 2, lanes), BF16)] * 2
+        return refs
+
+    def bind(self, part, out, refs):
+        self.part, self.out = part, out
+        (
+            self.x_land,
+            self.quarter,
+            self.z_land,
+            self.whole,
+            self.others,
+            self.wide,
+            self.send,
+            self.recv,
+            self.sum_send,
+            self.sum_recv,
+            self.all_send,
+            self.all_recv,
+            self.out_sem,
+        ) = refs[:13]
+        if self.halved:
+            self.half = part
+        else:
+            self.half, self.core_land = refs[13:]
+        self.x, self.core, self.z = (lax.axis_index(name) for name in ("x", "core", "dp"))
+        self.dp = lax.axis_size("dp")
+        self.to_core = {"core": 1 - self.core}
+        self.to_x = {"x": 1 - self.x}
+        self.sends = []
+
+    def copy(self, src, dst, send, recv, where):
+        return pltpu.make_async_remote_copy(
+            src_ref=src,
+            dst_ref=dst,
+            send_sem=send,
+            recv_sem=recv,
+            device_id=where,
+            device_id_type=MESH,
+        )
+
+    def part_of(self, ref, index, rows):
+        return ref.at[pl.ds(pl.multiple_of(index * rows, rows), rows)]
+
+    def chunk(self, ref, index):
+        if self.by_lane:
+            lanes = self.lanes // self.dp
+            return ref.at[:, pl.ds(pl.multiple_of(index * lanes, lanes), lanes)]
+        return self.part_of(ref, index, self.rows // 4 // self.dp)
+
+    def core_sum(self):
+        half = self.rows // 2
+        return self.copy(
+            self.part_of(self.part, 1 - self.core, half),
+            self.core_land,
+            self.send.at[0],
+            self.recv.at[0],
+            self.to_core,
+        )
+
+    def x_sum(self):
+        quarter = self.rows // 4
+        return self.copy(
+            self.part_of(self.half, 1 - self.x, quarter),
+            self.x_land,
+            self.send.at[1],
+            self.recv.at[1],
+            self.to_x,
+        )
+
+    def z_sum(self, j, step):
+        up = {"dp": self.z + step}
+        index = j
+        lands = index if step > 0 else jnp.where(self.z - 1 == index, self.dp, index)
+        return self.copy(
+            self.chunk(self.quarter, index),
+            self.z_land.at[lands],
+            self.sum_send.at[index],
+            self.sum_recv.at[lands],
+            up,
+        )
+
+    def z_all(self, j, step):
+        return self.copy(
+            self.chunk(self.whole, j),
+            self.chunk(self.whole, j),
+            self.all_send.at[0 if step > 0 else 1, j],
+            self.all_recv.at[j],
+            {"dp": self.z + step},
+        )
+
+    def spread(self, which):
+        src = self.others.at[0] if which == 2 else self.whole
+        return self.copy(
+            src,
+            self.others.at[which],
+            self.send.at[2 + which],
+            self.recv.at[2 + which],
+            self.to_x if which == 0 else self.to_core,
+        )
+
+    def write(self, at, core, x, value):
+        quarter = self.rows // 4
+        row = pl.multiple_of((2 * core + x) * quarter, quarter)
+        return pltpu.make_async_copy(
+            self.wide, self.out.at[pl.ds(row, quarter)], self.out_sem.at[at]
+        )
+
+    def emit(self, at, core, x, ref):
+        if at > 0:
+            self.last_write.wait()
+        self.wide[...] = ref[...].astype(F32)
+        self.last_write = self.write(at, core, x, ref)
+        self.last_write.start()
+
+    def add(self, into, left, right):
+        into[...] = (left[...].astype(F32) + right[...].astype(F32)).astype(BF16)
+
+    def hop(self, h):
+        last = self.dp - 1
+
+        @pl.when(self.z == h)
+        def _():
+            for j in range(last, h, -1):
+                if h > 0:
+                    self.wait_sum(j)
+                    self.add(self.chunk(self.quarter, j), self.chunk(self.quarter, j), self.z_land.at[j])
+                self.z_sum(j, 1).start()
+
+        @pl.when(self.z == last - h)
+        def _():
+            for j in range(0, last - h):
+                if h > 0:
+                    self.wait_sum(j)
+                    self.add(self.chunk(self.quarter, j), self.chunk(self.quarter, j), self.z_land.at[j])
+                self.z_sum(j, -1).start()
+
+    def wait_sum(self, lands):
+        self.copy(
+            self.z_land.at[lands],
+            self.z_land.at[lands],
+            self.sum_send.at[0],
+            self.sum_recv.at[lands],
+            self.to_x,
+        ).wait_recv()
+
+    def all_hop(self, h):
+        z, last = self.z, self.dp - 1
+        low, high = jnp.maximum(z - h, 0), jnp.minimum(z + h, last)
+
+        @pl.when(z >= h)
+        def _():
+            self.z_all(low, 1).wait_recv()
+
+        @pl.when((z >= h) & (z < last))
+        def _():
+            self.z_all(low, 1).start()
+
+        @pl.when(z <= last - h)
+        def _():
+            self.z_all(high, -1).wait_recv()
+
+        @pl.when((z <= last - h) & (z > 0))
+        def _():
+            self.z_all(high, -1).start()
+
+    def stages(self):
+        def start():
+            if self.halved:
+                self.x_sum().start()
+            else:
+                self.core_sum().start()
+
+        def fold_core():
+            if not self.halved:
+                self.core_sum().wait_recv()
+                self.add(
+                    self.half, self.part_of(self.part, self.core, self.rows // 2), self.core_land
+                )
+                self.x_sum().start()
+
+        def fold_x():
+            self.x_sum().wait_recv()
+            self.add(
+                self.quarter, self.part_of(self.half, self.x, self.rows // 4), self.x_land
+            )
+            self.hop(0)
+
+        def settle():
+            z, last = self.z, self.dp - 1
+            mine = self.chunk(self.quarter, z)
+
+            @pl.when(z > 0)
+            def _():
+                self.wait_sum(z)
+                self.add(mine, mine, self.z_land.at[z])
+
+            @pl.when(z < last)
+            def _():
+                self.wait_sum(self.dp)
+                self.add(mine, mine, self.z_land.at[self.dp])
+
+            self.chunk(self.whole, z)[...] = mine[...]
+
+            @pl.when(z < last)
+            def _():
+                self.z_all(z, 1).start()
+
+            @pl.when(z > 0)
+            def _():
+                self.z_all(z, -1).start()
+
+        def share():
+            self.all_hop(self.dp - 1)
+            self.spread(0).start()
+            self.spread(1).start()
+            self.emit(0, self.core, self.x, self.whole)
+
+        def pass_on():
+            self.spread(0).wait_recv()
+            self.spread(2).start()
+            self.emit(1, self.core, 1 - self.x, self.others.at[0])
+
+        def last():
+            self.spread(1).wait_recv()
+            self.emit(2, 1 - self.core, self.x, self.others.at[1])
+            self.spread(2).wait_recv()
+            self.emit(3, 1 - self.core, 1 - self.x, self.others.at[2])
+
+        return (
+            [start, fold_core, fold_x]
+            + [functools.partial(self.hop, h) for h in range(1, self.dp - 1)]
+            + [settle]
+            + [functools.partial(self.all_hop, h) for h in range(1, self.dp - 1)]
+            + [share, pass_on, last]
+        )
+
+    def drain(self):
+        z, last = self.z, self.dp - 1
+        if not self.halved:
+            self.core_sum().wait_send()
+        self.x_sum().wait_send()
+        for j in range(self.dp):
+
+            @pl.when(z < j)
+            def _():
+                self.z_sum(j, 1).wait_send()
+
+            @pl.when(z > j)
+            def _():
+                self.z_sum(j, -1).wait_send()
+
+            @pl.when((z >= j) & (z < last))
+            def _():
+                self.z_all(j, 1).wait_send()
+
+            @pl.when((z <= j) & (z > 0))
+            def _():
+                self.z_all(j, -1).wait_send()
+
+        for which in range(3):
+            self.spread(which).wait_send()
+        self.last_write.wait()
+
+
+def reduce_kernel(items, *refs):
+    count = len(items)
+    parts, outs, rest = refs[:count], refs[count : 2 * count], refs[2 * count :]
+    dp = lax.axis_size("dp")
+    z = lax.axis_index("dp")
+    for item, part, out in zip(items, parts, outs):
+        size = len(item.scratch(dp))
+        item.bind(part, out, rest[:size])
+        rest = rest[size:]
+    barrier = pltpu.get_barrier_semaphore()
+    pl.semaphore_signal(barrier, inc=1, device_id=items[0].to_core, device_id_type=MESH)
+    pl.semaphore_signal(barrier, inc=1, device_id=items[0].to_x, device_id_type=MESH)
+
+    @pl.when(z > 0)
+    def _():
+        pl.semaphore_signal(barrier, inc=1, device_id={"dp": z - 1}, device_id_type=MESH)
+
+    @pl.when(z < dp - 1)
+    def _():
+        pl.semaphore_signal(barrier, inc=1, device_id={"dp": z + 1}, device_id_type=MESH)
+
+    pl.semaphore_wait(barrier, 2 + jnp.minimum(z, 1) + jnp.minimum(dp - 1 - z, 1))
+    plans = [item.stages() for item in items]
+    for time in range(len(plans[0]) + count - 1):
+        for at, plan in enumerate(plans):
+            if 0 <= time - at < len(plan):
+                plan[time - at]()
+    for item in items:
+        item.drain()
+
+
+def reduce_all(parts, kinds, name, number):
+    dp = lax.axis_size("dp")
+    items = []
+    for part, (by_lane, halved) in zip(parts, kinds):
+        rows, lanes = part.shape
+        items.append(Reduction((2 * rows if halved else rows, lanes), by_lane, halved))
+    scratch = []
+    for item in items:
+        scratch += item.scratch(dp)
+    moved = sum(item.rows * item.lanes for item in items)
+    return pl.pallas_call(
+        functools.partial(reduce_kernel, items),
+        out_shape=tuple(jax.ShapeDtypeStruct((item.rows, item.lanes), F32) for item in items),
+        in_specs=[pl.BlockSpec(memory_space=pltpu.VMEM)] * len(items),
+        out_specs=(pl.BlockSpec(memory_space=pl.ANY),) * len(items),
+        scratch_shapes=scratch,
+        compiler_params=pltpu.CompilerParams(
+            vmem_limit_bytes=VMEM_BYTES, collective_id=number, has_side_effects=True
+        ),
+        cost_estimate=pl.CostEstimate(
+            flops=moved * 4, bytes_accessed=moved * 30, transcendentals=0
+        ),
+        name=name,
+    )(*parts)
 
 
 def swap(value, axis):
@@ -1020,49 +1549,31 @@
     x = lax.axis_index("x")
     everyone = ("x", "core", "tensor")
     meta = jnp.stack([tensor, core]).astype(jnp.int32)
-    meta_other = jnp.stack([1 - tensor, core]).astype(jnp.int32)
     one_row = lambda gain: gain.reshape(1, -1)
 
     cosine, sine = angle_tables(positions)
-    cuts = [0, 2 * SEG, 4 * SEG, rows]
-    adapted_parts, low_parts, head_parts = [], [], []
-    mine = [
-        jnp.einsum(
-            "rcd,cde->re", latent_embed[start:stop], adapter, preferred_element_type=F32
-        ).astype(BF16)
-        for start, stop in zip(cuts[:-1], cuts[1:])
-    ]
-    theirs = []
-    for i in range(len(mine)):
-        if i > 0:
-            mine[i], theirs[i - 1] = together(mine[i], theirs[i - 1])
-        theirs.append(swap(mine[i], "tensor"))
-    own_weights = (output_weight, gate_weight, up_weight, down_weight)
-    pieces = [cut(weight, 2 * x + core, weight.shape[0] // 4) for weight in own_weights]
-    *pieces, theirs[-1] = together(*pieces, theirs[-1])
-    weights = []
-    for weight, piece in zip(own_weights, pieces):
-        weights.append(weight)
-        weights.append(lax.all_gather(piece, ("tensor", "x", "core"), axis=0, tiled=True))
-    for i in range(len(mine)):
-        start, stop = cuts[i], cuts[i + 1]
-        sent, low = project(
-            mine[i],
-            theirs[i],
-            one_row(first_gain),
-            query_weight,
-            key_weight,
-            value_weight,
-            cosine[start:stop],
-            sine[start:stop],
-        )
-        head_parts.append(lax.all_to_all(sent, ("x", "core"), 0, 0, tiled=False))
-        low_parts.append(low)
-        adapted_parts.append(mine[i].astype(F32) + theirs[i].astype(F32))
-    adapted = cut(jnp.concatenate(adapted_parts, axis=0), tensor, half_rows)
-    first_low = jnp.concatenate(low_parts, axis=0)
-
-    attended, logsum = attention_forward(parents, head_parts)
+    mine = jnp.einsum(
+        "rcd,cde->re", latent_embed, adapter, preferred_element_type=F32
+    ).astype(BF16)
+    parts, first_low, theirs = enter(
+        mine, one_row(first_gain), query_weight, key_weight, value_weight, cosine, sine
+    )
+    adapted = cut(mine, tensor, half_rows).astype(F32) + cut(theirs, tensor, half_rows).astype(
+        F32
+    )
+    quarter = 2 * x + core
+    pair = jnp.concatenate(
+        [cut(weight, quarter, width // 4) for weight in (gate_weight, up_weight)], axis=1
+    )
+    stack = jnp.concatenate(
+        [cut(weight, quarter, weight.shape[0] // 4) for weight in (output_weight, down_weight)],
+        axis=0,
+    )
+    pair, stack, parts = together(pair, stack, parts)
+    pair_all = lax.all_gather(pair, ("tensor", "x", "core"), axis=0, tiled=True)
+    stack_all = lax.all_gather(stack, ("tensor", "x", "core"), axis=0, tiled=False)
+
+    attended, logsum = attention_forward(parents, parts)
     heads = lax.all_to_all(
         attended.reshape(8, half_rows, WIDE), everyone, 0, 0, tiled=False
     )
@@ -1074,8 +1585,7 @@
         third_low,
         mixed_low,
         hidden,
-        gate_low,
-        up_low,
+        pair_low,
         heads_back,
         gain_parts,
     ) = middle_section(
@@ -1084,7 +1594,7 @@
         heads,
         cotangent,
         (one_row(second_gain), one_row(third_gain), one_row(fourth_gain)),
-        weights,
+        (output_weight, gate_weight, up_weight, down_weight, pair_all, stack_all),
     )
     upstream = lax.all_to_all(heads_back, everyone, 0, 0, tiled=False).reshape(-1, WIDE)
     layer_other = swap(layer_half, "tensor")
@@ -1098,96 +1608,49 @@
 
     split = gate_weight.shape[1]
     inner = output_weight.shape[0]
-    own, other = slice(None, split), slice(split, None)
-    gate_sides = [fold(tn(third_low, gate_low[:, side]), core, "core") for side in (own, other)]
-    up_sides = [fold(tn(third_low, up_low[:, side]), core, "core") for side in (own, other)]
-    down_sides = [fold(tn(hidden[:, side], mixed_low), core, "core") for side in (own, other)]
-    output_sides = [
-        fold(tn(attended_all[:, side], attention_low), core, "core")
-        for side in (slice(None, inner), slice(inner, None))
-    ]
-    upstream, *sides = together(
-        upstream, *gate_sides, *up_sides, *down_sides, *output_sides
-    )
-    gate_sides, up_sides, down_sides, output_sides = (
-        sides[0:2],
-        sides[2:4],
-        sides[4:6],
-        sides[6:8],
-    )
-    gate_sides = [fold(side, x, "x") for side in gate_sides]
-    up_sides = [fold(side, x, "x") for side in up_sides]
-    down_kept = add_low(down_sides[0], swap(down_sides[1], "tensor"))
-    output_kept = add_low(output_sides[0], swap(output_sides[1], "tensor"))
+    sides = []
+    for left, right, cut_at in (
+        (third_low, pair_low, 2 * split),
+        (hidden, mixed_low, split),
+        (attended_all, attention_low, inner),
+    ):
+        for side in (slice(None, cut_at), slice(cut_at, None)):
+            part = (
+                tn(left, right[:, side]) if right is pair_low else tn(left[:, side], right)
+            )
+            sides.append(fold(part, core, "core"))
+    upstream, *sides = together(upstream, *sides)
+    away = [swap(side, "tensor") for side in sides[1::2]]
 
     table_cosine, table_sine = angle_tables(jnp.arange((TRUNK + 2) * SEG))
     sent = attention_backward(
-        parents, head_parts, upstream, attended, logsum, table_cosine, table_sine
-    )
-    parts = lax.all_to_all(
-        sent.reshape(4, rows, 3 * WIDE), ("x", "core"), 0, 0, tiled=False
-    )
-
-    def finish(value):
-        return unfold(unfold(value, x, "x"), core, "core").astype(F32)
-
-    gate_kept = add_low(gate_sides[0], swap(gate_sides[1], "tensor"))
-    up_kept = add_low(up_sides[0], swap(up_sides[1], "tensor"))
-    gate_sum, up_sum = lax.psum((gate_kept, up_kept), "dp")
-    parts, down_kept, output_kept = together(parts, down_kept, output_kept)
-    down_kept = fold(down_kept, x, "x")
-    output_kept = fold(output_kept, x, "x")
-    down_kept, output_kept, gate_sum, up_sum = together(down_kept, output_kept, gate_sum, up_sum)
-    down_sum, output_sum = lax.psum((down_kept, output_kept), "dp")
-
-    away, joined_away = input_back(
-        meta_other, parts, query_weight, key_weight, value_weight, BF16
-    )
-    home, joined_home = input_back(meta, parts, query_weight, key_weight, value_weight, F32)
-    away = swap(away, "tensor")
-    first_low_home = cut(first_low, tensor, half_rows)
-    first_low_away = cut(first_low, 1 - tensor, half_rows)
-    input_part = (
-        lax.dot_general(
-            first_low_home, joined_home, (((0,), (0,)), ((), ())), preferred_element_type=F32
-        )
-        + lax.dot_general(
-            first_low_away, joined_away, (((0,), (0,)), ((), ())), preferred_element_type=F32
-        )
-    ).astype(BF16)
-    input_kept = fold(fold(input_part, core, "core"), x, "x")
-    input_kept, down_sum, output_sum = together(input_kept, down_sum, output_sum)
-    input_sum = lax.psum(input_kept, "dp")
-    first_back = home + away.astype(F32)
-    first_out, first_normed, first_scale = normalize(adapted, first_gain)
-    adapted_part, first_gain_part = normalize_back(
-        first_back, first_gain, first_normed, first_scale
-    )
-    adapted_home = (middle_back + adapted_part).astype(BF16)
-    adapted_away = swap(adapted_home, "tensor")
-    adapted_low = jnp.concatenate(
-        [
-            jnp.where(tensor == 0, adapted_home, adapted_away),
-            jnp.where(tensor == 0, adapted_away, adapted_home),
-        ],
-        axis=0,
+        parents, parts, upstream, attended, logsum, table_cosine, table_sine
+    )
+    joined, adapted_low, first_gain_part = leave(
+        sent.reshape(4, rows, 3 * WIDE),
+        adapted,
+        middle_back,
+        one_row(first_gain),
+        query_weight,
+        key_weight,
+        value_weight,
     )
     adapter_part = jnp.einsum(
         "rcd,re->cde", latent_embed, adapted_low, preferred_element_type=F32
     ).astype(BF16)
-    adapter_kept = fold(fold(adapter_part.reshape(-1, width), core, "core"), x, "x")
-    adapter_kept, input_sum = together(adapter_kept, input_sum)
-    adapter_sum = lax.psum(adapter_kept, "dp")
+    kept = [add_low(own, theirs) for own, theirs in zip(sides[0::2], away)]
+    pair_total, down_total, output_total, input_total, adapter_total = reduce_all(
+        kept + [tn(first_low, joined), adapter_part.reshape(-1, width)],
+        [(False, True), (True, True), (False, True), (False, False), (False, False)],
+        "reduce_all",
+        2,
+    )
     latent_gradient = jnp.einsum("re,cde->rcd", adapted_low, adapter, preferred_element_type=F32)
-    gains = sum_small(jnp.concatenate([gain_parts[:3], first_gain_part[None]], axis=0))
-    gate_total, up_total = finish(gate_sum), finish(up_sum)
-    down_total, output_total = finish(down_sum), finish(output_sum)
-    input_total = finish(input_sum)
-    adapter_total = finish(adapter_sum).reshape(adapter.shape)
+    gains = sum_small(jnp.concatenate([gain_parts[:3], first_gain_part[:1]], axis=0))
     return (
         layer_out,
         latent_gradient,
-        adapter_total,
+        adapter_total.reshape(adapter.shape),
         gains[3],
         input_total[:, :inner],
         input_total[:, inner : 2 * inner],
@@ -1195,8 +1658,8 @@
         output_total,
         gains[0],
         gains[1],
-        gate_total,
-        up_total,
+        pair_total[:, :split],
+        pair_total[:, split:],
         down_total,
         gains[2],
     )

time: 859 us -> 877 us (1.021)
  Pallas kernels: 231 us -> 549 us
  waiting for transfers between devices: 340 us -> 136 us
  other arithmetic: 98.7 us -> 45.1 us
  starting transfers between devices: 65.6 us -> 23.8 us
    pallas_call x7 -> x5, Pallas kernels: 170 us -> 488 us  [the longest x1 194 us: reduce_all(): pl.pallas_call(functools.partial(reduce_kernel, items), out_shape=tuple((...]
    ppermute x43 -> x13, waiting for transfers between devices: 213 us -> 70.5 us  [swap(): return lax.ppermute(value, axis, [(0, 1), (1, 0)])]
    all_to_all x4 -> x0, waiting for transfers between devices: 53.8 us -> none  [the longest x3 53.8 us: on_device_paired(): head_parts.append(lax.all_to_all(sent, ('x', 'core'), 0, 0, tiled=False))]
    psum x4 -> x0, waiting for transfers between devices: 43.3 us -> none  [the longest x1 30.3 us: on_device_paired(): adapter_sum = lax.psum(adapter_kept, 'dp')]
    all_gather x4 -> x2, waiting for transfers between devices: 5.39 us -> 41.3 us  [the longest x1 41.3 us: on_device_paired(): pair_all = lax.all_gather(pair, ('tensor', 'x', 'core'), axis=0, tiled=True)]
    ppermute x43 -> x13, starting transfers between devices: 35.7 us -> 11.5 us  [swap(): return lax.ppermute(value, axis, [(0, 1), (1, 0)])]
    convert_element_type x7 -> x0, other arithmetic: 20.6 us -> none  [the longest x6 15.3 us: finish(): return unfold(unfold(value, x, 'x'), core, 'core').astype(F32)]
    select_n x13 -> x0, other arithmetic: 19.3 us -> none  [the longest x12 17.3 us: unfold(): jnp.where(index == 0, value, other)]
  transfers between devices with their start and end apart: 59 -> 19, of which waited for: 25 -> 4; matrix products, arithmetic and copies ran while one was open for 19% -> 9% of each run, Pallas kernels for 20% -> 25%
where the time goes in v2:
time: 877 us; the launch traced here: 867 us
  Pallas kernels  549 us (63%)
  waiting for transfers between devices  136 us (16%)
  local copies, waits for them, and re-layouts  58.6 us (7%)
  other arithmetic  45.1 us (5%)
  matrix products  38.6 us (4%)
  starting transfers between devices  23.8 us (3%)
  between operations  15 us (2%)
    pallas_call x1, Pallas kernels, reduce_all(): pl.pallas_call(functools.partial(reduce_kernel, items), out_shape=tuple((...  194 us
    pallas_call x1, Pallas kernels, attention_backward(): pl.pallas_call(attention_back_kernel, out_shape=jax.ShapeDtypeStruct((tok...  79.2 us
    pallas_call x1, Pallas kernels, enter(): pl.pallas_call(enter_kernel, out_shape=(jax.ShapeDtypeStruct((peers, rows...  78.4 us
    pallas_call x1, Pallas kernels, leave(): pl.pallas_call(leave_kernel, out_shape=(jax.ShapeDtypeStruct((rows, 3 * i...  73 us
    ppermute x13, waiting for transfers between devices, swap(): return lax.ppermute(value, axis, [(0, 1), (1, 0)])  70.5 us
    pallas_call x1, Pallas kernels, attention_forward(): pl.pallas_call(attention_kernel, out_shape=(jax.ShapeDtypeStruct((tokens,...  63.5 us
    pallas_call x1, Pallas kernels, middle_section(): pl.pallas_call(middle_kernel, grid_spec=pltpu.PrefetchScalarGridSpec(num_...  61.7 us
    all_gather x1, waiting for transfers between devices, on_device_paired(): pair_all = lax.all_gather(pair, ('tensor', 'x', 'core'), axis=0, tiled=True)  41.3 us
  transfers between devices with their start and end apart: 19, of which 4 were waited for; matrix products, arithmetic and copies ran while one was open for 9% of the time, Pallas kernels for 25%

profile of v2, /device:TPU:0, one launch (start us, length us, event | category | flops | bytes accessed | tf_op | source)
XLA Modules:
  0.0 866.7 jit_solution(12988467591228554720)
XLA Ops:
  8.1 7.4 copy.31
  21.3 5.9 bitcast_convert_fusion.mine
  27.2 3.7 fusion.12
  30.9 78.4 %enter.1 = (bf16[4,1280,384]{2,1,0:T(8,128)(2,1)}, bf16[1280,1024]{1,0:T(8,128)(2,1)}, bf16[1280,1024]{1,0:T(8,128)(2,1)}) custom-call(bf16[1280,1024]{1,0:T(8,128)(2,1)} %bitcast_convert_fusion.mine, f32[1,1024]{1,0:T(1,128)} %bitcast.57, bf16[1024,512]{1,0:T(8,128)(2,1)} %query_w.3, bf16[1024,512]{1,0:T(8,128)(2,1)} %key_w.3, bf16[1024,512]{1,0:T(8,128)(2,1)} %value_w.3, ...), custom_call_target="tpu_custom_call" | custom-call | flops 4026531840 | bytes 209715200 | tf_op jit(solution)/shard_map/enter/pallas_call | solution.py:727
  110.1 63.5 %attention_forward.1 = (bf16[5120,128]{1,0:T(8,128)(2,1)}, f32[5120,128]{1,0:T(8,128)}) custom-call(s32[1,20]{1,0:T(1,128)} %parents.3, bf16[5120,384]{1,0:T(8,128)(2,1)} %bitcast.59), custom_call_target="tpu_custom_call" | custom-call | flops 10200547328 | bytes 7864320 | tf_op jit(solution)/shard_map/attention_forward/pallas_call | solution.py:446
  173.6 3.8 all-to-all-start
  181.6 23.7 %all-to-all-done.heads = bf16[8,640,128]{2,1,0:T(8,128)(2,1)S(1)} async-done(((bf16[8,640,128]{2,1,0:T(8,128)(2,1)}), bf16[8,640,128]{2,1,0:T(8,128)(2,1)S(1)}, u32[]{:S(2)}, u32[]{:S(2)}) %all-to-all-start) | async-done | bytes 1310752 | tf_op jit(solution)/shard_map/all_to_all | solution.py:1577
  205.4 41.3 %all-gather.4.cloned.1.call-done.pair_all = bf16[2048,2816]{1,0:T(8,128)(2,1)} async-done(((bf16[256,2816]{1,0:T(8,128)(2,1)}), bf16[2048,2816]{1,0:T(8,128)(2,1)}) %all-gather.4.cloned.1.call-update) | async-done | bytes 11534352 | tf_op jit(solution)/shard_map/all_gather | solution.py:1573
  246.7 61.7 %middle_section.1 = (bf16[640,1024]{1,0:T(8,128)(2,1)}, f32[640,1024]{1,0:T(8,128)}, bf16[640,1024]{1,0:T(8,128)(2,1)}, bf16[640,1024]{1,0:T(8,128)(2,1)}, bf16[...) custom-call(s32[2]{0:T(128)} %pad_add_fusion.meta, ...), custom_call_target="tpu_custom_call" | custom-call | flops 24830279680 | bytes 43319296 | tf_op jit(solution)/shard_map/middle_section/pallas_call | solution.py:918
  308.4 7.3 convolution_convert_fusion
  315.8 5.5 convolution_convert_fusion.1
  342.7 6.3 fusion.11
  349.0 4.5 all-to-all-start.1
  365.2 4.3 add_convert_fusion.1
  369.6 4.2 add_convert_fusion.2
  373.8 79.2 %attention_backward.1 = bf16[5120,384]{1,0:T(8,128)(2,1)} custom-call(s32[1,20]{1,0:T(1,128)} %parents.3, bf16[5120,384]{1,0:T(8,128)(2,1)} %bitcast.60, bf16[5120,128]{1,0:T(8,128)(2,1)} %bitcast.10.upstream, bf16[5120,128]{1,0:T(8,128)(2,1)} %get-tuple-element.50.attended, f32[5120,128]{1,0:T(8,128)} %get-tuple-element.62.logsum, ...), custom_call_target="tpu_custom_call" | custom-call | flops 25501368320 | bytes 15728640 | tf_op jit(solution)/shard_map/attention_backward/pallas_call | solution.py:592
  452.9 73.0 %leave.1 = (bf16[1280,1536]{1,0:T(8,128)(2,1)}, bf16[1280,1024]{1,0:T(8,128)(2,1)}, f32[8,1024]{1,0:T(8,128)}) custom-call(bf16[4,1280,384]{2,1,0:T(8,128)(2,1)} %bitcast.61, f32[640,1024]{1,0:T(8,128)} %convert_add_fusion.adapted, f32[640,1024]{1,0:T(8,128)} %get-tuple-element.63.middle_back, f32[1,1024]{1,0:T(1,128)} %bitcast.58, ...), custom_call_target="tpu_custom_call" | custom-call | flops 4026531840 | bytes 209715200 | tf_op jit(solution)/shard_map/leave/pallas_call | solution.py:1110
  540.1 6.1 convolution_convert_fusion.4.refs_3_
  547.8 4.0 fusion.6
  557.3 10.7 %copy.32 = f32[1280,2,512]{2,1,0:T(2,128)} copy(f32[1280,2,512]{2,0,1:T(8,128)S(1)} %fusion.4) | data formatting | bytes 10485760
  569.6 10.8 %collective-permute-done.8 = bf16[704,1024]{1,0:T(8,128)(2,1)S(1)} collective-permute-done((bf16[704,1024]{1,0:T(8,128)(2,1)S(1)}, bf16[704,1024]{1,0:T(8,128)(2,1)S(1)}, u32[]{:S(2)}, u32[]{:S(2)}) %collective-permute-start.8) | collective-permute-done | bytes 1441824 | tf_op jit(solution)/shard_map/ppermute | solution.py:1485
  582.1 59.6 %collective-permute-done.7 = bf16[512,2816]{1,0:T(8,128)(2,1)S(1)} collective-permute-done((bf16[512,2816]{1,0:T(8,128)(2,1)S(1)}, bf16[512,2816]{1,0:T(8,128)(2,1)S(1)}, u32[]{:S(2)}, u32[]{:S(2)}) %collective-permute-start.7) | collective-permute-done | bytes 2883616 | tf_op jit(solution)/shard_map/ppermute | solution.py:1485
  644.0 193.7 %reduce_all.1 = (f32[1024,2816]{1,0:T(8,128)}, f32[1408,1024]{1,0:T(8,128)}, f32[512,1024]{1,0:T(8,128)}, f32[1024,1536]{1,0:T(8,128)}, f32[1024,1024]{1,0:T(8,128)}) custom-call(bf16[512,2816]{1,0:T(8,128)(2,1)} %add_convert_fusion.refs_0_, bf16[704,1024]{1,0:T(8,128)(2,1)} %add_convert_fusion.3.refs_1_, bf16[256,1024]{1,0:T(8,128)(2,1)} %add_convert_fusion.6.refs_2_, ...), custom_call_target="tpu_custom_call" | custom-call | flops 29884416 | bytes 224133120 | tf_op jit(solution)/shard_map/reduce_all/pallas_call | solution.py:1468
  837.7 9.6 %fusion.19 = (f32[1024,1408]{1,0:T(8,128)}, f32[1024,1408]{1,0:T(8,128)}) fusion(f32[1024,2816]{1,0:T(8,128)} %get-tuple-element.78), kind=kLoop, calls=%fused_computation.60 | loop fusion | bytes 23068672 | tf_op jit(solution)/shard_map/slice | solution.py:1662
  (150 shorter events, 83.6 us)
Async XLA Ops:
  7.2 14.1 %copy-start = (bf16[2,512,1024]{2,1,0:T(8,128)(2,1)S(1)}, bf16[2,512,1024]{2,1,0:T(8,128)(2,1)}, u32[]{:S(2)}) copy-start(bf16[2,512,1024]{2,1,0:T(8,128)(2,1)} %param.17) | copy-start | bytes 6291460
  7.2 198.2 %all-gather.6.cloned.1.call-start = ((), (), s32[]{:S(2)}) async-start(), calls=%async_computation.3 | async-start | bytes 8847360 | tf_op jit(solution)/shard_map/all_gather | solution.py:1574
  7.3 19.9 %copy-start.18 = (f32[128]{0:T(128)}, f32[128]{0:T(128)S(1)}, u32[]{:S(2)}) copy-start(f32[128]{0:T(128)S(1)} %get-tuple-element.110) | copy-start | bytes 1540
  109.3 137.4 %all-gather.4.cloned.1.call-start = ((), (), s32[]{:S(2)}) async-start(), calls=%async_computation.2 | async-start | bytes 12976128 | tf_op jit(solution)/shard_map/all_gather | solution.py:1573
  173.6 31.8 %all-to-all-start = ((bf16[8,640,128]{2,1,0:T(8,128)(2,1)}), bf16[8,640,128]{2,1,0:T(8,128)(2,1)S(1)}, u32[]{:S(2)}, u32[]{:S(2)}) async-start(bf16[8,640,128]{2,1,0:T(8,128)(2,1)} %bitcast.48), calls=%async_computation | async-start | bytes 2621440 | tf_op jit(solution)/shard_map/all_to_all | solution.py:1577
  205.4 41.3 %copy-start.14 = (bf16[8,640,128]{2,1,0:T(8,128)(2,1)}, bf16[8,640,128]{2,1,0:T(8,128)(2,1)S(1)}, u32[]{:S(2)}) copy-start(bf16[8,640,128]{2,1,0:T(8,128)(2,1)S(1)} %all-to-all-done.heads) | copy-start | bytes 3932164
  315.7 15.9 %copy-start.4 = (bf16[1024,2816]{1,0:T(8,128)(2,1)}, bf16[1024,2816]{1,0:T(8,128)(2,1)S(1)}, u32[]{:S(2)}) copy-start(bf16[1024,2816]{1,0:T(8,128)(2,1)S(1)} %convolution_convert_fusion) | copy-start | bytes 17301508
  322.4 20.0 %collective-permute-start.6 = (bf16[256,1024]{1,0:T(8,128)(2,1)S(1)}, bf16[256,1024]{1,0:T(8,128)(2,1)}, u32[]{:S(2)}, u32[]{:S(2)}) collective-permute-start(bf16[256,1024]{1,0:T(8,128)(2,1)S(1)} %constant_dynamic-slice_fusion), channel_id=1, source_target_pairs={{0,2},{2,0},{1,3},{3,1},{4,6},{6,4},{5,7},{7,5},{8,10},{10,8},{9,1... | collective-permute-start | bytes 1572872 | tf_op jit(solution)/shard_map/ppermute | solution.py:1485
  331.3 29.5 %collective-permute-start.4 = (bf16[704,1024]{1,0:T(8,128)(2,1)}, bf16[704,1024]{1,0:T(8,128)(2,1)S(1)}, u32[]{:S(2)}, u32[]{:S(2)}) collective-permute-start(bf16[704,1024]{1,0:T(8,128)(2,1)} %constant_dynamic-slice_fusion.2), channel_id=1, source_target_pairs={{0,2},{2,0},{1,3},{3,1},{4,6},{6,4},{5,7},{7,5},{8,10},{10,8},{9,1... | collective-permute-start | bytes 4325384 | tf_op jit(solution)/shard_map/ppermute | solution.py:1485
  333.4 31.8 %collective-permute-start.2 = (bf16[512,2816]{1,0:T(8,128)(2,1)}, bf16[512,2816]{1,0:T(8,128)(2,1)}, u32[]{:S(2)}, u32[]{:S(2)}) collective-permute-start(bf16[512,2816]{1,0:T(8,128)(2,1)} %constant_dynamic-slice_fusion.4), channel_id=1, source_target_pairs={{0,2},{2,0},{1,3},{3,1},{4,6},{6,4},{5,7},{7,5},{8,10},{10,8},{9,1... | collective-permute-start | bytes 8650760 | tf_op jit(solution)/shard_map/ppermute | solution.py:1485
  335.4 34.2 %collective-permute-start.1 = (bf16[512,2816]{1,0:T(8,128)(2,1)}, bf16[512,2816]{1,0:T(8,128)(2,1)}, u32[]{:S(2)}, u32[]{:S(2)}) collective-permute-start(bf16[512,2816]{1,0:T(8,128)(2,1)} %constant_dynamic-slice_fusion.5), channel_id=1, source_target_pairs={{0,2},{2,0},{1,3},{3,1},{4,6},{6,4},{5,7},{7,5},{8,10},{10,8},{9,1... | collective-permute-start | bytes 8650760 | tf_op jit(solution)/shard_map/ppermute | solution.py:1485
  341.0 15.8 %collective-permute-start.5 = (bf16[256,1024]{1,0:T(8,128)(2,1)}, bf16[256,1024]{1,0:T(8,128)(2,1)}, u32[]{:S(2)}, u32[]{:S(2)}) collective-permute-start(bf16[256,1024]{1,0:T(8,128)(2,1)} %constant_dynamic-slice_fusion.1), channel_id=1, source_target_pairs={{0,2},{2,0},{1,3},{3,1},{4,6},{6,4},{5,7},{7,5},{8,10},{10,8},{9,1... | collective-permute-start | bytes 1572872 | tf_op jit(solution)/shard_map/ppermute | solution.py:1485
  342.4 20.2 %collective-permute-start.3 = (bf16[704,1024]{1,0:T(8,128)(2,1)}, bf16[704,1024]{1,0:T(8,128)(2,1)}, u32[]{:S(2)}, u32[]{:S(2)}) collective-permute-start(bf16[704,1024]{1,0:T(8,128)(2,1)} %constant_dynamic-slice_fusion.3), channel_id=1, source_target_pairs={{0,2},{2,0},{1,3},{3,1},{4,6},{6,4},{5,7},{7,5},{8,10},{10,8},{9,1... | collective-permute-start | bytes 4325384 | tf_op jit(solution)/shard_map/ppermute | solution.py:1485
  349.0 24.8 %all-to-all-start.1 = ((bf16[8,640,128]{2,1,0:T(8,128)(2,1)}), bf16[8,640,128]{2,1,0:T(8,128)(2,1)}, u32[]{:S(2)}, u32[]{:S(2)}) async-start(bf16[8,640,128]{2,1,0:T(8,128)(2,1)} %get-tuple-element.54), calls=%async_computation.1 | async-start | bytes 2621440 | tf_op jit(solution)/shard_map/all_to_all | solution.py:1599
  356.7 172.5 %collective-permute-start = (bf16[640,1024]{1,0:T(8,128)(2,1)}, bf16[640,1024]{1,0:T(8,128)(2,1)}, u32[]{:S(2)}, u32[]{:S(2)}) collective-permute-start(bf16[640,1024]{1,0:T(8,128)(2,1)} %get-tuple-element.53), channel_id=1, source_target_pairs={{0,1},{1,0},{2,3},{3,2},{4,5},{5,4},{6,7},{7,6},{8,9},{9,8},{10,11... | collective-permute-start | bytes 3932168 | tf_op jit(solution)/shard_map/ppermute | solution.py:1485
  526.7 4.6 collective-permute-start.10
  531.3 7.2 collective-permute-start.11
  534.7 33.8 %collective-permute-start.9 = (bf16[256,1024]{1,0:T(8,128)(2,1)S(1)}, bf16[256,1024]{1,0:T(8,128)(2,1)S(1)}, u32[]{:S(2)}, u32[]{:S(2)}) collective-permute-start(bf16[256,1024]{1,0:T(8,128)(2,1)S(1)} %copy-done.17), channel_id=1, source_target_pairs={{0,1},{1,0},{2,3},{3,2},{4,5},{5,4},{6,7},{7,6},{8,9},{9,8},{10,11... | collective-permute-start | bytes 1572872 | tf_op jit(solution)/shard_map/ppermute | solution.py:1485
  536.4 43.9 %collective-permute-start.8 = (bf16[704,1024]{1,0:T(8,128)(2,1)S(1)}, bf16[704,1024]{1,0:T(8,128)(2,1)S(1)}, u32[]{:S(2)}, u32[]{:S(2)}) collective-permute-start(bf16[704,1024]{1,0:T(8,128)(2,1)S(1)} %copy-done.13), channel_id=1, source_target_pairs={{0,1},{1,0},{2,3},{3,2},{4,5},{5,4},{6,7},{7,6},{8,9},{9,8},{10,11... | collective-permute-start | bytes 4325384 | tf_op jit(solution)/shard_map/ppermute | solution.py:1485
  536.8 105.0 %collective-permute-start.7 = (bf16[512,2816]{1,0:T(8,128)(2,1)S(1)}, bf16[512,2816]{1,0:T(8,128)(2,1)S(1)}, u32[]{:S(2)}, u32[]{:S(2)}) collective-permute-start(bf16[512,2816]{1,0:T(8,128)(2,1)S(1)} %copy-done.6), channel_id=1, source_target_pairs={{0,1},{1,0},{2,3},{3,2},{4,5},{5,4},{6,7},{7,6},{8,9},{9,8},{10,11... | collective-permute-start | bytes 8650760 | tf_op jit(solution)/shard_map/ppermute | solution.py:1485
  538.5 7.7 collective-permute-start.12
  546.2 5.6 collective-permute-start.13
  551.8 16.1 %collective-permute-start.14 = (f32[4,1024]{1,0:T(4,128)S(1)}, f32[4,1024]{1,0:T(4,128)S(1)}, u32[]{:S(2)}, u32[]{:S(2)}) collective-permute-start(f32[4,1024]{1,0:T(4,128)S(1)} %add.140), channel_id=1, source_target_pairs={{0,16},{16,0},{8,24},{24,8},{1,17},{17,1},{9,25},{25,9},{2,18},{18... | collective-permute-start | bytes 49160 | tf_op jit(solution)/shard_map/ppermute | solution.py:1516
  568.6 73.2 %copy-start.1 = (bf16[512,2816]{1,0:T(8,128)(2,1)S(1)}, bf16[512,2816]{1,0:T(8,128)(2,1)}, u32[]{:S(2)}) copy-start(bf16[512,2816]{1,0:T(8,128)(2,1)} %add_convert_fusion.2) | copy-start | bytes 8650756
  (30 other events, 184.2 us)
Sparse Core Ops, SparseCore 0:
  109.4 52.9 all-gather.5
  164.9 81.7 all-gather.3

commit v3 on v2

--- a/solution.py
+++ b/solution.py
@@ -346,6 +346,47 @@
             role[TRUNK + BRANCH + b * LEAVES + leaf] = child[role[TRUNK + b] * BRANCH + leaf]
 
 
+def roles_kernel(parents, parts, role, place, out, child, count):
+    find_roles(parents, child, count, role)
+    for i in range(SEGS):
+        place[role[i]] = i
+    pick_segments(role, parts, out)
+
+
+def pick_segments(order, source, out):
+    for i in range(SEGS):
+        out[segment(i), :] = source[segment(order[i]), :]
+
+
+def sort_parts(parents, parts):
+    smem = pl.BlockSpec(memory_space=pltpu.SMEM)
+    vmem = pl.BlockSpec(memory_space=pltpu.VMEM)
+    return pl.pallas_call(
+        roles_kernel,
+        out_shape=(jax.ShapeDtypeStruct((SEGS,), jnp.int32),) * 2
+        + (jax.ShapeDtypeStruct(parts.shape, parts.dtype),),
+        in_specs=[smem, vmem],
+        out_specs=(smem, smem, vmem),
+        scratch_shapes=[
+            pltpu.SMEM((SEGS * BRANCH,), jnp.int32),
+            pltpu.SMEM((SEGS,), jnp.int32),
+        ],
+        name="sort_parts",
+    )(parents, parts)
+
+
+def pick(order, source):
+    smem = pl.BlockSpec(memory_space=pltpu.SMEM)
+    vmem = pl.BlockSpec(memory_space=pltpu.VMEM)
+    return pl.pallas_call(
+        pick_segments,
+        out_shape=jax.ShapeDtypeStruct(source.shape, source.dtype),
+        in_specs=[smem, vmem],
+        out_specs=vmem,
+        name="pick",
+    )(order, source)
+
+
 def heads_apart(values, first):
     zero = jnp.zeros_like(values)
     return jnp.concatenate(
@@ -353,14 +394,106 @@
     )
 
 
-def attention_kernel(
-    parents, parts, out, logsum, qr, kr, v0, v1, kept, acc, top, total, child, count, role
-):
-    find_roles(parents, child, count, role)
+MESH = pl.DeviceIdType.MESH
+
+
+def at_step(index, plan):
+    for step, calls in plan.items():
+
+        @pl.when(index == step)
+        def _(calls=calls):
+            for call in calls:
+                call()
+
+
+class Fetch:
+    def __init__(self, shape, pieces):
+        self.rows, self.lanes = shape
+        self.pieces = pieces
+
+    def scratch(self):
+        return [pltpu.SemaphoreType.DMA((4, self.pieces))] * 2
+
+    def bind(self, own, out, refs):
+        self.own, self.out = own, out
+        self.send, self.recv = refs
+        self.x, self.core = lax.axis_index("x"), lax.axis_index("core")
+        self.to_core = {"core": 1 - self.core}
+        self.to_x = {"x": 1 - self.x}
+        self.to_tensor = {"tensor": 1 - lax.axis_index("tensor")}
+
+    def copy(self, kind, piece):
+        rows = self.rows // 4 // self.pieces
+        x = 1 - self.x if kind == 3 else self.x
+        row = (2 * x + self.core) * (self.rows // 4) + piece * rows
+        here = pl.ds(pl.multiple_of(row, 16), rows)
+        return pltpu.make_async_remote_copy(
+            src_ref=(self.own if kind == 0 else self.out).at[here],
+            dst_ref=self.out.at[here],
+            send_sem=self.send.at[kind, piece],
+            recv_sem=self.recv.at[kind, piece],
+            device_id=(self.to_tensor, self.to_x, self.to_core, self.to_core)[kind],
+            device_id_type=MESH,
+        )
+
+    def start(self):
+        for piece in range(self.pieces):
+            self.copy(0, piece).start()
+
+    def second(self, piece):
+        self.copy(0, piece).wait_recv()
+        self.copy(1, piece).start()
+        self.copy(2, piece).start()
+
+    def third(self, piece):
+        self.copy(1, piece).wait_recv()
+        self.copy(3, piece).start()
+
+    def drain(self):
+        for piece in range(self.pieces):
+            for kind in range(4):
+                self.copy(kind, piece).wait_send()
+            self.copy(2, piece).wait_recv()
+            self.copy(3, piece).wait_recv()
+
+
+def attention_kernel(fetches, *refs):
+    parts = refs[0]
+    count = len(fetches)
+    own_weights, refs = refs[1 : 1 + count], refs[1 + count :]
+    out, logsum, other_weights = refs[0], refs[1], refs[2 : 2 + count]
+    qr, kr, v0, v1, kept, acc, top, total = refs[2 + count : 10 + count]
+    sems = refs[10 + count :]
+    for i, fetch in enumerate(fetches):
+        fetch.bind(own_weights[i], other_weights[i], sems[2 * i : 2 * i + 2])
+    output, gate, up, down = fetches
+    barrier = pltpu.get_barrier_semaphore()
+    for target in (gate.to_core, gate.to_x, gate.to_tensor):
+        pl.semaphore_signal(barrier, inc=1, device_id=target, device_id_type=MESH)
+    pl.semaphore_wait(barrier, 3)
+    for fetch in fetches:
+        fetch.start()
+    call = functools.partial
+    leaf_plan = {
+        2: [call(output.second, 0)],
+        4: [call(gate.second, 0), call(output.third, 0)],
+        6: [call(gate.second, 1)],
+        7: [call(gate.third, 0)],
+    }
+    branch_plan = {
+        0: [call(up.second, 0)],
+        1: [call(gate.third, 1)],
+        2: [call(up.second, 1)],
+        3: [call(up.third, 0)],
+    }
+    trunk_plan = {
+        3: [call(down.second, 0), call(up.third, 1)],
+        6: [call(down.second, 1)],
+    }
     first = lax.broadcasted_iota(jnp.int32, (SEG, WIDE), 1) < DH
 
     def sort(i, _):
-        here, source = segment(i), segment(role[i])
+        here = source = segment(i)
         qr[here, :] = parts[source, 0:WIDE] * jnp.asarray(DH**-0.5, BF16)
         kr[here, :] = parts[source, WIDE : 2 * WIDE]
         value = parts[source, 2 * WIDE : 3 * WIDE]
@@ -419,56 +552,232 @@
         whole = jnp.sum(total[...], axis=1, keepdims=True)
         inverse = 1.0 / whole
         log = most + jnp.log(whole)
-        here = segment(role[index])
+        here = segment(index)
         out[here, :] = (acc[...] * jnp.where(first, inverse[:SEG], inverse[SEG:])).astype(BF16)
         logsum[here, :] = jnp.where(first, log[:SEG], log[SEG:])
 
     def trunk(i, _):
+        at_step(i, trunk_plan)
         query(i, i, SEG, [])
         return 0
 
     def branch(i, _):
+        at_step(i, branch_plan)
         query(TRUNK + i, TRUNK * SEG // KEYS, KEYS, [])
         return 0
 
     def leaf(i, _):
+        at_step(i, leaf_plan)
         query(TRUNK + BRANCH + i, TRUNK * SEG // KEYS, KEYS, [TRUNK + i // LEAVES])
         return 0
 
+    lax.fori_loop(0, BRANCH * LEAVES, leaf, 0)
+    lax.fori_loop(0, BRANCH, branch, 0)
     lax.fori_loop(0, TRUNK, trunk, 0)
-    lax.fori_loop(0, BRANCH, branch, 0)
-    lax.fori_loop(0, BRANCH * LEAVES, leaf, 0)
-
-
-def attention_forward(parents, parts):
+    down.third(0)
+
+    down.third(1)
+    for fetch in fetches:
+        fetch.drain()
+
+
+def attention_forward(parts, weights):
+    fetches = [Fetch(weight.shape, 1 if i == 0 else 2) for i, weight in enumerate(weights)]
+    sems = []
+    for fetch in fetches:
+        sems += fetch.scratch()
+    hbm = pl.BlockSpec(memory_space=pl.ANY)
     tokens = SEGS * SEG
     vmem = pl.BlockSpec(memory_space=pltpu.VMEM)
     return pl.pallas_call(
-        attention_kernel,
+        functools.partial(attention_kernel, fetches),
         out_shape=(
             jax.ShapeDtypeStruct((tokens, WIDE), BF16),
             jax.ShapeDtypeStruct((tokens, WIDE), F32),
-        ),
-        in_specs=[pl.BlockSpec(memory_space=pltpu.SMEM), vmem],
-        out_specs=(vmem, vmem),
+        )
+        + tuple(jax.ShapeDtypeStruct(weight.shape, BF16) for weight in weights),
+        in_specs=[vmem] + [hbm] * len(weights),
+        out_specs=(vmem, vmem) + (hbm,) * len(weights),
         scratch_shapes=[pltpu.VMEM((tokens, WIDE), BF16)] * 4
         + [
             pltpu.VMEM((TRUNK, 2 * SEG, KEYS), F32),
             pltpu.VMEM((SEG, WIDE), F32),
             pltpu.VMEM((2 * SEG, 128), F32),
             pltpu.VMEM((2 * SEG, 128), F32),
-            pltpu.SMEM((SEGS * BRANCH,), jnp.int32),
-            pltpu.SMEM((SEGS,), jnp.int32),
-            pltpu.SMEM((SEGS,), jnp.int32),
-        ],
-        compiler_params=pltpu.CompilerParams(vmem_limit_bytes=VMEM_BYTES),
+        ]
+        + sems,
+        compiler_params=pltpu.CompilerParams(
+            vmem_limit_bytes=VMEM_BYTES, collective_id=4, has_side_effects=True
+        ),
         cost_estimate=pl.CostEstimate(
             flops=152 * 2 * 4 * SEG * SEG * 128,
             bytes_accessed=tokens * WIDE * 12,
             transcendentals=152 * 2 * SEG * SEG,
         ),
         name="attention_forward",
-    )(parents, parts.reshape(tokens, 3 * WIDE))
+    )(parts, *weights)
+
+
+def add_rows(dst, dst_row, left, left_row, right, right_row, rows, step=32):
+    def one(i, _):
+        at = i * step
+        total = left[pl.ds(pl.multiple_of(left_row + at, step), step), :].astype(F32)
+        total += right[pl.ds(pl.multiple_of(right_row + at, step), step), :].astype(F32)
+        dst[pl.ds(pl.multiple_of(dst_row + at, step), step), :] = total.astype(BF16)
+        return 0
+
+    lax.fori_loop(0, rows // step, one, 0)
+
+
+class PairFold:
+    def __init__(self, shape, x_first, pieces=1):
+        self.rows, self.lanes = shape
+        self.x_first = x_first
+        self.pieces = pieces if x_first else 2
+
+    def scratch(self):
+        half, quarter = (self.rows // 2, self.lanes), (self.rows // 4, self.lanes)
+        return (
+            [pltpu.VMEM(half, BF16)] * 4
+            + [pltpu.VMEM(quarter, BF16)] * (2 if self.x_first else 1)
+            + [pltpu.VMEM(quarter if self.x_first else half, BF16)]
+            + [pltpu.SemaphoreType.DMA((2,))] * 3
+            + [pltpu.SemaphoreType.DMA((2, self.pieces))] * 2
+            + [pltpu.SemaphoreType.DMA((self.pieces,))] * 2
+        )
+
+    def bind(self, parts, out, refs):
+        self.parts, self.out = parts, out
+        self.keep, self.land = refs[0:2], refs[2:4]
+        count = 2 if self.x_first else 1
+        self.x_land = refs[4 : 4 + count]
+        (
+            self.y_land,
+            self.local,
+            self.core_send,
+            self.core_recv,
+            self.x_send,
+            self.x_recv,
+            self.y_send,
+            self.y_recv,
+        ) = refs[4 + count :]
+        self.x, self.core = lax.axis_index("x"), lax.axis_index("core")
+        self.to_core = {"core": 1 - self.core}
+        self.to_x = {"x": 1 - self.x}
+        self.to_tensor = {"tensor": 1 - lax.axis_index("tensor")}
+        self.half, self.quarter = self.rows // 2, self.rows // 4
+
+    def rows_at(self, ref, row, rows):
+        return ref.at[pl.ds(pl.multiple_of(row, 32), rows)]
+
+    def remote(self, src, dst, send, recv, where):
+        return pltpu.make_async_remote_copy(
+            src_ref=src,
+            dst_ref=dst,
+            send_sem=send,
+            recv_sem=recv,
+            device_id=where,
+            device_id_type=MESH,
+        )
+
+    def over_core(self, side):
+        return self.remote(
+            self.rows_at(self.parts[side], (1 - self.core) * self.half, self.half),
+            self.land[side],
+            self.core_send.at[side],
+            self.core_recv.at[side],
+            self.to_core,
+        )
+
+    def kept(self, side):
+        return pltpu.make_async_copy(
+            self.rows_at(self.parts[side], self.core * self.half, self.half),
+            self.keep[side],
+            self.local.at[side],
+        )
+
+    def over_x(self, side, piece):
+        rows = self.quarter // self.pieces if self.x_first else self.quarter
+        start = piece * rows if self.x_first else 0
+        return self.remote(
+            self.rows_at(self.keep[side], (1 - self.x) * self.quarter + start, rows),
+            self.rows_at(self.x_land[side], start, rows),
+            self.x_send.at[side, piece],
+            self.x_recv.at[side, piece],
+            self.to_x,
+        )
+
+    def over_tensor(self, piece):
+        if self.x_first:
+            rows = self.quarter // self.pieces
+            source, target = self.x * self.quarter + piece * rows, piece * rows
+        else:
+            rows = self.quarter
+            source = (1 - self.x if piece == 0 else self.x) * rows
+            target = source
+        return self.remote(
+            self.rows_at(self.keep[1], source, rows),
+            self.rows_at(self.y_land, target, rows),
+            self.y_send.at[piece],
+            self.y_recv.at[piece],
+            self.to_tensor,
+        )
+
+    def start(self):
+        for side in range(2):
+            self.over_core(side).start()
+            self.kept(side).start()
+
+    def fold_core(self):
+        for side in (1, 0):
+            self.kept(side).wait()
+            self.over_core(side).wait_recv()
+            add_rows(self.keep[side], 0, self.keep[side], 0, self.land[side], 0, self.half)
+        for piece in range(self.pieces):
+            if self.x_first:
+                self.over_x(1, piece).start()
+                self.over_x(0, piece).start()
+            else:
+                self.over_tensor(piece).start()
+
+    def second(self, piece):
+        if self.x_first:
+            rows = self.quarter // self.pieces
+            at = self.x * self.quarter + piece * rows
+            for side in (1, 0):
+                self.over_x(side, piece).wait_recv()
+                keep, land = self.keep[side], self.x_land[side]
+                add_rows(keep, at, keep, at, land, piece * rows, rows)
+                if side == 1:
+                    self.over_tensor(piece).start()
+        else:
+            at = (1 - self.x if piece == 0 else self.x) * self.quarter
+            self.over_tensor(piece).wait_recv()
+            add_rows(self.keep[0], at, self.keep[0], at, self.y_land, at, self.quarter)
+            if piece == 0:
+                self.over_x(0, 0).start()
+
+    def third(self, piece):
+        if self.x_first:
+            rows = self.quarter // self.pieces
+            self.over_tensor(piece).wait_recv()
+            at = self.x * self.quarter + piece * rows
+            add_rows(self.out, piece * rows, self.keep[0], at, self.y_land, piece * rows, rows)
+        elif piece == 0:
+            self.over_x(0, 0).wait_recv()
+            at = self.x * self.quarter
+            add_rows(self.out, 0, self.keep[0], at, self.x_land[0], 0, self.quarter)
+
+    def drain(self):
+        for side in range(2):
+            self.over_core(side).wait_send()
+        for piece in range(self.pieces):
+            if self.x_first:
+                self.over_x(0, piece).wait_send()
+                self.over_x(1, piece).wait_send()
+            self.over_tensor(piece).wait_send()
+        if not self.x_first:
+            self.over_x(0, 0).wait_send()
 
 
 def swap_halves(values, low):
@@ -477,33 +786,36 @@
     )
 
 
-def attention_back_kernel(
-    parents,
-    parts,
-    upstream,
-    attended,
-    logsum,
-    cosine,
-    sine,
-    out,
-    qr,
-    kr,
-    vr,
-    kt,
-    dk,
-    dv,
-    dqt,
-    child,
-    count,
-    role,
-):
-    find_roles(parents, child, count, role)
+def attention_back_kernel(folds, *refs):
+    parts, upstream, attended, logsum, cosine, sine = refs[:6]
+    sides, refs = refs[6 : 6 + 2 * len(folds)], refs[6 + 2 * len(folds) :]
+    out, sums, refs = refs[0], refs[1 : 1 + len(folds)], refs[1 + len(folds) :]
+    qr, kr, vr, kt, dk, dv, dqt = refs[:7]
+    refs = refs[7:]
+    for i, fold in enumerate(folds):
+        size = len(fold.scratch())
+        fold.bind(sides[2 * i : 2 * i + 2], sums[i], refs[:size])
+        refs = refs[size:]
+    gate, down, up, output = folds
+    barrier = pltpu.get_barrier_semaphore()
+    for target in (gate.to_core, gate.to_x, gate.to_tensor):
+        pl.semaphore_signal(barrier, inc=1, device_id=target, device_id_type=MESH)
+    pl.semaphore_wait(barrier, 3)
+    for fold in folds:
+        fold.start()
+    call = functools.partial
+    leaf_plan = {
+        2: [gate.fold_core, up.fold_core],
+        3: [down.fold_core, output.fold_core],
+    }
+    branch_plan = {3: [call(gate.second, 0), call(up.second, 0), call(output.second, 0)]}
+    trunk_plan = {5: [call(up.second, 1), call(output.second, 1)]}
     lane = lax.broadcasted_iota(jnp.int32, (SEG, WIDE), 1)
     first = lane < DH
     low = (lane % DH) < (DH // 2)
 
     def sort(i, _):
-        here, source = segment(i), segment(role[i])
+        here = source = segment(i)
         qr[here, :] = parts[source, 0:WIDE] * jnp.asarray(DH**-0.5, BF16)
         key = parts[source, WIDE : 2 * WIDE]
         kr[here, :] = key
@@ -523,11 +835,11 @@
         return values * cosine[at, :] - swap_halves(values, low) * sine[at, :]
 
     def query(index, depth, count_big, big, extra):
-        here = segment(role[index])
+        here = segment(index)
         queries = heads_apart(qr[segment(index), :], first)
         up = upstream[here, :]
         ups = heads_apart(up, first)
-        turned = logsum[here, :].T
+        turned = logsum[segment(index), :].T
         log = jnp.concatenate([turned[0:1, :], turned[DH : DH + 1, :]], axis=1)
         product = (up.astype(F32) * attended[here, :].astype(F32)).T
         inner = jnp.concatenate(
@@ -561,14 +873,17 @@
         out[here, 0:WIDE] = rope_back(both.T, depth).astype(BF16)
 
     def leaf(i, _):
+        at_step(i, leaf_plan)
         query(TRUNK + BRANCH + i, TRUNK + 1, TRUNK * SEG // KEYS, KEYS, [TRUNK + i // LEAVES])
         return 0
 
     def branch(i, _):
+        at_step(i, branch_plan)
         query(TRUNK + i, TRUNK, TRUNK * SEG // KEYS, KEYS, [])
         return 0
 
     def trunk(i, _):
+        at_step(i, trunk_plan)
         query(i, i, i, SEG, [])
         return 0
 
@@ -576,41 +891,58 @@
     lax.fori_loop(0, BRANCH, branch, 0)
     lax.fori_loop(0, TRUNK, trunk, 0)
 
-    def finish(i, _):
-        here = segment(role[i])
+    down.second(0)
+
+    def settle(i, _):
+        here = segment(i)
         depth = jnp.where(i < TRUNK + BRANCH, jnp.minimum(i, TRUNK), TRUNK + 1)
-        out[here, WIDE : 2 * WIDE] = rope_back(dk[segment(i), :], depth).astype(BF16)
-        out[here, 2 * WIDE : 3 * WIDE] = dv[segment(i), :].astype(BF16)
+        out[here, WIDE : 2 * WIDE] = rope_back(dk[here, :], depth).astype(BF16)
+        out[here, 2 * WIDE : 3 * WIDE] = dv[here, :].astype(BF16)
         return 0
 
-    lax.fori_loop(0, SEGS, finish, 0)
-
-
-def attention_backward(parents, parts, upstream, attended, logsum, cosine, sine):
+    lax.fori_loop(0, SEGS, settle, 0)
+    for fold in (gate, up, output, down):
+        fold.third(0)
+    for fold in folds:
+        fold.drain()
+
+
+def attention_backward(parts, upstream, attended, logsum, cosine, sine, sides):
     tokens = SEGS * SEG
     vmem = pl.BlockSpec(memory_space=pltpu.VMEM)
+    folds = [PairFold(own.shape, i < 2) for i, own in enumerate(sides[::2])]
+    scratch = []
+    for fold in folds:
+        scratch += fold.scratch()
     return pl.pallas_call(
-        attention_back_kernel,
-        out_shape=jax.ShapeDtypeStruct((tokens, 3 * WIDE), BF16),
-        in_specs=[pl.BlockSpec(memory_space=pltpu.SMEM)] + [vmem] * 6,
-        out_specs=vmem,
+        functools.partial(attention_back_kernel, folds),
+        out_shape=(jax.ShapeDtypeStruct((tokens, 3 * WIDE), BF16),)
+        + tuple(jax.ShapeDtypeStruct((fold.rows // 4, fold.lanes), BF16) for fold in folds),
+        in_specs=[vmem] * 6 + [pl.BlockSpec(memory_space=pl.ANY)] * len(sides),
+        out_specs=(vmem,) * (1 + len(folds)),
         scratch_shapes=[pltpu.VMEM((tokens, WIDE), BF16)] * 3
         + [pltpu.VMEM((WIDE, tokens), BF16)]
         + [pltpu.VMEM((tokens, WIDE), F32)] * 2
-        + [
-            pltpu.VMEM((WIDE, 2 * SEG), F32),
-            pltpu.SMEM((SEGS * BRANCH,), jnp.int32),
-            pltpu.SMEM((SEGS,), jnp.int32),
-            pltpu.SMEM((SEGS,), jnp.int32),
-        ],
-        compiler_params=pltpu.CompilerParams(vmem_limit_bytes=VMEM_BYTES),
+        + [pltpu.VMEM((WIDE, 2 * SEG), F32)]
+        + scratch,
+        compiler_params=pltpu.CompilerParams(
+            vmem_limit_bytes=VMEM_BYTES, collective_id=3, has_side_effects=True
+        ),
         cost_estimate=pl.CostEstimate(
             flops=152 * 2 * 10 * SEG * SEG * 128,
             bytes_accessed=tokens * WIDE * 24,
             transcendentals=152 * 2 * SEG * SEG,
         ),
         name="attention_backward",
-    )(parents, parts.reshape(tokens, 3 * WIDE), upstream, attended, logsum, cosine, sine)
+    )(
+        parts,
+        upstream,
+        attended,
+        logsum,
+        cosine,
+        sine,
+        *sides,
+    )
 
 
 def angle_tables(positions):
@@ -619,9 +951,6 @@
     angle = positions.astype(F32)[:, None] * freq[None, :]
     sign = jnp.where((lane % DH) < DH // 2, -1.0, 1.0)
     return jnp.cos(angle), jnp.sin(angle) * sign[None, :]
-
-
-MESH = pl.DeviceIdType.MESH
 
 
 def neighbours():
@@ -764,8 +1093,10 @@
     wg_own,
     wu_own,
     wd_own,
-    pair_all,
-    stack_all,
+    wo_other,
+    wg_other,
+    wu_other,
+    wd_other,
     layer_out,
     middle_out,
     attended_out,
@@ -794,27 +1125,22 @@
         dst = weight.at[pl.ds(row, rows), pl.ds(lane, lanes)]
         copies.append(pltpu.make_async_copy(src, dst, sem.at[len(copies)]))
 
-    quarters = stack_all.shape[0] // 2
-    first_other = (1 - tensor) * quarters
-    inner, split = wo_own.shape[0], wg_own.shape[1]
-    width = wg_own.shape[0]
-    for weight, own, start in ((wo, wo_own, 0), (wd, wd_own, inner // quarters)):
-        rows = own.shape[0]
+    for weight, own, other, by_lane in (
+        (wo, wo_own, wo_other, False),
+        (wg, wg_own, wg_other, True),
+        (wu, wu_own, wu_other, True),
+        (wd, wd_own, wd_other, False),
+    ):
+        rows, lanes = own.shape
         copy(own, weight, 0, 0)
-        for i in range(quarters):
-            piece = stack_all.at[first_other + i, pl.ds(start, rows // quarters)]
-            copy(piece, weight, rows + i * (rows // quarters), 0)
-    others = pl.ds(pl.multiple_of((1 - tensor) * width, width), width)
-    for weight, own, lane in ((wg, wg_own, 0), (wu, wu_own, split)):
-        copy(own, weight, 0, 0)
-        copy(pair_all.at[others, pl.ds(lane, split)], weight, 0, split)
+        copy(other, weight, 0 if by_lane else rows, lanes if by_lane else 0)
 
     @pl.when(step == 0)
     def _():
         for copy in copies:
             copy.start()
         gains_out[...] = jnp.zeros_like(gains_out)
-        for copy in copies[: 1 + quarters]:
+        for copy in copies[:2]:
             copy.wait()
 
     groups = heads.shape[0] // 2
@@ -841,7 +1167,7 @@
 
     @pl.when(step == 0)
     def _():
-        for copy in copies[1 + quarters :]:
+        for copy in copies[2:]:
             copy.wait()
 
     sums[...] = jnp.zeros_like(sums)
@@ -928,7 +1254,7 @@
                 gain,
                 gain,
             ]
-            + [hbm] * 6,
+            + [hbm] * 8,
             out_specs=(
                 row,
                 row,
@@ -949,7 +1275,7 @@
                 pltpu.VMEM((hidden // HIDDEN, block, HIDDEN), F32),
                 pltpu.VMEM((hidden // HIDDEN, block, HIDDEN), F32),
                 pltpu.VMEM((block, width), F32),
-                pltpu.SemaphoreType.DMA((14,)),
+                pltpu.SemaphoreType.DMA((8,)),
             ],
         ),
         out_shape=(
@@ -974,34 +1300,356 @@
     )(meta, adapted, heads, cotangent, *gains, *weights)
 
 
+class Reduction:
+    def __init__(self, shape, by_lane=False, folded=False, cuts=None):
+        self.rows, self.lanes = shape
+        self.by_lane = by_lane
+        self.folded = folded
+        self.cuts = cuts or [self.lanes]
+
+    def outputs(self):
+        return [jax.ShapeDtypeStruct((self.rows, lanes), F32) for lanes in self.cuts]
+
+    def scratch(self, dp):
+        rows, lanes = self.rows, self.lanes
+        quarter = (rows // 4, lanes)
+        chunk = (rows // 4, lanes // dp) if self.by_lane else (rows // 4 // dp, lanes)
+        refs = [
+            pltpu.VMEM(quarter, BF16),
+            pltpu.VMEM((dp + 1,) + chunk, BF16),
+            pltpu.VMEM(quarter, BF16),
+            pltpu.VMEM((3,) + quarter, BF16),
+            [pltpu.VMEM((rows // 4, cut), F32) for cut in self.cuts],
+            pltpu.SemaphoreType.DMA((5,)),
+            pltpu.SemaphoreType.DMA((5,)),
+            pltpu.SemaphoreType.DMA((dp,)),
+            pltpu.SemaphoreType.DMA((dp + 1,)),
+            pltpu.SemaphoreType.DMA((2, dp)),
+            pltpu.SemaphoreType.DMA((dp,)),
+            pltpu.SemaphoreType.DMA((len(self.cuts),)),
+        ]
+        refs = refs[:4] + refs[4] + refs[5:]
+        if not self.folded:
+            refs += [pltpu.VMEM((rows // 2, lanes), BF16)] * 2 + [pltpu.VMEM(quarter, BF16)]
+        return refs
+
+    def bind(self, part, outs, refs):
+        self.part, self.outs = part, outs
+        count = len(self.cuts)
+        self.quarter, self.z_land, self.whole, self.others = refs[:4]
+        self.wide = refs[4 : 4 + count]
+        (
+            self.send,
+            self.recv,
+            self.sum_send,
+            self.sum_recv,
+            self.all_send,
+            self.all_recv,
+            self.out_sem,
+        ) = refs[4 + count : 11 + count]
+        if not self.folded:
+            self.half, self.core_land, self.x_land = refs[11 + count :]
+        self.x, self.core, self.z = (lax.axis_index(name) for name in ("x", "core", "dp"))
+        self.dp = lax.axis_size("dp")
+        self.to_core = {"core": 1 - self.core}
+        self.to_x = {"x": 1 - self.x}
+        self.sends = []
+
+    def copy(self, src, dst, send, recv, where):
+        return pltpu.make_async_remote_copy(
+            src_ref=src,
+            dst_ref=dst,
+            send_sem=send,
+            recv_sem=recv,
+            device_id=where,
+            device_id_type=MESH,
+        )
+
+    def part_of(self, ref, index, rows):
+        return ref.at[pl.ds(pl.multiple_of(index * rows, rows), rows)]
+
+    def chunk(self, ref, index):
+        if self.by_lane:
+            lanes = self.lanes // self.dp
+            return ref.at[:, pl.ds(pl.multiple_of(index * lanes, lanes), lanes)]
+        return self.part_of(ref, index, self.rows // 4 // self.dp)
+
+    def core_sum(self):
+        half = self.rows // 2
+        return self.copy(
+            self.part_of(self.part, 1 - self.core, half),
+            self.core_land,
+            self.send.at[0],
+            self.recv.at[0],
+            self.to_core,
+        )
+
+    def x_sum(self):
+        quarter = self.rows // 4
+        return self.copy(
+            self.part_of(self.half, 1 - self.x, quarter),
+            self.x_land,
+            self.send.at[1],
+            self.recv.at[1],
+            self.to_x,
+        )
+
+    def z_sum(self, j, step):
+        up = {"dp": self.z + step}
+        index = j
+        lands = index if step > 0 else jnp.where(self.z - 1 == index, self.dp, index)
+        return self.copy(
+            self.chunk(self.quarter, index),
+            self.z_land.at[lands],
+            self.sum_send.at[index],
+            self.sum_recv.at[lands],
+            up,
+        )
+
+    def z_all(self, j, step):
+        return self.copy(
+            self.chunk(self.whole, j),
+            self.chunk(self.whole, j),
+            self.all_send.at[0 if step > 0 else 1, j],
+            self.all_recv.at[j],
+            {"dp": self.z + step},
+        )
+
+    def spread(self, which):
+        src = self.others.at[0] if which == 2 else self.whole
+        return self.copy(
+            src,
+            self.others.at[which],
+            self.send.at[2 + which],
+            self.recv.at[2 + which],
+            self.to_x if which == 0 else self.to_core,
+        )
+
+    def writes(self, at):
+        quarter = self.rows // 4
+        core = self.core if at < 2 else 1 - self.core
+        x = self.x if at % 2 == 0 else 1 - self.x
+        row = pl.multiple_of((2 * core + x) * quarter, quarter)
+        return [
+            pltpu.make_async_copy(wide, out.at[pl.ds(row, quarter)], self.out_sem.at[i])
+            for i, (wide, out) in enumerate(zip(self.wide, self.outs))
+        ]
+
+    def emit(self, at, ref):
+        if at > 0:
+            for copy in self.writes(at - 1):
+                copy.wait()
+        lane = 0
+        for wide, lanes in zip(self.wide, self.cuts):
+            wide[...] = ref[:, lane : lane + lanes].astype(F32)
+            lane += lanes
+        for copy in self.writes(at):
+            copy.start()
+
+    def add(self, into, left, right):
+        into[...] = (left[...].astype(F32) + right[...].astype(F32)).astype(BF16)
+
+    def hop(self, h):
+        last = self.dp - 1
+
+        @pl.when(self.z == h)
+        def _():
+            for j in range(last, h, -1):
+                if h > 0:
+                    self.wait_sum(j)
+                    self.add(self.chunk(self.quarter, j), self.chunk(self.quarter, j), self.z_land.at[j])
+                self.z_sum(j, 1).start()
+
+        @pl.when(self.z == last - h)
+        def _():
+            for j in range(0, last - h):
+                if h > 0:
+                    self.wait_sum(j)
+                    self.add(self.chunk(self.quarter, j), self.chunk(self.quarter, j), self.z_land.at[j])
+                self.z_sum(j, -1).start()
+
+    def wait_sum(self, lands):
+        self.copy(
+            self.z_land.at[lands],
+            self.z_land.at[lands],
+            self.sum_send.at[0],
+            self.sum_recv.at[lands],
+            self.to_x,
+        ).wait_recv()
+
+    def all_hop(self, h):
+        z, last = self.z, self.dp - 1
+        low, high = jnp.maximum(z - h, 0), jnp.minimum(z + h, last)
+
+        @pl.when(z >= h)
+        def _():
+            self.z_all(low, 1).wait_recv()
+
+        @pl.when((z >= h) & (z < last))
+        def _():
+            self.z_all(low, 1).start()
+
+        @pl.when(z <= last - h)
+        def _():
+            self.z_all(high, -1).wait_recv()
+
+        @pl.when((z <= last - h) & (z > 0))
+        def _():
+            self.z_all(high, -1).start()
+
+    def stages(self):
+        def start():
+            self.core_sum().start()
+
+        def fold_core():
+            self.core_sum().wait_recv()
+            self.add(
+                self.half, self.part_of(self.part, self.core, self.rows // 2), self.core_land
+            )
+            self.x_sum().start()
+
+        def begin():
+            self.quarter[...] = self.part[...]
+            self.hop(0)
+
+        def fold_x():
+            self.x_sum().wait_recv()
+            self.add(
+                self.quarter, self.part_of(self.half, self.x, self.rows // 4), self.x_land
+            )
+            self.hop(0)
+
+        def settle():
+            z, last = self.z, self.dp - 1
+            mine = self.chunk(self.quarter, z)
+
+            @pl.when(z > 0)
+            def _():
+                self.wait_sum(z)
+                self.add(mine, mine, self.z_land.at[z])
+
+            @pl.when(z < last)
+            def _():
+                self.wait_sum(self.dp)
+                self.add(mine, mine, self.z_land.at[self.dp])
+
+            self.chunk(self.whole, z)[...] = mine[...]
+
+            @pl.when(z < last)
+            def _():
+                self.z_all(z, 1).start()
+
+            @pl.when(z > 0)
+            def _():
+                self.z_all(z, -1).start()
+
+        def share():
+            self.all_hop(self.dp - 1)
+            self.spread(0).start()
+            self.spread(1).start()
+            self.emit(0, self.whole)
+
+        def pass_on():
+            self.spread(0).wait_recv()
+            self.spread(2).start()
+            self.emit(1, self.others.at[0])
+
+        def last():
+            self.spread(1).wait_recv()
+            self.emit(2, self.others.at[1])
+            self.spread(2).wait_recv()
+            self.emit(3, self.others.at[2])
+
+        return (
+            ([begin] if self.folded else [start, fold_core, fold_x])
+            + [functools.partial(self.hop, h) for h in range(1, self.dp - 1)]
+            + [settle]
+            + [functools.partial(self.all_hop, h) for h in range(1, self.dp - 1)]
+            + [share, pass_on, last]
+        )
+
+    def drain(self):
+        z, last = self.z, self.dp - 1
+        if not self.folded:
+            self.core_sum().wait_send()
+            self.x_sum().wait_send()
+        for j in range(self.dp):
+
+            @pl.when(z < j)
+            def _():
+                self.z_sum(j, 1).wait_send()
+
+            @pl.when(z > j)
+            def _():
+                self.z_sum(j, -1).wait_send()
+
+            @pl.when((z >= j) & (z < last))
+            def _():
+                self.z_all(j, 1).wait_send()
+
+            @pl.when((z <= j) & (z > 0))
+            def _():
+                self.z_all(j, -1).wait_send()
+
+        for which in range(3):
+            self.spread(which).wait_send()
+        for copy in self.writes(3):
+            copy.wait()
+
+
+def bind_all(items, parts, outs, scratch):
+    dp = lax.axis_size("dp")
+    for item, part in zip(items, parts):
+        size = len(item.scratch(dp))
+        item.bind(part, outs[: len(item.cuts)], scratch[:size])
+        outs, scratch = outs[len(item.cuts) :], scratch[size:]
+
+
+def waves(plans):
+    length = max(len(plan) + i for i, plan in enumerate(plans))
+    return [
+        [plan[t - i] for i, plan in enumerate(plans) if 0 <= t - i < len(plan)]
+        for t in range(length)
+    ]
+
+
+def greet_line(barrier):
+    z, last = lax.axis_index("dp"), lax.axis_size("dp") - 1
+
+    @pl.when(z > 0)
+    def _():
+        pl.semaphore_signal(barrier, inc=1, device_id={"dp": z - 1}, device_id_type=MESH)
+
+    @pl.when(z < last)
+    def _():
+        pl.semaphore_signal(barrier, inc=1, device_id={"dp": z + 1}, device_id_type=MESH)
+
+    return jnp.minimum(z, 1) + jnp.minimum(last - z, 1)
+
+
 LEAVE = 128
 
 
-def leave_kernel(
-    sent,
-    adapted,
-    middle_back,
-    gain,
-    query_w,
-    key_w,
-    value_w,
-    joined,
-    adapted_low,
-    gain_out,
-    landed,
-    away,
-    away_landed,
-    part_send,
-    part_recv,
-    away_send,
-    away_recv,
-    low_send,
-    low_recv,
-):
+def leave_kernel(items, *refs):
+    sent, adapted, middle_back, gain, query_w, key_w, value_w = refs[:7]
+    parts, refs = refs[7 : 7 + len(items)], refs[7 + len(items) :]
+    joined, adapted_low, gain_out = refs[:3]
+    count = sum(len(item.cuts) for item in items)
+    outs, refs = refs[3 : 3 + count], refs[3 + count :]
+    landed, away, away_landed = refs[:3]
+    part_send, part_recv, away_send, away_recv, low_send, low_recv = refs[3:9]
+    bind_all(items, parts, outs, refs[9:])
+    plans = [item.stages() for item in items]
+    stages = list(zip(*plans))
+    away_plan = {0: stages[0]}
+    home_plan = {1: stages[1], 4: stages[2]}
     me, others = neighbours()
     tensor = lax.axis_index("tensor")
     tensor_peer = {"tensor": 1 - tensor}
-    greet(tensor_peer, others)
+    barrier = pltpu.get_barrier_semaphore()
+    for target in [tensor_peer] + [where for _, where in others]:
+        pl.semaphore_signal(barrier, inc=1, device_id=target, device_id_type=MESH)
+    pl.semaphore_wait(barrier, 1 + len(others) + greet_line(barrier))
     half = adapted.shape[0]
     inner = query_w.shape[1]
     steps = half // LEAVE
@@ -1069,6 +1717,7 @@
     def away_step(i, _):
         away[block(0, i), :] = input_grad(0, i).astype(BF16)
         hand_over(i).start()
+        at_step(i, away_plan)
         return 0
 
     lax.fori_loop(0, steps, away_step, 0)
@@ -1086,9 +1735,15 @@
         gain_out[0:1, :] += jnp.sum(upstream * normed, axis=0, keepdims=True)
         adapted_low[block(tensor * half, i), :] = (middle_back[rows, :] + inward).astype(BF16)
         share(i).start()
+        at_step(i, home_plan)
         return 0
 
     lax.fori_loop(0, steps, home_step, 0)
+    for wave in waves([plan[3:] for plan in plans]):
+        for call in wave:
+            call()
+    for item in items:
+        item.drain()
 
     def finish(i, _):
         for side in range(2):
@@ -1101,21 +1756,30 @@
     lax.fori_loop(0, steps, finish, 0)
 
 
-def leave(sent, adapted, middle_back, gain, query_w, key_w, value_w):
+def leave(sent, adapted, middle_back, gain, query_w, key_w, value_w, parts, kinds):
+    items = [
+        Reduction((4 * part.shape[0], part.shape[1]), by_lane, True, cuts)
+        for part, (by_lane, cuts) in zip(parts, kinds)
+    ]
+    scratch, outs = [], []
+    for item in items:
+        scratch += item.scratch(lax.axis_size("dp"))
+        outs += item.outputs()
     peers, rows, lanes = sent.shape
     half, width = adapted.shape
     inner = query_w.shape[1]
     steps = half // LEAVE
     vmem = pl.BlockSpec(memory_space=pltpu.VMEM)
     return pl.pallas_call(
-        leave_kernel,
+        functools.partial(leave_kernel, items),
         out_shape=(
             jax.ShapeDtypeStruct((rows, 3 * inner), BF16),
             jax.ShapeDtypeStruct((rows, width), BF16),
             jax.ShapeDtypeStruct((8, width), F32),
-        ),
-        in_specs=[vmem] * 7,
-        out_specs=(vmem,) * 3,
+        )
+        + tuple(outs),
+        in_specs=[vmem] * (7 + len(items)),
+        out_specs=(vmem,) * 3 + (pl.BlockSpec(memory_space=pl.ANY),) * len(outs),
         scratch_shapes=[
             pltpu.VMEM((peers, rows, lanes), BF16),
             pltpu.VMEM((half, width), BF16),
@@ -1123,7 +1787,8 @@
             pltpu.SemaphoreType.DMA((2, steps, 3)),
             pltpu.SemaphoreType.DMA((2, steps, 3)),
         ]
-        + [pltpu.SemaphoreType.DMA((steps,))] * 4,
+        + [pltpu.SemaphoreType.DMA((steps,))] * 4
+        + scratch,
         compiler_params=pltpu.CompilerParams(
             vmem_limit_bytes=VMEM_BYTES, collective_id=1, has_side_effects=True
         ),
@@ -1131,353 +1796,50 @@
             flops=2 * rows * width * 3 * inner, bytes_accessed=200 << 20, transcendentals=rows
         ),
         name="leave",
-    )(sent, adapted, middle_back, gain, query_w, key_w, value_w)
-
-
-class Reduction:
-    def __init__(self, shape, by_lane, halved):
-        self.rows, self.lanes = shape
-        self.by_lane = by_lane
-        self.halved = halved
-
-    def scratch(self, dp):
-        rows, lanes = self.rows, self.lanes
-        quarter = (rows // 4, lanes)
-        chunk = (rows // 4, lanes // dp) if self.by_lane else (rows // 4 // dp, lanes)
-        refs = [
-            pltpu.VMEM(quarter, BF16),
-            pltpu.VMEM(quarter, BF16),
-            pltpu.VMEM((dp + 1,) + chunk, BF16),
-            pltpu.VMEM(quarter, BF16),
-            pltpu.VMEM((3,) + quarter, BF16),
-            pltpu.VMEM(quarter, F32),
-            pltpu.SemaphoreType.DMA((5,)),
-            pltpu.SemaphoreType.DMA((5,)),
-            pltpu.SemaphoreType.DMA((dp,)),
-            pltpu.SemaphoreType.DMA((dp + 1,)),
-            pltpu.SemaphoreType.DMA((2, dp)),
-            pltpu.SemaphoreType.DMA((dp,)),
-            pltpu.SemaphoreType.DMA((4,)),
-        ]
-        if not self.halved:
-            refs += [pltpu.VMEM((rows // 2, lanes), BF16)] * 2
-        return refs
-
-    def bind(self, part, out, refs):
-        self.part, self.out = part, out
-        (
-            self.x_land,
-            self.quarter,
-            self.z_land,
-            self.whole,
-            self.others,
-            self.wide,
-            self.send,
-            self.recv,
-            self.sum_send,
-            self.sum_recv,
-            self.all_send,
-            self.all_recv,
-            self.out_sem,
-        ) = refs[:13]
-        if self.halved:
-            self.half = part
-        else:
-            self.half, self.core_land = refs[13:]
-        self.x, self.core, self.z = (lax.axis_index(name) for name in ("x", "core", "dp"))
-        self.dp = lax.axis_size("dp")
-        self.to_core = {"core": 1 - self.core}
-        self.to_x = {"x": 1 - self.x}
-        self.sends = []
-
-    def copy(self, src, dst, send, recv, where):
-        return pltpu.make_async_remote_copy(
-            src_ref=src,
-            dst_ref=dst,
-            send_sem=send,
-            recv_sem=recv,
-            device_id=where,
-            device_id_type=MESH,
-        )
-
-    def part_of(self, ref, index, rows):
-        return ref.at[pl.ds(pl.multiple_of(index * rows, rows), rows)]
-
-    def chunk(self, ref, index):
-        if self.by_lane:
-            lanes = self.lanes // self.dp
-            return ref.at[:, pl.ds(pl.multiple_of(index * lanes, lanes), lanes)]
-        return self.part_of(ref, index, self.rows // 4 // self.dp)
-
-    def core_sum(self):
-        half = self.rows // 2
-        return self.copy(
-            self.part_of(self.part, 1 - self.core, half),
-            self.core_land,
-            self.send.at[0],
-            self.recv.at[0],
-            self.to_core,
-        )
-
-    def x_sum(self):
-        quarter = self.rows // 4
-        return self.copy(
-            self.part_of(self.half, 1 - self.x, quarter),
-            self.x_land,
-            self.send.at[1],
-            self.recv.at[1],
-            self.to_x,
-        )
-
-    def z_sum(self, j, step):
-        up = {"dp": self.z + step}
-        index = j
-        lands = index if step > 0 else jnp.where(self.z - 1 == index, self.dp, index)
-        return self.copy(
-            self.chunk(self.quarter, index),
-            self.z_land.at[lands],
-            self.sum_send.at[index],
-            self.sum_recv.at[lands],
-            up,
-        )
-
-    def z_all(self, j, step):
-        return self.copy(
-            self.chunk(self.whole, j),
-            self.chunk(self.whole, j),
-            self.all_send.at[0 if step > 0 else 1, j],
-            self.all_recv.at[j],
-            {"dp": self.z + step},
-        )
-
-    def spread(self, which):
-        src = self.others.at[0] if which == 2 else self.whole
-        return self.copy(
-            src,
-            self.others.at[which],
-            self.send.at[2 + which],
-            self.recv.at[2 + which],
-            self.to_x if which == 0 else self.to_core,
-        )
-
-    def write(self, at, core, x, value):
-        quarter = self.rows // 4
-        row = pl.multiple_of((2 * core + x) * quarter, quarter)
-        return pltpu.make_async_copy(
-            self.wide, self.out.at[pl.ds(row, quarter)], self.out_sem.at[at]
-        )
-
-    def emit(self, at, core, x, ref):
-        if at > 0:
-            self.last_write.wait()
-        self.wide[...] = ref[...].astype(F32)
-        self.last_write = self.write(at, core, x, ref)
-        self.last_write.start()
-
-    def add(self, into, left, right):
-        into[...] = (left[...].astype(F32) + right[...].astype(F32)).astype(BF16)
-
-    def hop(self, h):
-        last = self.dp - 1
-
-        @pl.when(self.z == h)
-        def _():
-            for j in range(last, h, -1):
-                if h > 0:
-                    self.wait_sum(j)
-                    self.add(self.chunk(self.quarter, j), self.chunk(self.quarter, j), self.z_land.at[j])
-                self.z_sum(j, 1).start()
-
-        @pl.when(self.z == last - h)
-        def _():
-            for j in range(0, last - h):
-                if h > 0:
-                    self.wait_sum(j)
-                    self.add(self.chunk(self.quarter, j), self.chunk(self.quarter, j), self.z_land.at[j])
-                self.z_sum(j, -1).start()
-
-    def wait_sum(self, lands):
-        self.copy(
-            self.z_land.at[lands],
-            self.z_land.at[lands],
-            self.sum_send.at[0],
-            self.sum_recv.at[lands],
-            self.to_x,
-        ).wait_recv()
-
-    def all_hop(self, h):
-        z, last = self.z, self.dp - 1
-        low, high = jnp.maximum(z - h, 0), jnp.minimum(z + h, last)
-
-        @pl.when(z >= h)
-        def _():
-            self.z_all(low, 1).wait_recv()
-
-        @pl.when((z >= h) & (z < last))
-        def _():
-            self.z_all(low, 1).start()
-
-        @pl.when(z <= last - h)
-        def _():
-            self.z_all(high, -1).wait_recv()
-
-        @pl.when((z <= last - h) & (z > 0))
-        def _():
-            self.z_all(high, -1).start()
-
-    def stages(self):
-        def start():
-            if self.halved:
-                self.x_sum().start()
-            else:
-                self.core_sum().start()
-
-        def fold_core():
-            if not self.halved:
-                self.core_sum().wait_recv()
-                self.add(
-                    self.half, self.part_of(self.part, self.core, self.rows // 2), self.core_land
-                )
-                self.x_sum().start()
-
-        def fold_x():
-            self.x_sum().wait_recv()
-            self.add(
-                self.quarter, self.part_of(self.half, self.x, self.rows // 4), self.x_land
-            )
-            self.hop(0)
-
-        def settle():
-            z, last = self.z, self.dp - 1
-            mine = self.chunk(self.quarter, z)
-
-            @pl.when(z > 0)
-            def _():
-                self.wait_sum(z)
-                self.add(mine, mine, self.z_land.at[z])
-
-            @pl.when(z < last)
-            def _():
-                self.wait_sum(self.dp)
-                self.add(mine, mine, self.z_land.at[self.dp])
-
-            self.chunk(self.whole, z)[...] = mine[...]
-
-            @pl.when(z < last)
-            def _():
-                self.z_all(z, 1).start()
-
-            @pl.when(z > 0)
-            def _():
-                self.z_all(z, -1).start()
-
-        def share():
-            self.all_hop(self.dp - 1)
-            self.spread(0).start()
-            self.spread(1).start()
-            self.emit(0, self.core, self.x, self.whole)
-
-        def pass_on():
-            self.spread(0).wait_recv()
-            self.spread(2).start()
-            self.emit(1, self.core, 1 - self.x, self.others.at[0])
-
-        def last():
-            self.spread(1).wait_recv()
-            self.emit(2, 1 - self.core, self.x, self.others.at[1])
-            self.spread(2).wait_recv()
-            self.emit(3, 1 - self.core, 1 - self.x, self.others.at[2])
-
-        return (
-            [start, fold_core, fold_x]
-            + [functools.partial(self.hop, h) for h in range(1, self.dp - 1)]
-            + [settle]
-            + [functools.partial(self.all_hop, h) for h in range(1, self.dp - 1)]
-            + [share, pass_on, last]
-        )
-
-    def drain(self):
-        z, last = self.z, self.dp - 1
-        if not self.halved:
-            self.core_sum().wait_send()
-        self.x_sum().wait_send()
-        for j in range(self.dp):
-
-            @pl.when(z < j)
-            def _():
-                self.z_sum(j, 1).wait_send()
-
-            @pl.when(z > j)
-            def _():
-                self.z_sum(j, -1).wait_send()
-
-            @pl.when((z >= j) & (z < last))
-            def _():
-                self.z_all(j, 1).wait_send()
-
-            @pl.when((z <= j) & (z > 0))
-            def _():
-                self.z_all(j, -1).wait_send()
-
-        for which in range(3):
-            self.spread(which).wait_send()
-        self.last_write.wait()
+    )(sent, adapted, middle_back, gain, query_w, key_w, value_w, *parts)
 
 
 def reduce_kernel(items, *refs):
     count = len(items)
-    parts, outs, rest = refs[:count], refs[count : 2 * count], refs[2 * count :]
-    dp = lax.axis_size("dp")
-    z = lax.axis_index("dp")
-    for item, part, out in zip(items, parts, outs):
-        size = len(item.scratch(dp))
-        item.bind(part, out, rest[:size])
-        rest = rest[size:]
+    outs = sum(len(item.cuts) for item in items)
+    bind_all(items, refs[:count], refs[count : count + outs], refs[count + outs :])
     barrier = pltpu.get_barrier_semaphore()
-    pl.semaphore_signal(barrier, inc=1, device_id=items[0].to_core, device_id_type=MESH)
-    pl.semaphore_signal(barrier, inc=1, device_id=items[0].to_x, device_id_type=MESH)
-
-    @pl.when(z > 0)
-    def _():
-        pl.semaphore_signal(barrier, inc=1, device_id={"dp": z - 1}, device_id_type=MESH)
-
-    @pl.when(z < dp - 1)
-    def _():
-        pl.semaphore_signal(barrier, inc=1, device_id={"dp": z + 1}, device_id_type=MESH)
-
-    pl.semaphore_wait(barrier, 2 + jnp.minimum(z, 1) + jnp.minimum(dp - 1 - z, 1))
+    for target in (items[0].to_core, items[0].to_x):
+        pl.semaphore_signal(barrier, inc=1, device_id=target, device_id_type=MESH)
+    pl.semaphore_wait(barrier, 2 + greet_line(barrier))
     plans = [item.stages() for item in items]
-    for time in range(len(plans[0]) + count - 1):
-        for at, plan in enumerate(plans):
-            if 0 <= time - at < len(plan):
-                plan[time - at]()
+    for plan in plans:
+        plan[0]()
+    for plan in plans:
+        plan[1]()
+    for wave in waves([plan[2:] for plan in plans]):
+        for call in wave:
+            call()
     for item in items:
         item.drain()
 
 
-def reduce_all(parts, kinds, name, number):
+def reduce_all(parts, cuts):
     dp = lax.axis_size("dp")
-    items = []
-    for part, (by_lane, halved) in zip(parts, kinds):
-        rows, lanes = part.shape
-        items.append(Reduction((2 * rows if halved else rows, lanes), by_lane, halved))
-    scratch = []
+    items = [Reduction(part.shape, cuts=cut) for part, cut in zip(parts, cuts)]
+    scratch, outs = [], []
     for item in items:
         scratch += item.scratch(dp)
+        outs += item.outputs()
     moved = sum(item.rows * item.lanes for item in items)
     return pl.pallas_call(
         functools.partial(reduce_kernel, items),
-        out_shape=tuple(jax.ShapeDtypeStruct((item.rows, item.lanes), F32) for item in items),
+        out_shape=tuple(outs),
         in_specs=[pl.BlockSpec(memory_space=pltpu.VMEM)] * len(items),
-        out_specs=(pl.BlockSpec(memory_space=pl.ANY),) * len(items),
+        out_specs=(pl.BlockSpec(memory_space=pl.ANY),) * len(outs),
         scratch_shapes=scratch,
         compiler_params=pltpu.CompilerParams(
-            vmem_limit_bytes=VMEM_BYTES, collective_id=number, has_side_effects=True
+            vmem_limit_bytes=VMEM_BYTES, collective_id=2, has_side_effects=True
         ),
         cost_estimate=pl.CostEstimate(
             flops=moved * 4, bytes_accessed=moved * 30, transcendentals=0
         ),
-        name=name,
+        name="reduce_all",
     )(*parts)
 
 
@@ -1561,21 +1923,11 @@
     adapted = cut(mine, tensor, half_rows).astype(F32) + cut(theirs, tensor, half_rows).astype(
         F32
     )
-    quarter = 2 * x + core
-    pair = jnp.concatenate(
-        [cut(weight, quarter, width // 4) for weight in (gate_weight, up_weight)], axis=1
-    )
-    stack = jnp.concatenate(
-        [cut(weight, quarter, weight.shape[0] // 4) for weight in (output_weight, down_weight)],
-        axis=0,
-    )
-    pair, stack, parts = together(pair, stack, parts)
-    pair_all = lax.all_gather(pair, ("tensor", "x", "core"), axis=0, tiled=True)
-    stack_all = lax.all_gather(stack, ("tensor", "x", "core"), axis=0, tiled=False)
-
-    attended, logsum = attention_forward(parents, parts)
+    role, place, parts = sort_parts(parents, parts.reshape(-1, 3 * WIDE))
+    own_weights = (output_weight, gate_weight, up_weight, down_weight)
+    attended, logsum, *other_weights = attention_forward(parts, own_weights)
     heads = lax.all_to_all(
-        attended.reshape(8, half_rows, WIDE), everyone, 0, 0, tiled=False
+        pick(place, attended).reshape(8, half_rows, WIDE), everyone, 0, 0, tiled=False
     )
     (
         layer_half,
@@ -1594,7 +1946,7 @@
         heads,
         cotangent,
         (one_row(second_gain), one_row(third_gain), one_row(fourth_gain)),
-        (output_weight, gate_weight, up_weight, down_weight, pair_all, stack_all),
+        own_weights + tuple(other_weights),
     )
     upstream = lax.all_to_all(heads_back, everyone, 0, 0, tiled=False).reshape(-1, WIDE)
     layer_other = swap(layer_half, "tensor")
@@ -1609,57 +1961,61 @@
     split = gate_weight.shape[1]
     inner = output_weight.shape[0]
     sides = []
-    for left, right, cut_at in (
-        (third_low, pair_low, 2 * split),
-        (hidden, mixed_low, split),
-        (attended_all, attention_low, inner),
-    ):
-        for side in (slice(None, cut_at), slice(cut_at, None)):
-            part = (
-                tn(left, right[:, side]) if right is pair_low else tn(left[:, side], right)
-            )
-            sides.append(fold(part, core, "core"))
-    upstream, *sides = together(upstream, *sides)
-    away = [swap(side, "tensor") for side in sides[1::2]]
-
+    lanes = [pair_low[:, i * split : (i + 1) * split] for i in range(4)]
+    sides += [tn(third_low, lanes[0]), tn(third_low, lanes[2])]
+    sides += [tn(hidden[:, :split], mixed_low), tn(hidden[:, split:], mixed_low)]
+    sides += [tn(third_low, lanes[1]), tn(third_low, lanes[3])]
+    sides += [
+        tn(attended_all[:, :inner], attention_low),
+        tn(attended_all[:, inner:], attention_low),
+    ]
     table_cosine, table_sine = angle_tables(jnp.arange((TRUNK + 2) * SEG))
-    sent = attention_backward(
-        parents, parts, upstream, attended, logsum, table_cosine, table_sine
-    )
-    joined, adapted_low, first_gain_part = leave(
-        sent.reshape(4, rows, 3 * WIDE),
+    sent, *sums = attention_backward(
+        parts, pick(role, upstream), attended, logsum, table_cosine, table_sine, sides
+    )
+    (
+        joined,
+        adapted_low,
+        first_gain_part,
+        gate_total,
+        down_total,
+        up_total,
+        output_total,
+    ) = leave(
+        pick(place, sent).reshape(4, rows, 3 * WIDE),
         adapted,
         middle_back,
         one_row(first_gain),
         query_weight,
         key_weight,
         value_weight,
+        sums,
+        [(False, None), (True, None), (False, None), (False, None)],
     )
     adapter_part = jnp.einsum(
         "rcd,re->cde", latent_embed, adapted_low, preferred_element_type=F32
     ).astype(BF16)
-    kept = [add_low(own, theirs) for own, theirs in zip(sides[0::2], away)]
-    pair_total, down_total, output_total, input_total, adapter_total = reduce_all(
-        kept + [tn(first_low, joined), adapter_part.reshape(-1, width)],
-        [(False, True), (True, True), (False, True), (False, False), (False, False)],
-        "reduce_all",
-        2,
-    )
+    query_total, key_total, value_total, *adapter_total = reduce_all(
+        [tn(first_low, joined[:, i * inner : (i + 1) * inner]) for i in range(3)]
+        + [adapter_part[0], adapter_part[1]],
+        [None] * 5,
+    )
+    adapter_total = jnp.stack(adapter_total)
     latent_gradient = jnp.einsum("re,cde->rcd", adapted_low, adapter, preferred_element_type=F32)
     gains = sum_small(jnp.concatenate([gain_parts[:3], first_gain_part[:1]], axis=0))
     return (
         layer_out,
         latent_gradient,
-        adapter_total.reshape(adapter.shape),
+        adapter_total,
         gains[3],
-        input_total[:, :inner],
-        input_total[:, inner : 2 * inner],
-        input_total[:, 2 * inner :],
+        query_total,
+        key_total,
+        value_total,
         output_total,
         gains[0],
         gains[1],
-        pair_total[:, :split],
-        pair_total[:, split:],
+        gate_total,
+        up_total,
         down_total,
         gains[2],
     )

time: 877 us -> 714 us (0.81)
  waiting for transfers between devices: 136 us -> 6.95 us
  local copies, waits for them, and re-layouts: 58.6 us -> 33.9 us
  matrix products: 38.6 us -> 60.5 us
  other arithmetic: 45.1 us -> 25 us
  Pallas kernels: 549 us -> 563 us
  between operations: 15 us -> 1.18 us
    ppermute x13 -> x4, waiting for transfers between devices: 70.5 us -> 0.3 us  [swap(): return lax.ppermute(value, axis, [(0, 1), (1, 0)])]
    all_gather x2 -> x0, waiting for transfers between devices: 41.3 us -> none  [the longest x1 41.3 us: on_device_paired(): pair_all = lax.all_gather(pair, ('tensor', 'x', 'core'), axis=0, tiled=True)]
    convert_element_type x9 -> x0, other arithmetic: 22.3 us -> none  [add_low(): return (left.astype(F32) + right.astype(F32)).astype(BF16)]
    dot_general x7 -> x11, matrix products: 25.7 us -> 44.4 us  [tn(): lax.dot_general(left, right, (((0,), (0,)), ((), ())), preferred_element_...]
    all_to_all x1, waiting for transfers between devices: 23.7 us -> 6.64 us  [on_device_paired(): lax.all_to_all(pick(place, attended).reshape(8, half_rows, WIDE), everyon...]
    pallas_call x4 -> x8, Pallas kernels: 409 us -> 423 us  [the longest x1 151 us: leave(): pl.pallas_call(functools.partial(leave_kernel, items), out_shape=(jax.Sha...]
    slice x2 -> x0, local copies, waits for them, and re-layouts: 13 us -> none  [the longest x1 9.64 us: on_device_paired(): pair_total[:, split:]]
    dynamic_slice x9 -> x0, local copies, waits for them, and re-layouts: 10.4 us -> none  [cut(): return lax.dynamic_slice_in_dim(value, index * rows, rows, 0)]
  transfers between devices with their start and end apart: 19 -> 8, of which waited for: 4 -> 2; matrix products, arithmetic and copies ran while one was open for 9% -> 9% of each run, Pallas kernels for 25% -> 48%
where the time goes in v3:
time: 714 us; the launch traced here: 708 us
  Pallas kernels  563 us (79%)
  matrix products  60.5 us (8%)
  local copies, waits for them, and re-layouts  33.9 us (5%)
  other arithmetic  25 us (4%)
  starting transfers between devices  17.5 us (2%)
    pallas_call x1, Pallas kernels, leave(): pl.pallas_call(functools.partial(leave_kernel, items), out_shape=(jax.Sha...  151 us
    pallas_call x1, Pallas kernels, attention_backward(): pl.pallas_call(functools.partial(attention_back_kernel, folds), out_shape...  105 us
    pallas_call x1, Pallas kernels, reduce_all(): pl.pallas_call(functools.partial(reduce_kernel, items), out_shape=tuple(o...  78.5 us
    pallas_call x1, Pallas kernels, enter(): pl.pallas_call(enter_kernel, out_shape=(jax.ShapeDtypeStruct((peers, rows...  78.3 us
    pallas_call x1, Pallas kernels, attention_forward(): pl.pallas_call(functools.partial(attention_kernel, fetches), out_shape=(j...  74.7 us
    pallas_call x1, Pallas kernels, middle_section(): pl.pallas_call(middle_kernel, grid_spec=pltpu.PrefetchScalarGridSpec(num_...  61.7 us
    dot_general x11, matrix products, tn(): lax.dot_general(left, right, (((0,), (0,)), ((), ())), preferred_element_...  44.4 us
    unnamed x60, local copies, waits for them, and re-layouts  31 us
  transfers between devices with their start and end apart: 8, of which 2 were waited for; matrix products, arithmetic and copies ran while one was open for 9% of the time, Pallas kernels for 48%

profile of v3, /device:TPU:0, one launch (start us, length us, event | category | flops | bytes accessed | tf_op | source)
XLA Modules:
  0.0 707.8 jit_solution(12137966984957745698)
XLA Ops:
  2.3 5.9 bitcast_convert_fusion.mine
  8.1 3.7 fusion.20
  11.9 78.3 %enter.1 = (bf16[4,1280,384]{2,1,0:T(8,128)(2,1)}, bf16[1280,1024]{1,0:T(8,128)(2,1)}, bf16[1280,1024]{1,0:T(8,128)(2,1)}) custom-call(bf16[1280,1024]{1,0:T(8,128)(2,1)} %bitcast_convert_fusion.mine, f32[1,1024]{1,0:T(1,128)} %bitcast.66, bf16[1024,512]{1,0:T(8,128)(2,1)} %refs_4_.3, bf16[1024,512]{1,0:T(8,128)(2,1)} %refs_5_.1, bf16[1024,512]{1,0:T(8,128)(2,1)} %refs_6_.1, ...), custom_call_target="tpu_custom_call" | custom-call | flops 4026531840 | bytes 209715200 | tf_op jit(solution)/shard_map/enter/pallas_call | solution.py:1056
  90.2 4.5 sort_parts.1
  94.7 74.7 %attention_forward.1 = (bf16[5120,128]{1,0:T(8,128)(2,1)}, f32[5120,128]{1,0:T(8,128)}, bf16[512,1024]{1,0:T(8,128)(2,1)}, bf16[1024,1408]{1,0:T(8,128)(2,1)}, b...) custom-call(bf16[5120,384]{1,0:T(8,128)(2,1)} %get-tuple-element.56.refs_0_, bf16[512,1024]{1,0:T(8,128)(2,1)} %wo_own.1, ...), custom_call_target="tpu_custom_call" | custom-call | flops 10200547328 | bytes 7864320 | tf_op jit(solution)/shard_map/attention_forward/pallas_call | solution.py:592
  171.9 3.7 all-to-all-start
  176.3 3.8 convert_add_fusion.adapted.refs_1_
  180.0 6.3 fusion.16
  186.3 6.6 all-to-all-done.heads
  194.0 61.7 %middle_section.1 = (bf16[640,1024]{1,0:T(8,128)(2,1)}, f32[640,1024]{1,0:T(8,128)}, bf16[640,1024]{1,0:T(8,128)(2,1)}, bf16[640,1024]{1,0:T(8,128)(2,1)}, bf16[...) custom-call(s32[2]{0:T(128)} %pad_add_fusion.meta, ...), custom_call_target="tpu_custom_call" | custom-call | flops 24830279680 | bytes 43319296 | tf_op jit(solution)/shard_map/middle_section/pallas_call | solution.py:1244
  255.7 6.3 convolution_convert_fusion.refs_11_
  261.9 6.0 convolution_convert_fusion.1.refs_10_
  268.0 4.0 convolution_convert_fusion.2.refs_9_
  272.0 4.0 convolution_convert_fusion.3.refs_8_
  287.4 5.4 convolution_convert_fusion.4.refs_7_
  292.8 5.4 convolution_convert_fusion.5.refs_6_
  301.8 105.1 %attention_backward.1 = (bf16[5120,384]{1,0:T(8,128)(2,1)}, bf16[256,1408]{1,0:T(8,128)(2,1)}, bf16[352,1024]{1,0:T(8,128)(2,1)}, bf16[256,1408]{1,0:T(8,128)(2,1)}, bf16[128,1024]{1,0:T(8,128)(2,1)}) custom-call(bf16[5120,384]{1,0:T(8,128)(2,1)} %get-tuple-element.56.refs_0_, bf16[5120,128]{1,0:T(8,128)(2,1)} %pick.4.refs_1_, ...), custom_call_target="tpu_custom_call" | custom-call | flops 25501368320 | bytes 15728640 | tf_op jit(solution)/shard_map/attention_backward/pallas_call | solution.py:917
  406.9 4.4 pick.5
  411.3 150.6 %leave.1 = (bf16[1280,1536]{1,0:T(8,128)(2,1)}, bf16[1280,1024]{1,0:T(8,128)(2,1)}, f32[8,1024]{1,0:T(8,128)}, f32[1024,1408]{1,0:T(8,128)}, f32[1408,1024]{1,0:...) custom-call(bf16[4,1280,384]{2,1,0:T(8,128)(2,1)} %bitcast.55, f32[640,1024]{1,0:T(8,128)} %convert_add_fusion.adapted.refs_1_, ...), custom_call_target="tpu_custom_call" | custom-call | flops 4026531840 | bytes 209715200 | tf_op jit(solution)/shard_map/leave/pallas_call | solution.py:1773
  561.8 5.6 convert_bitcast_fusion
  567.5 4.7 fusion.2
  586.9 78.5 %reduce_all.1 = (f32[1024,512]{1,0:T(8,128)}, f32[1024,512]{1,0:T(8,128)}, f32[1024,512]{1,0:T(8,128)}, f32[512,1024]{1,0:T(8,128)}, f32[512,1024]{1,0:T(8,128)}) custom-call(bf16[1024,512]{1,0:T(8,128)(2,1)} %convolution_convert_fusion.8.refs_0_, bf16[1024,512]{1,0:T(8,128)(2,1)} %convolution_convert_fusion.7.refs_1_, ...), custom_call_target="tpu_custom_call" | custom-call | flops 10485760 | bytes 78643200 | tf_op jit(solution)/shard_map/reduce_all/pallas_call | solution.py:1830
  669.0 5.0 pad_maximum_fusion
  674.0 10.7 %copy.34 = f32[1280,2,512]{2,1,0:T(2,128)} copy(f32[1280,2,512]{2,0,1:T(8,128)S(1)} %bitcast.52) | data formatting | bytes 10485760
  (100 shorter events, 61.7 us)
Async XLA Ops:
  171.9 21.0 %all-to-all-start = ((bf16[8,640,128]{2,1,0:T(8,128)(2,1)}), bf16[8,640,128]{2,1,0:T(8,128)(2,1)S(1)}, u32[]{:S(2)}, u32[]{:S(2)}) async-start(bf16[8,640,128]{2,1,0:T(8,128)(2,1)} %bitcast.53), calls=%async_computation | async-start | bytes 2621440 | tf_op jit(solution)/shard_map/all_to_all | solution.py:1929
  255.7 6.3 copy-start.15
  261.9 6.0 copy-start.14
  261.9 6.0 copy-start.17
  276.0 22.2 %all-to-all-start.1 = ((bf16[8,640,128]{2,1,0:T(8,128)(2,1)}), bf16[8,640,128]{2,1,0:T(8,128)(2,1)S(1)}, u32[]{:S(2)}, u32[]{:S(2)}) async-start(bf16[8,640,128]{2,1,0:T(8,128)(2,1)} %get-tuple-element.64), calls=%async_computation.1 | async-start | bytes 2621440 | tf_op jit(solution)/shard_map/all_to_all | solution.py:1951
  279.8 405.5 %collective-permute-start = (bf16[640,1024]{1,0:T(8,128)(2,1)}, bf16[640,1024]{1,0:T(8,128)(2,1)}, u32[]{:S(2)}, u32[]{:S(2)}) collective-permute-start(bf16[640,1024]{1,0:T(8,128)(2,1)} %get-tuple-element.62), channel_id=1, source_target_pairs={{0,1},{1,0},{2,3},{3,2},{4,5},{5,4},{6,7},{7,6},{8,9},{9,8},{10,11... | collective-permute-start | bytes 3932168 | tf_op jit(solution)/shard_map/ppermute | solution.py:1847
  561.8 5.6 copy-start.10
  567.5 8.9 %copy-start.9 = (bf16[1280,1536]{1,0:T(8,128)(2,1)S(1)}, bf16[1280,1536]{1,0:T(8,128)(2,1)}, u32[]{:S(2)}) copy-start(bf16[1280,1536]{1,0:T(8,128)(2,1)} %get-tuple-element.80) | copy-start | bytes 11796484
  567.5 8.9 %copy-start.13 = (bf16[1280,1024]{1,0:T(8,128)(2,1)S(1)}, bf16[1280,1024]{1,0:T(8,128)(2,1)}, u32[]{:S(2)}) copy-start(bf16[1280,1024]{1,0:T(8,128)(2,1)} %get-tuple-element.79) | copy-start | bytes 7864324
  572.9 6.0 collective-permute-start.1
  579.0 2.6 collective-permute-start.2
  581.6 3.8 collective-permute-start.3
  585.4 80.1 %collective-permute-start.4 = (f32[4,1024]{1,0:T(4,128)S(1)}, f32[4,1024]{1,0:T(4,128)S(1)}, u32[]{:S(2)}, u32[]{:S(2)}) collective-permute-start(f32[4,1024]{1,0:T(4,128)S(1)} %add.56), channel_id=1, source_target_pairs={{0,8},{8,0},{16,24},{24,16},{1,9},{9,1},{17,25},{25,17},{2,10},{10... | collective-permute-start | bytes 49160 | tf_op jit(solution)/shard_map/ppermute | solution.py:1878
  586.9 87.1 %slice-start.6 = ((s8[5242880]{0:T(1024)(128)(4,1)}), s8[1048576]{0:T(1024)(128)(4,1)S(1)}, s32[]{:S(2)}) async-start(s8[5242880]{0:T(1024)(128)(4,1)} %bitcast.51), calls=%async_computation.8 | async-start | bytes 2097152
  665.5 19.2 %collective-permute-start.5 = (f32[4,1024]{1,0:T(4,128)S(1)}, f32[4,1024]{1,0:T(4,128)S(1)}, u32[]{:S(2)}, u32[]{:S(2)}) collective-permute-start(f32[4,1024]{1,0:T(4,128)S(1)} %add.57), channel_id=1, source_target_pairs={{0,16},{16,0},{8,24},{24,8},{1,17},{17,1},{9,25},{25,9},{2,18},{18... | collective-permute-start | bytes 49160 | tf_op jit(solution)/shard_map/ppermute | solution.py:1878
  669.0 5.0 slice-start.7
  674.0 11.3 %copy-start.7 = (bf16[640,1024]{1,0:T(8,128)(2,1)S(1)}, bf16[640,1024]{1,0:T(8,128)(2,1)}, u32[]{:S(2)}) copy-start(bf16[640,1024]{1,0:T(8,128)(2,1)} %get-tuple-element.62) | copy-start | bytes 3932164
  686.8 4.7 copy-start.4
  686.8 6.0 copy-start.3
  690.1 7.1 %slice-start.4 = ((s8[5767168]{0:T(1024)(128)(4,1)}), s8[4194304]{0:T(1024)(128)(4,1)S(1)}, s32[]{:S(2)}) async-start(s8[5767168]{0:T(1024)(128)(4,1)} %bitcast.49), calls=%async_computation.6 | async-start | bytes 8388608
  691.5 9.6 %slice-start.2 = ((s8[5767168]{0:T(1024)(128)(4,1)}), s8[4194304]{0:T(1024)(128)(4,1)S(1)}, s32[]{:S(2)}) async-start(s8[5767168]{0:T(1024)(128)(4,1)} %bitcast.47), calls=%async_computation.4 | async-start | bytes 8388608
  692.8 5.4 slice-start.5
  695.9 5.2 slice-start.3
  698.2 5.8 slice-start
  (10 other events, 27.2 us)

commit v4 on v3

--- a/solution.py
+++ b/solution.py
@@ -788,7 +788,14 @@
 
 def attention_back_kernel(folds, *refs):
     parts, upstream, attended, logsum, cosine, sine = refs[:6]
-    sides, refs = refs[6 : 6 + 2 * len(folds)], refs[6 + 2 * len(folds) :]
+    pair_grad, down_grad, output_grad = refs[6:9]
+    refs = refs[9:]
+    split, hidden = folds[0].lanes, folds[1].rows
+    inner = folds[3].rows
+    sides = [pair_grad.at[:, pl.ds(0, split)], pair_grad.at[:, pl.ds(2 * split, split)]]
+    sides += [down_grad.at[pl.ds(0, hidden)], down_grad.at[pl.ds(hidden, hidden)]]
+    sides += [pair_grad.at[:, pl.ds(split, split)], pair_grad.at[:, pl.ds(3 * split, split)]]
+    sides += [output_grad.at[pl.ds(0, inner)], output_grad.at[pl.ds(inner, inner)]]
     out, sums, refs = refs[0], refs[1 : 1 + len(folds)], refs[1 + len(folds) :]
     qr, kr, vr, kt, dk, dv, dqt = refs[:7]
     refs = refs[7:]
@@ -907,10 +914,10 @@
         fold.drain()
 
 
-def attention_backward(parts, upstream, attended, logsum, cosine, sine, sides):
+def attention_backward(parts, upstream, attended, logsum, cosine, sine, grads, shapes):
     tokens = SEGS * SEG
     vmem = pl.BlockSpec(memory_space=pltpu.VMEM)
-    folds = [PairFold(own.shape, i < 2) for i, own in enumerate(sides[::2])]
+    folds = [PairFold(shape, i < 2) for i, shape in enumerate(shapes)]
     scratch = []
     for fold in folds:
         scratch += fold.scratch()
@@ -918,7 +925,7 @@
         functools.partial(attention_back_kernel, folds),
         out_shape=(jax.ShapeDtypeStruct((tokens, 3 * WIDE), BF16),)
         + tuple(jax.ShapeDtypeStruct((fold.rows // 4, fold.lanes), BF16) for fold in folds),
-        in_specs=[vmem] * 6 + [pl.BlockSpec(memory_space=pl.ANY)] * len(sides),
+        in_specs=[vmem] * 6 + [pl.BlockSpec(memory_space=pl.ANY)] * len(grads),
         out_specs=(vmem,) * (1 + len(folds)),
         scratch_shapes=[pltpu.VMEM((tokens, WIDE), BF16)] * 3
         + [pltpu.VMEM((WIDE, tokens), BF16)]
@@ -941,7 +948,7 @@
         logsum,
         cosine,
         sine,
-        *sides,
+        *grads,
     )
 
 
@@ -1301,54 +1308,56 @@
 
 
 class Reduction:
-    def __init__(self, shape, by_lane=False, folded=False, cuts=None):
+    def __init__(self, shape, by_lane=False, kind="all", cuts=None):
         self.rows, self.lanes = shape
         self.by_lane = by_lane
-        self.folded = folded
+        self.kind = kind
         self.cuts = cuts or [self.lanes]
 
-    def outputs(self):
+    def chunk_shape(self, dp):
+        rows, lanes = self.rows // 4, self.lanes
+        return (rows, lanes // dp) if self.by_lane else (rows // dp, lanes)
+
+    def outputs(self, dp):
+        if self.kind == "sum":
+            return [jax.ShapeDtypeStruct(self.chunk_shape(dp), BF16)]
         return [jax.ShapeDtypeStruct((self.rows, lanes), F32) for lanes in self.cuts]
 
     def scratch(self, dp):
         rows, lanes = self.rows, self.lanes
-        quarter = (rows // 4, lanes)
-        chunk = (rows // 4, lanes // dp) if self.by_lane else (rows // 4 // dp, lanes)
-        refs = [
-            pltpu.VMEM(quarter, BF16),
-            pltpu.VMEM((dp + 1,) + chunk, BF16),
-            pltpu.VMEM(quarter, BF16),
-            pltpu.VMEM((3,) + quarter, BF16),
-            [pltpu.VMEM((rows // 4, cut), F32) for cut in self.cuts],
-            pltpu.SemaphoreType.DMA((5,)),
-            pltpu.SemaphoreType.DMA((5,)),
-            pltpu.SemaphoreType.DMA((dp,)),
-            pltpu.SemaphoreType.DMA((dp + 1,)),
-            pltpu.SemaphoreType.DMA((2, dp)),
-            pltpu.SemaphoreType.DMA((dp,)),
-            pltpu.SemaphoreType.DMA((len(self.cuts),)),
-        ]
-        refs = refs[:4] + refs[4] + refs[5:]
-        if not self.folded:
-            refs += [pltpu.VMEM((rows // 2, lanes), BF16)] * 2 + [pltpu.VMEM(quarter, BF16)]
-        return refs
+        half, quarter = pltpu.VMEM((rows // 2, lanes), BF16), pltpu.VMEM((rows // 4, lanes), BF16)
+        dma = pltpu.SemaphoreType.DMA
+        refs = {}
+        if self.kind == "all":
+            refs.update(half=half, core_land=half, x_land=quarter)
+            refs.update(fold_send=dma((2,)), fold_recv=dma((2,)))
+        if self.kind != "gather":
+            refs.update(
+                quarter=quarter,
+                z_land=pltpu.VMEM((dp + 1,) + self.chunk_shape(dp), BF16),
+                sum_send=dma((dp,)),
+                sum_recv=dma((dp + 1,)),
+            )
+        if self.kind != "sum":
+            refs.update(
+                whole=quarter,
+                others=pltpu.VMEM((3, rows // 4, lanes), BF16),
+                send=dma((3,)),
+                recv=dma((3,)),
+                all_send=dma((2, dp)),
+                all_recv=dma((dp,)),
+                out_sem=dma((len(self.cuts),)),
+            )
+            for i, cut in enumerate(self.cuts):
+                refs[f"wide{i}"] = pltpu.VMEM((rows // 4, cut), F32)
+        self.names = list(refs)
+        return list(refs.values())
 
     def bind(self, part, outs, refs):
         self.part, self.outs = part, outs
-        count = len(self.cuts)
-        self.quarter, self.z_land, self.whole, self.others = refs[:4]
-        self.wide = refs[4 : 4 + count]
-        (
-            self.send,
-            self.recv,
-            self.sum_send,
-            self.sum_recv,
-            self.all_send,
-            self.all_recv,
-            self.out_sem,
-        ) = refs[4 + count : 11 + count]
-        if not self.folded:
-            self.half, self.core_land, self.x_land = refs[11 + count :]
+        for name, ref in zip(self.names, refs):
+            setattr(self, name, ref)
+        self.wide = [getattr(self, f"wide{i}", None) for i in range(len(self.cuts))]
         self.x, self.core, self.z = (lax.axis_index(name) for name in ("x", "core", "dp"))
         self.dp = lax.axis_size("dp")
         self.to_core = {"core": 1 - self.core}
@@ -1379,8 +1388,8 @@
         return self.copy(
             self.part_of(self.part, 1 - self.core, half),
             self.core_land,
-            self.send.at[0],
-            self.recv.at[0],
+            self.fold_send.at[0],
+            self.fold_recv.at[0],
             self.to_core,
         )
 
@@ -1389,8 +1398,8 @@
         return self.copy(
             self.part_of(self.half, 1 - self.x, quarter),
             self.x_land,
-            self.send.at[1],
-            self.recv.at[1],
+            self.fold_send.at[1],
+            self.fold_recv.at[1],
             self.to_x,
         )
 
@@ -1420,8 +1429,8 @@
         return self.copy(
             src,
             self.others.at[which],
-            self.send.at[2 + which],
-            self.recv.at[2 + which],
+            self.send.at[which],
+            self.recv.at[which],
             self.to_x if which == 0 else self.to_core,
         )
 
@@ -1533,7 +1542,18 @@
                 self.wait_sum(self.dp)
                 self.add(mine, mine, self.z_land.at[self.dp])
 
-            self.chunk(self.whole, z)[...] = mine[...]
+            if self.kind == "sum":
+                self.outs[0][...] = mine[...]
+            else:
+                self.chunk(self.whole, z)[...] = mine[...]
+                gather()
+
+        def place():
+            self.chunk(self.whole, self.z)[...] = self.part[...]
+            gather()
+
+        def gather():
+            z, last = self.z, self.dp - 1
 
             @pl.when(z < last)
             def _():
@@ -1560,28 +1580,34 @@
             self.spread(2).wait_recv()
             self.emit(3, self.others.at[2])
 
-        return (
-            ([begin] if self.folded else [start, fold_core, fold_x])
-            + [functools.partial(self.hop, h) for h in range(1, self.dp - 1)]
-            + [settle]
-            + [functools.partial(self.all_hop, h) for h in range(1, self.dp - 1)]
-            + [share, pass_on, last]
-        )
+        sums = [functools.partial(self.hop, h) for h in range(1, self.dp - 1)] + [settle]
+        gathers = [functools.partial(self.all_hop, h) for h in range(1, self.dp - 1)]
+        gathers += [share, pass_on, last]
+        return {
+            "all": [start, fold_core, fold_x] + sums + gathers,
+            "sum": [begin] + sums,
+            "gather": [place] + gathers,
+        }[self.kind]
 
     def drain(self):
         z, last = self.z, self.dp - 1
-        if not self.folded:
+        if self.kind == "all":
             self.core_sum().wait_send()
             self.x_sum().wait_send()
+        if self.kind != "gather":
+            for j in range(self.dp):
+
+                @pl.when(z < j)
+                def _():
+                    self.z_sum(j, 1).wait_send()
+
+                @pl.when(z > j)
+                def _():
+                    self.z_sum(j, -1).wait_send()
+
+        if self.kind == "sum":
+            return
         for j in range(self.dp):
-
-            @pl.when(z < j)
-            def _():
-                self.z_sum(j, 1).wait_send()
-
-            @pl.when(z > j)
-            def _():
-                self.z_sum(j, -1).wait_send()
 
             @pl.when((z >= j) & (z < last))
             def _():
@@ -1739,9 +1765,8 @@
         return 0
 
     lax.fori_loop(0, steps, home_step, 0)
-    for wave in waves([plan[3:] for plan in plans]):
-        for call in wave:
-            call()
+    for call in stages[3]:
+        call()
     for item in items:
         item.drain()
 
@@ -1756,15 +1781,16 @@
     lax.fori_loop(0, steps, finish, 0)
 
 
-def leave(sent, adapted, middle_back, gain, query_w, key_w, value_w, parts, kinds):
+def leave(sent, adapted, middle_back, gain, query_w, key_w, value_w, parts, by_lanes):
     items = [
-        Reduction((4 * part.shape[0], part.shape[1]), by_lane, True, cuts)
-        for part, (by_lane, cuts) in zip(parts, kinds)
+        Reduction((4 * part.shape[0], part.shape[1]), by_lane, "sum")
+        for part, by_lane in zip(parts, by_lanes)
     ]
+    dp = lax.axis_size("dp")
     scratch, outs = [], []
     for item in items:
-        scratch += item.scratch(lax.axis_size("dp"))
-        outs += item.outputs()
+        scratch += item.scratch(dp)
+        outs += item.outputs(dp)
     peers, rows, lanes = sent.shape
     half, width = adapted.shape
     inner = query_w.shape[1]
@@ -1779,7 +1805,7 @@
         )
         + tuple(outs),
         in_specs=[vmem] * (7 + len(items)),
-        out_specs=(vmem,) * 3 + (pl.BlockSpec(memory_space=pl.ANY),) * len(outs),
+        out_specs=(vmem,) * (3 + len(outs)),
         scratch_shapes=[
             pltpu.VMEM((peers, rows, lanes), BF16),
             pltpu.VMEM((half, width), BF16),
@@ -1807,25 +1833,29 @@
     for target in (items[0].to_core, items[0].to_x):
         pl.semaphore_signal(barrier, inc=1, device_id=target, device_id_type=MESH)
     pl.semaphore_wait(barrier, 2 + greet_line(barrier))
-    plans = [item.stages() for item in items]
+    plans = [item.stages() for item in items if item.kind == "all"]
+    gathers = [item.stages() for item in items if item.kind == "gather"]
     for plan in plans:
+        plan[0]()
+    for plan in gathers:
         plan[0]()
     for plan in plans:
         plan[1]()
-    for wave in waves([plan[2:] for plan in plans]):
+    for wave in waves([plan[2:] for plan in plans] + [plan[1:] for plan in gathers]):
         for call in wave:
             call()
     for item in items:
         item.drain()
 
 
-def reduce_all(parts, cuts):
+def reduce_all(parts, chunks, shapes, by_lanes):
     dp = lax.axis_size("dp")
-    items = [Reduction(part.shape, cuts=cut) for part, cut in zip(parts, cuts)]
+    items = [Reduction(part.shape) for part in parts]
+    items += [Reduction(shape, by_lane, "gather") for shape, by_lane in zip(shapes, by_lanes)]
     scratch, outs = [], []
     for item in items:
         scratch += item.scratch(dp)
-        outs += item.outputs()
+        outs += item.outputs(dp)
     moved = sum(item.rows * item.lanes for item in items)
     return pl.pallas_call(
         functools.partial(reduce_kernel, items),
@@ -1840,7 +1870,44 @@
             flops=moved * 4, bytes_accessed=moved * 30, transcendentals=0
         ),
         name="reduce_all",
-    )(*parts)
+    )(*parts, *chunks)
+
+
+def latent_kernel(low, weight, out):
+    rows, inputs, lanes = low.shape[0], weight.shape[0], weight.shape[1]
+    blocks = lanes // 128
+    for at in range(inputs):
+        values = nt(low[...], weight[at])
+        for block in range(blocks):
+            out[pl.ds(block * inputs + at, rows, stride=blocks * inputs), :] = values[
+                :, block * 128 : (block + 1) * 128
+            ]
+
+
+def latent_grad(low, adapter):
+    tokens, width = low.shape
+    inputs, lanes, _ = adapter.shape
+    blocks = lanes // 128
+    step = SEG
+    flat = pl.pallas_call(
+        latent_kernel,
+        grid=(tokens // step,),
+        out_shape=jax.ShapeDtypeStruct((tokens * blocks * inputs, 128), F32),
+        in_specs=[
+            pl.BlockSpec((step, width), lambda i: (i, 0)),
+            pl.BlockSpec(adapter.shape, lambda i: (0, 0, 0)),
+        ],
+        out_specs=pl.BlockSpec((step * blocks * inputs, 128), lambda i: (i, 0)),
+        compiler_params=pltpu.CompilerParams(vmem_limit_bytes=VMEM_BYTES),
+        cost_estimate=pl.CostEstimate(
+            flops=2 * tokens * width * lanes * inputs,
+            bytes_accessed=tokens * (2 * width + 4 * lanes * inputs) + 2 * width * lanes * inputs,
+            transcendentals=0,
+        ),
+        name="latent_grad",
+    )(low, adapter)
+    flat = flat.reshape(tokens, blocks, inputs, 128)
+    return flat.transpose(0, 2, 1, 3).reshape(tokens, inputs, lanes)
 
 
 def swap(value, axis):
@@ -1958,29 +2025,24 @@
         axis=0,
     ).astype(F32)
 
-    split = gate_weight.shape[1]
     inner = output_weight.shape[0]
-    sides = []
-    lanes = [pair_low[:, i * split : (i + 1) * split] for i in range(4)]
-    sides += [tn(third_low, lanes[0]), tn(third_low, lanes[2])]
-    sides += [tn(hidden[:, :split], mixed_low), tn(hidden[:, split:], mixed_low)]
-    sides += [tn(third_low, lanes[1]), tn(third_low, lanes[3])]
-    sides += [
-        tn(attended_all[:, :inner], attention_low),
-        tn(attended_all[:, inner:], attention_low),
-    ]
+    grads = (
+        tn(third_low, pair_low),
+        tn(hidden, mixed_low),
+        tn(attended_all, attention_low),
+    )
+    shapes = [gate_weight.shape, down_weight.shape, up_weight.shape, output_weight.shape]
+
     table_cosine, table_sine = angle_tables(jnp.arange((TRUNK + 2) * SEG))
+    by_lanes = [False, True, False, False]
     sent, *sums = attention_backward(
-        parts, pick(role, upstream), attended, logsum, table_cosine, table_sine, sides
+        parts, pick(role, upstream), attended, logsum, table_cosine, table_sine, grads, shapes
     )
     (
         joined,
         adapted_low,
         first_gain_part,
-        gate_total,
-        down_total,
-        up_total,
-        output_total,
+        *chunks,
     ) = leave(
         pick(place, sent).reshape(4, rows, 3 * WIDE),
         adapted,
@@ -1990,23 +2052,34 @@
         key_weight,
         value_weight,
         sums,
-        [(False, None), (True, None), (False, None), (False, None)],
+        by_lanes,
     )
     adapter_part = jnp.einsum(
         "rcd,re->cde", latent_embed, adapted_low, preferred_element_type=F32
     ).astype(BF16)
-    query_total, key_total, value_total, *adapter_total = reduce_all(
+    (
+        query_total,
+        key_total,
+        value_total,
+        adapter_first,
+        adapter_second,
+        gate_total,
+        down_total,
+        up_total,
+        output_total,
+    ) = reduce_all(
         [tn(first_low, joined[:, i * inner : (i + 1) * inner]) for i in range(3)]
         + [adapter_part[0], adapter_part[1]],
-        [None] * 5,
-    )
-    adapter_total = jnp.stack(adapter_total)
-    latent_gradient = jnp.einsum("re,cde->rcd", adapted_low, adapter, preferred_element_type=F32)
+        chunks,
+        shapes,
+        by_lanes,
+    )
+    latent_gradient = latent_grad(adapted_low, adapter)
     gains = sum_small(jnp.concatenate([gain_parts[:3], first_gain_part[:1]], axis=0))
     return (
         layer_out,
         latent_gradient,
-        adapter_total,
+        jnp.stack([adapter_first, adapter_second]),
         gains[3],
         query_total,
         key_total,

time: 714 us -> 673 us (0.943)
  matrix products: 60.5 us -> 44.1 us
  Pallas kernels: 563 us -> 551 us
  local copies, waits for them, and re-layouts: 33.9 us -> 22.5 us
    pallas_call x1, Pallas kernels: 151 us -> 75.6 us  [leave(): pl.pallas_call(functools.partial(leave_kernel, items), out_shape=(jax.Sha...]
    pallas_call x1, Pallas kernels: 78.5 us -> 134 us  [reduce_all(): pl.pallas_call(functools.partial(reduce_kernel, items), out_shape=tuple(o...]
    dot_general x11 -> x6, matrix products: 44.4 us -> 31.8 us  [tn(): lax.dot_general(left, right, (((0,), (0,)), ((), ())), preferred_element_...]
    unnamed x60 -> x47, local copies, waits for them, and re-layouts: 31 us -> 19.6 us
    pallas_call x0 -> x1, Pallas kernels: none -> 7.94 us  [latent_grad(): pl.pallas_call(latent_kernel, grid=(tokens // step,), out_shape=jax.Shape...]
  transfers between devices with their start and end apart: 8 -> 8, of which waited for: 2 -> 2; matrix products, arithmetic and copies ran while one was open for 9% -> 8% of each run, Pallas kernels for 48% -> 49%
where the time goes in v4:
time: 673 us; the launch traced here: 666 us
  Pallas kernels  551 us (82%)
  matrix products  44.1 us (7%)
  other arithmetic  24.7 us (4%)
  local copies, waits for them, and re-layouts  22.5 us (3%)
  starting transfers between devices  13.5 us (2%)
  waiting for transfers between devices  8.96 us (1%)
    pallas_call x1, Pallas kernels, reduce_all(): pl.pallas_call(functools.partial(reduce_kernel, items), out_shape=tuple(o...  134 us
    pallas_call x1, Pallas kernels, attention_backward(): pl.pallas_call(functools.partial(attention_back_kernel, folds), out_shape...  105 us
    pallas_call x1, Pallas kernels, enter(): pl.pallas_call(enter_kernel, out_shape=(jax.ShapeDtypeStruct((peers, rows...  78.1 us
    pallas_call x1, Pallas kernels, leave(): pl.pallas_call(functools.partial(leave_kernel, items), out_shape=(jax.Sha...  75.6 us
    pallas_call x1, Pallas kernels, attention_forward(): pl.pallas_call(functools.partial(attention_kernel, fetches), out_shape=(j...  74.7 us
    pallas_call x1, Pallas kernels, middle_section(): pl.pallas_call(middle_kernel, grid_spec=pltpu.PrefetchScalarGridSpec(num_...  61.7 us
    dot_general x6, matrix products, tn(): lax.dot_general(left, right, (((0,), (0,)), ((), ())), preferred_element_...  31.8 us
    unnamed x47, local copies, waits for them, and re-layouts  19.6 us
  transfers between devices with their start and end apart: 8, of which 2 were waited for; matrix products, arithmetic and copies ran while one was open for 8% of the time, Pallas kernels for 49%

profile of v4, /device:TPU:0, one launch (start us, length us, event | category | flops | bytes accessed | tf_op | source)
XLA Modules:
  0.0 665.9 jit_solution(420581691614618789)
XLA Ops:
  1.4 6.8 %bitcast_convert_fusion.mine = bf16[1280,1024]{1,0:T(8,128)(2,1)} fusion(bf16[2,512,1024]{2,1,0:T(8,128)(2,1)} %weight.1, bf16[1280,2,512]{2,1,0:T(2,128)(2,1)} %param.16), kind=kOutput, calls=%fused_computation.2 | convolution fusion | flops 2685665280 | bytes 7340032 | tf_op jit(solution)/shard_map/rcd,cde->re/dot_general | solution.py:1984
  8.1 3.7 fusion.12
  11.8 78.1 %enter.1 = (bf16[4,1280,384]{2,1,0:T(8,128)(2,1)}, bf16[1280,1024]{1,0:T(8,128)(2,1)}, bf16[1280,1024]{1,0:T(8,128)(2,1)}) custom-call(bf16[1280,1024]{1,0:T(8,128)(2,1)} %bitcast_convert_fusion.mine, f32[1,1024]{1,0:T(1,128)} %bitcast.64, bf16[1024,512]{1,0:T(8,128)(2,1)} %refs_4_.3, bf16[1024,512]{1,0:T(8,128)(2,1)} %refs_5_.1, bf16[1024,512]{1,0:T(8,128)(2,1)} %refs_6_.1, ...), custom_call_target="tpu_custom_call" | custom-call | flops 4026531840 | bytes 209715200 | tf_op jit(solution)/shard_map/enter/pallas_call | solution.py:1063
  90.0 4.5 sort_parts.1
  94.5 74.7 %attention_forward.1 = (bf16[5120,128]{1,0:T(8,128)(2,1)}, f32[5120,128]{1,0:T(8,128)}, bf16[512,1024]{1,0:T(8,128)(2,1)}, bf16[1024,1408]{1,0:T(8,128)(2,1)}, b...) custom-call(bf16[5120,384]{1,0:T(8,128)(2,1)} %get-tuple-element.60.refs_0_, bf16[512,1024]{1,0:T(8,128)(2,1)} %wo_own.1, ...), custom_call_target="tpu_custom_call" | custom-call | flops 10200547328 | bytes 7864320 | tf_op jit(solution)/shard_map/attention_forward/pallas_call | solution.py:592
  171.7 3.8 all-to-all-start
  176.1 3.7 convert_add_fusion.adapted.refs_1_
  179.8 6.3 fusion.8
  186.0 6.7 %all-to-all-done.heads = bf16[8,640,128]{2,1,0:T(8,128)(2,1)S(1)} async-done(((bf16[8,640,128]{2,1,0:T(8,128)(2,1)}), bf16[8,640,128]{2,1,0:T(8,128)(2,1)S(1)}, u32[]{:S(2)}, u32[]{:S(2)}) %all-to-all-start) | async-done | bytes 1310752 | tf_op jit(solution)/shard_map/all_to_all | solution.py:1996
  193.8 61.7 %middle_section.1 = (bf16[640,1024]{1,0:T(8,128)(2,1)}, f32[640,1024]{1,0:T(8,128)}, bf16[640,1024]{1,0:T(8,128)(2,1)}, bf16[640,1024]{1,0:T(8,128)(2,1)}, bf16[...) custom-call(s32[2]{0:T(128)} %pad_add_fusion.meta, ...), custom_call_target="tpu_custom_call" | custom-call | flops 24830279680 | bytes 43319296 | tf_op jit(solution)/shard_map/middle_section/pallas_call | solution.py:1251
  255.5 4.0 all-to-all-start.1
  261.5 14.5 %convolution_convert_fusion.refs_6_ = bf16[1024,5632]{1,0:T(8,128)(2,1)} fusion(bf16[640,1024]{1,0:T(8,128)(2,1)} %get-tuple-element.70, bf16[640,5632]{1,0:T(8,128)(2,1)} %get-tuple-element.71), kind=kOutput, calls=%fused_computation | convolution fusion | flops 7387742208 | bytes 20054016 | tf_op jit(solution)/shard_map/dot_general | solution.py:1950
  276.0 3.2 convolution_convert_fusion.2.refs_8_
  279.2 6.5 convolution_convert_fusion.1.refs_7_
  289.3 105.2 %attention_backward.1 = (bf16[5120,384]{1,0:T(8,128)(2,1)}, bf16[256,1408]{1,0:T(8,128)(2,1)}, bf16[352,1024]{1,0:T(8,128)(2,1)}, bf16[256,1408]{1,0:T(8,128)(2,1)}, bf16[128,1024]{1,0:T(8,128)(2,1)}) custom-call(bf16[5120,384]{1,0:T(8,128)(2,1)} %get-tuple-element.60.refs_0_, bf16[5120,128]{1,0:T(8,128)(2,1)} %pick.4.refs_1_, ...), custom_call_target="tpu_custom_call" | custom-call | flops 25501368320 | bytes 15728640 | tf_op jit(solution)/shard_map/attention_backward/pallas_call | solution.py:924
  394.5 4.4 pick.5
  398.9 75.6 %leave.1 = (bf16[1280,1536]{1,0:T(8,128)(2,1)}, bf16[1280,1024]{1,0:T(8,128)(2,1)}, f32[8,1024]{1,0:T(8,128)}, bf16[64,1408]{1,0:T(8,128)(2,1)}, bf16[352,256]{1...) custom-call(bf16[4,1280,384]{2,1,0:T(8,128)(2,1)} %bitcast.53, ...), custom_call_target="tpu_custom_call" | custom-call | flops 4026531840 | bytes 209715200 | tf_op jit(solution)/shard_map/leave/pallas_call | solution.py:1799
  474.5 5.6 convert_bitcast_fusion
  496.0 7.9 %latent_grad.1 = f32[10240,128]{1,0:T(8,128)} custom-call(bf16[1280,1024]{1,0:T(8,128)(2,1)} %get-tuple-element.82.low, bf16[2,512,1024]{2,1,0:T(8,128)(2,1)} %weight.1), custom_call_target="tpu_custom_call" | custom-call | flops 2684354560 | bytes 9961472 | tf_op jit(solution)/shard_map/latent_grad/pallas_call | solution.py:1892
  503.9 133.9 %reduce_all.1 = (f32[1024,512]{1,0:T(8,128)}, f32[1024,512]{1,0:T(8,128)}, f32[1024,512]{1,0:T(8,128)}, f32[512,1024]{1,0:T(8,128)}, f32[512,1024]{1,0:T(8,128)}...) custom-call(bf16[1024,512]{1,0:T(8,128)(2,1)} %convolution_convert_fusion.5.refs_0_, ...), custom_call_target="tpu_custom_call" | custom-call | flops 29884416 | bytes 224133120 | tf_op jit(solution)/shard_map/reduce_all/pallas_call | solution.py:1860
  637.9 4.8 pad_maximum_fusion
  644.9 3.3 maximum_convert_fusion
  656.2 2.9 copy.52
  659.1 2.9 copy.53
  (81 shorter events, 40.0 us)
Async XLA Ops:
  171.7 21.1 %all-to-all-start = ((bf16[8,640,128]{2,1,0:T(8,128)(2,1)}), bf16[8,640,128]{2,1,0:T(8,128)(2,1)S(1)}, u32[]{:S(2)}, u32[]{:S(2)}) async-start(bf16[8,640,128]{2,1,0:T(8,128)(2,1)} %bitcast.51), calls=%async_computation | async-start | bytes 2621440 | tf_op jit(solution)/shard_map/all_to_all | solution.py:1996
  255.5 4.0 copy-start.7
  255.5 4.0 copy-start.6
  255.5 30.3 %all-to-all-start.1 = ((bf16[8,640,128]{2,1,0:T(8,128)(2,1)}), bf16[8,640,128]{2,1,0:T(8,128)(2,1)S(1)}, u32[]{:S(2)}, u32[]{:S(2)}) async-start(bf16[8,640,128]{2,1,0:T(8,128)(2,1)} %get-tuple-element.68), calls=%async_computation.1 | async-start | bytes 2621440 | tf_op jit(solution)/shard_map/all_to_all | solution.py:2018
  259.5 383.9 %collective-permute-start = (bf16[640,1024]{1,0:T(8,128)(2,1)S(1)}, bf16[640,1024]{1,0:T(8,128)(2,1)}, u32[]{:S(2)}, u32[]{:S(2)}) collective-permute-start(bf16[640,1024]{1,0:T(8,128)(2,1)S(1)} %copy-done.6), channel_id=1, source_target_pairs={{0,1},{1,0},{2,3},{3,2},{4,5},{5,4},{6,7},{7,6},{8,9},{9,8},{10,11... | collective-permute-start | bytes 3932168 | tf_op jit(solution)/shard_map/ppermute | solution.py:1914
  261.5 14.5 %copy-start.10 = (bf16[640,1024]{1,0:T(8,128)(2,1)S(1)}, bf16[640,1024]{1,0:T(8,128)(2,1)}, u32[]{:S(2)}) copy-start(bf16[640,1024]{1,0:T(8,128)(2,1)} %get-tuple-element.74) | copy-start | bytes 3932164
  261.5 14.5 %copy-start.11 = (bf16[640,1024]{1,0:T(8,128)(2,1)S(1)}, bf16[640,1024]{1,0:T(8,128)(2,1)}, u32[]{:S(2)}) copy-start(bf16[640,1024]{1,0:T(8,128)(2,1)} %get-tuple-element.75) | copy-start | bytes 3932164
  276.0 3.2 copy-start.12
  474.5 9.3 %copy-start.8 = (bf16[1280,1536]{1,0:T(8,128)(2,1)S(1)}, bf16[1280,1536]{1,0:T(8,128)(2,1)}, u32[]{:S(2)}) copy-start(bf16[1280,1536]{1,0:T(8,128)(2,1)} %get-tuple-element.84) | copy-start | bytes 11796484
  474.5 9.3 %copy-start.9 = (bf16[1280,1024]{1,0:T(8,128)(2,1)S(1)}, bf16[1280,1024]{1,0:T(8,128)(2,1)}, u32[]{:S(2)}) copy-start(bf16[1280,1024]{1,0:T(8,128)(2,1)} %get-tuple-element.83) | copy-start | bytes 7864324
  480.9 7.9 %collective-permute-start.1 = (f32[4,1024]{1,0:T(4,128)S(1)}, f32[4,1024]{1,0:T(4,128)S(1)}, u32[]{:S(2)}, u32[]{:S(2)}) collective-permute-start(f32[4,1024]{1,0:T(4,128)S(1)} %pad_maximum_fusion.1), channel_id=1, source_target_pairs={{0,1},{1,0},{2,3},{3,2},{4,5},{5,4},{6,7},{7,6},{8,9},{9,8},{10,11... | collective-permute-start | bytes 49160 | tf_op jit(solution)/shard_map/ppermute | solution.py:1914
  488.9 2.6 collective-permute-start.2
  491.5 3.8 collective-permute-start.3
  495.3 142.5 %collective-permute-start.4 = (f32[4,1024]{1,0:T(4,128)S(1)}, f32[4,1024]{1,0:T(4,128)S(1)}, u32[]{:S(2)}, u32[]{:S(2)}) collective-permute-start(f32[4,1024]{1,0:T(4,128)S(1)} %add.56), channel_id=1, source_target_pairs={{0,8},{8,0},{16,24},{24,16},{1,9},{9,1},{17,25},{25,17},{2,10},{10... | collective-permute-start | bytes 49160 | tf_op jit(solution)/shard_map/ppermute | solution.py:1945
  637.8 4.9 collective-permute-start.5
  644.8 3.3 copy-start.4
  644.9 4.7 copy-start.3
  644.9 6.0 copy-start.2
  648.2 7.1 %slice-start.4 = ((s8[5767168]{0:T(1024)(128)(4,1)}), s8[4194304]{0:T(1024)(128)(4,1)S(1)}, s32[]{:S(2)}) async-start(s8[5767168]{0:T(1024)(128)(4,1)} %bitcast.48), calls=%async_computation.6 | async-start | bytes 8388608
  649.5 9.6 %slice-start.2 = ((s8[5767168]{0:T(1024)(128)(4,1)}), s8[4194304]{0:T(1024)(128)(4,1)S(1)}, s32[]{:S(2)}) async-start(s8[5767168]{0:T(1024)(128)(4,1)} %bitcast.46), calls=%async_computation.4 | async-start | bytes 8388608
  650.8 5.4 slice-start.5
  654.0 5.2 slice-start.3
  656.2 5.8 slice-start
  659.1 4.0 slice-start.1
  (4 other events, 8.4 us)

commit v5 on v4

--- a/solution.py
+++ b/solution.py
@@ -1308,7 +1308,8 @@
 
 
 class Reduction:
-    def __init__(self, shape, by_lane=False, kind="all", cuts=None):
+    def __init__(self, shape, by_lane=False, kind="all", cuts=None, base=0):
+        self.base = base
         self.rows, self.lanes = shape
         self.by_lane = by_lane
         self.kind = kind
@@ -1321,6 +1322,8 @@
     def outputs(self, dp):
         if self.kind == "sum":
             return [jax.ShapeDtypeStruct(self.chunk_shape(dp), BF16)]
+        if self.base > 0:
+            return []
         return [jax.ShapeDtypeStruct((self.rows, lanes), F32) for lanes in self.cuts]
 
     def scratch(self, dp):
@@ -1438,7 +1441,7 @@
         quarter = self.rows // 4
         core = self.core if at < 2 else 1 - self.core
         x = self.x if at % 2 == 0 else 1 - self.x
-        row = pl.multiple_of((2 * core + x) * quarter, quarter)
+        row = pl.multiple_of(self.base + (2 * core + x) * quarter, quarter)
         return [
             pltpu.make_async_copy(wide, out.at[pl.ds(row, quarter)], self.out_sem.at[i])
             for i, (wide, out) in enumerate(zip(self.wide, self.outs))
@@ -1627,14 +1630,16 @@
     dp = lax.axis_size("dp")
     for item, part in zip(items, parts):
         size = len(item.scratch(dp))
-        item.bind(part, outs[: len(item.cuts)], scratch[:size])
-        outs, scratch = outs[len(item.cuts) :], scratch[size:]
-
-
-def waves(plans):
-    length = max(len(plan) + i for i, plan in enumerate(plans))
+        if item.base == 0:
+            own, outs = outs[: len(item.cuts)], outs[len(item.cuts) :]
+        item.bind(part, own, scratch[:size])
+        scratch = scratch[size:]
+
+
+def waves(plans, offsets):
+    length = max(len(plan) + i for i, plan in zip(offsets, plans))
     return [
-        [plan[t - i] for i, plan in enumerate(plans) if 0 <= t - i < len(plan)]
+        [plan[t - i] for i, plan in zip(offsets, plans) if 0 <= t - i < len(plan)]
         for t in range(length)
     ]
 
@@ -1657,14 +1662,14 @@
 
 
 def leave_kernel(items, *refs):
-    sent, adapted, middle_back, gain, query_w, key_w, value_w = refs[:7]
-    parts, refs = refs[7 : 7 + len(items)], refs[7 + len(items) :]
-    joined, adapted_low, gain_out = refs[:3]
+    sent, adapted, middle_back, first_low, gain, query_w, key_w, value_w = refs[:8]
+    parts, refs = refs[8 : 8 + len(items)], refs[8 + len(items) :]
+    grads, adapted_low, gain_out = refs[:3], refs[3], refs[4]
     count = sum(len(item.cuts) for item in items)
-    outs, refs = refs[3 : 3 + count], refs[3 + count :]
-    landed, away, away_landed = refs[:3]
-    part_send, part_recv, away_send, away_recv, low_send, low_recv = refs[3:9]
-    bind_all(items, parts, outs, refs[9:])
+    outs, refs = refs[5 : 5 + count], refs[5 + count :]
+    landed, away, away_landed, joined, grad_sum = refs[:5]
+    part_send, part_recv, away_send, away_recv, low_send, low_recv = refs[5:11]
+    bind_all(items, parts, outs, refs[11:])
     plans = [item.stages() for item in items]
     stages = list(zip(*plans))
     away_plan = {0: stages[0]}
@@ -1726,6 +1731,7 @@
         lax.fori_loop(0, steps, begin, 0)
     landed[me] = sent[me]
     gain_out[...] = jnp.zeros_like(gain_out)
+    grad_sum[...] = jnp.zeros_like(grad_sum)
 
     def input_grad(side, i):
         for at in range(len(others)):
@@ -1734,15 +1740,23 @@
         for at in range(3):
             for group in range(landed.shape[0]):
                 to = at * inner + group * WIDE
-                joined[here, to : to + WIDE] = landed[group, here, at * WIDE : (at + 1) * WIDE]
-        total = nt(joined[here, 0:inner], query_w[...])
-        total += nt(joined[here, inner : 2 * inner], key_w[...])
-        total += nt(joined[here, 2 * inner : 3 * inner], value_w[...])
+                joined[:, to : to + WIDE] = landed[group, here, at * WIDE : (at + 1) * WIDE]
+        total = nt(joined[:, 0:inner], query_w[...])
+        total += nt(joined[:, inner : 2 * inner], key_w[...])
+        total += nt(joined[:, 2 * inner : 3 * inner], value_w[...])
         return total
+
+    def weight_grad(side, i):
+        here = block((tensor if side else 1 - tensor) * half, i)
+        low = first_low[here, :].T
+        for at in range(3):
+            lanes = slice(at * inner, (at + 1) * inner)
+            grad_sum[:, lanes] += nn(low, joined[:, lanes])
 
     def away_step(i, _):
         away[block(0, i), :] = input_grad(0, i).astype(BF16)
         hand_over(i).start()
+        weight_grad(0, i)
         at_step(i, away_plan)
         return 0
 
@@ -1761,10 +1775,13 @@
         gain_out[0:1, :] += jnp.sum(upstream * normed, axis=0, keepdims=True)
         adapted_low[block(tensor * half, i), :] = (middle_back[rows, :] + inward).astype(BF16)
         share(i).start()
+        weight_grad(1, i)
         at_step(i, home_plan)
         return 0
 
     lax.fori_loop(0, steps, home_step, 0)
+    for at in range(3):
+        grads[at][...] = grad_sum[:, at * inner : (at + 1) * inner].astype(BF16)
     for call in stages[3]:
         call()
     for item in items:
@@ -1781,7 +1798,9 @@
     lax.fori_loop(0, steps, finish, 0)
 
 
-def leave(sent, adapted, middle_back, gain, query_w, key_w, value_w, parts, by_lanes):
+def leave(
+    sent, adapted, middle_back, first_low, gain, query_w, key_w, value_w, parts, by_lanes
+):
     items = [
         Reduction((4 * part.shape[0], part.shape[1]), by_lane, "sum")
         for part, by_lane in zip(parts, by_lanes)
@@ -1798,18 +1817,20 @@
     vmem = pl.BlockSpec(memory_space=pltpu.VMEM)
     return pl.pallas_call(
         functools.partial(leave_kernel, items),
-        out_shape=(
-            jax.ShapeDtypeStruct((rows, 3 * inner), BF16),
+        out_shape=(jax.ShapeDtypeStruct((width, inner), BF16),) * 3
+        + (
             jax.ShapeDtypeStruct((rows, width), BF16),
             jax.ShapeDtypeStruct((8, width), F32),
         )
         + tuple(outs),
-        in_specs=[vmem] * (7 + len(items)),
-        out_specs=(vmem,) * (3 + len(outs)),
+        in_specs=[vmem] * (8 + len(items)),
+        out_specs=(vmem,) * (5 + len(outs)),
         scratch_shapes=[
             pltpu.VMEM((peers, rows, lanes), BF16),
             pltpu.VMEM((half, width), BF16),
             pltpu.VMEM((half, width), BF16),
+            pltpu.VMEM((LEAVE, 3 * inner), BF16),
+            pltpu.VMEM((width, 3 * inner), F32),
             pltpu.SemaphoreType.DMA((2, steps, 3)),
             pltpu.SemaphoreType.DMA((2, steps, 3)),
         ]
@@ -1819,20 +1840,145 @@
             vmem_limit_bytes=VMEM_BYTES, collective_id=1, has_side_effects=True
         ),
         cost_estimate=pl.CostEstimate(
-            flops=2 * rows * width * 3 * inner, bytes_accessed=200 << 20, transcendentals=rows
+            flops=4 * rows * width * 3 * inner, bytes_accessed=200 << 20, transcendentals=rows
         ),
         name="leave",
-    )(sent, adapted, middle_back, gain, query_w, key_w, value_w, *parts)
-
-
-def reduce_kernel(items, *refs):
+    )(sent, adapted, middle_back, first_low, gain, query_w, key_w, value_w, *parts)
+
+
+class SmallSum:
+    def __init__(self, shape):
+        self.shape = shape
+
+    def scratch(self, dp):
+        return [
+            pltpu.VMEM((3,) + self.shape, F32),
+            pltpu.VMEM((3,) + self.shape, F32),
+            pltpu.VMEM((dp,) + self.shape, F32),
+            pltpu.SemaphoreType.DMA((3,)),
+            pltpu.SemaphoreType.DMA((3,)),
+            pltpu.SemaphoreType.DMA((2, dp)),
+            pltpu.SemaphoreType.DMA((dp,)),
+        ]
+
+    def bind(self, part, out, refs):
+        self.part, self.out = part, out
+        (
+            self.mine,
+            self.theirs,
+            self.line,
+            self.send,
+            self.recv,
+            self.line_send,
+            self.line_recv,
+        ) = refs
+        self.z, self.dp = lax.axis_index("dp"), lax.axis_size("dp")
+        self.targets = [{name: 1 - lax.axis_index(name)} for name in ("tensor", "core", "x")]
+
+    def pair(self, at):
+        return pltpu.make_async_remote_copy(
+            src_ref=self.mine.at[at],
+            dst_ref=self.theirs.at[at],
+            send_sem=self.send.at[at],
+            recv_sem=self.recv.at[at],
+            device_id=self.targets[at],
+            device_id_type=MESH,
+        )
+
+    def pass_along(self, j, step):
+        return pltpu.make_async_remote_copy(
+            src_ref=self.line.at[j],
+            dst_ref=self.line.at[j],
+            send_sem=self.line_send.at[0 if step > 0 else 1, j],
+            recv_sem=self.line_recv.at[j],
+            device_id={"dp": self.z + step},
+            device_id_type=MESH,
+        )
+
+    def stages(self):
+        def begin():
+            self.mine[0] = self.part[...]
+            self.pair(0).start()
+
+        def fold(at):
+            self.pair(at - 1).wait_recv()
+            total = self.mine[at - 1] + self.theirs[at - 1]
+            if at < 3:
+                self.mine[at] = total
+                self.pair(at).start()
+            else:
+                self.line[self.z] = total
+                self.send_on(self.z, self.z)
+
+        def hop(h):
+            z, last = self.z, self.dp - 1
+            low, high = jnp.maximum(z - h, 0), jnp.minimum(z + h, last)
+
+            @pl.when(z >= h)
+            def _():
+                self.pass_along(low, 1).wait_recv()
+
+            @pl.when((z >= h) & (z < last))
+            def _():
+                self.pass_along(low, 1).start()
+
+            @pl.when(z <= last - h)
+            def _():
+                self.pass_along(high, -1).wait_recv()
+
+            @pl.when((z <= last - h) & (z > 0))
+            def _():
+                self.pass_along(high, -1).start()
+
+        def last():
+            total = self.line[0]
+            for j in range(1, self.dp):
+                total = total + self.line[j]
+            self.out[...] = total
+
+        call = functools.partial
+        return (
+            [begin]
+            + [call(fold, at) for at in (1, 2, 3)]
+            + [call(hop, h) for h in range(1, self.dp)]
+            + [last]
+        )
+
+    def send_on(self, up, down):
+        @pl.when(self.z < self.dp - 1)
+        def _():
+            self.pass_along(up, 1).start()
+
+        @pl.when(self.z > 0)
+        def _():
+            self.pass_along(down, -1).start()
+
+    def drain(self):
+        z, last = self.z, self.dp - 1
+        for at in range(3):
+            self.pair(at).wait_send()
+        for j in range(self.dp):
+
+            @pl.when((z >= j) & (z < last))
+            def _():
+                self.pass_along(j, 1).wait_send()
+
+            @pl.when((z <= j) & (z > 0))
+            def _():
+                self.pass_along(j, -1).wait_send()
+
+
+def reduce_kernel(items, small, *refs):
     count = len(items)
-    outs = sum(len(item.cuts) for item in items)
-    bind_all(items, refs[:count], refs[count : count + outs], refs[count + outs :])
+    outs = sum(len(item.cuts) for item in items if item.base == 0)
+    parts, refs = refs[: count + 1], refs[count + 1 :]
+    small_refs = len(small.scratch(lax.axis_size("dp")))
+    small.bind(parts[count], refs[outs], refs[outs + 1 : outs + 1 + small_refs])
+    bind_all(items, parts[:count], refs[:outs], refs[outs + 1 + small_refs :])
     barrier = pltpu.get_barrier_semaphore()
-    for target in (items[0].to_core, items[0].to_x):
+    for target in small.targets:
         pl.semaphore_signal(barrier, inc=1, device_id=target, device_id_type=MESH)
-    pl.semaphore_wait(barrier, 2 + greet_line(barrier))
+    pl.semaphore_wait(barrier, 3 + greet_line(barrier))
     plans = [item.stages() for item in items if item.kind == "all"]
     gathers = [item.stages() for item in items if item.kind == "gather"]
     for plan in plans:
@@ -1841,27 +1987,34 @@
         plan[0]()
     for plan in plans:
         plan[1]()
-    for wave in waves([plan[2:] for plan in plans] + [plan[1:] for plan in gathers]):
+    offsets = list(range(len(plans))) + [2 + i for i in range(len(gathers))]
+    rest = [plan[2:] for plan in plans] + [plan[1:] for plan in gathers] + [small.stages()]
+    for wave in waves(rest, offsets + [1]):
         for call in wave:
             call()
-    for item in items:
+    for item in items + [small]:
         item.drain()
 
 
-def reduce_all(parts, chunks, shapes, by_lanes):
+def reduce_all(parts, chunks, shapes, by_lanes, gains):
     dp = lax.axis_size("dp")
-    items = [Reduction(part.shape) for part in parts]
+    items = [Reduction(part.shape) for part in parts[:-1]]
+    items.append(Reduction(parts[-1].shape, base=parts[-2].shape[0]))
     items += [Reduction(shape, by_lane, "gather") for shape, by_lane in zip(shapes, by_lanes)]
-    scratch, outs = [], []
+    small = SmallSum(gains.shape)
+    scratch, outs = small.scratch(dp), []
     for item in items:
         scratch += item.scratch(dp)
         outs += item.outputs(dp)
+    both = len(parts) - 2
+    outs[both] = jax.ShapeDtypeStruct((2 * parts[-1].shape[0], parts[-1].shape[1]), F32)
     moved = sum(item.rows * item.lanes for item in items)
     return pl.pallas_call(
-        functools.partial(reduce_kernel, items),
-        out_shape=tuple(outs),
-        in_specs=[pl.BlockSpec(memory_space=pltpu.VMEM)] * len(items),
-        out_specs=(pl.BlockSpec(memory_space=pl.ANY),) * len(outs),
+        functools.partial(reduce_kernel, items, small),
+        out_shape=tuple(outs) + (jax.ShapeDtypeStruct(gains.shape, F32),),
+        in_specs=[pl.BlockSpec(memory_space=pltpu.VMEM)] * (len(items) + 1),
+        out_specs=(pl.BlockSpec(memory_space=pl.ANY),) * len(outs)
+        + (pl.BlockSpec(memory_space=pltpu.VMEM),),
         scratch_shapes=scratch,
         compiler_params=pltpu.CompilerParams(
             vmem_limit_bytes=VMEM_BYTES, collective_id=2, has_side_effects=True
@@ -1870,7 +2023,7 @@
             flops=moved * 4, bytes_accessed=moved * 30, transcendentals=0
         ),
         name="reduce_all",
-    )(*parts, *chunks)
+    )(*parts, *chunks, gains)
 
 
 def latent_kernel(low, weight, out):
@@ -1936,14 +2089,6 @@
     return jnp.concatenate(
         [jnp.where(index == 0, value, other), jnp.where(index == 0, other, value)], axis=0
     )
-
-
-def sum_small(value):
-    for axis in ("tensor", "core", "x"):
-        value = value + swap(value, axis)
-    for pairs in ([(0, 1), (1, 0), (2, 3), (3, 2)], [(0, 2), (2, 0), (1, 3), (3, 1)]):
-        value = value + lax.ppermute(value, "dp", pairs)
-    return value
 
 
 def tn(left, right):
@@ -2039,7 +2184,9 @@
         parts, pick(role, upstream), attended, logsum, table_cosine, table_sine, grads, shapes
     )
     (
-        joined,
+        query_part,
+        key_part,
+        value_part,
         adapted_low,
         first_gain_part,
         *chunks,
@@ -2047,6 +2194,7 @@
         pick(place, sent).reshape(4, rows, 3 * WIDE),
         adapted,
         middle_back,
+        first_low,
         one_row(first_gain),
         query_weight,
         key_weight,
@@ -2061,25 +2209,24 @@
         query_total,
         key_total,
         value_total,
-        adapter_first,
-        adapter_second,
+        adapter_total,
         gate_total,
         down_total,
         up_total,
         output_total,
+        gains,
     ) = reduce_all(
-        [tn(first_low, joined[:, i * inner : (i + 1) * inner]) for i in range(3)]
-        + [adapter_part[0], adapter_part[1]],
+        [query_part, key_part, value_part, adapter_part[0], adapter_part[1]],
         chunks,
         shapes,
         by_lanes,
+        jnp.concatenate([gain_parts[:3], first_gain_part[:5]], axis=0),
     )
     latent_gradient = latent_grad(adapted_low, adapter)
-    gains = sum_small(jnp.concatenate([gain_parts[:3], first_gain_part[:1]], axis=0))
     return (
         layer_out,
         latent_gradient,
-        jnp.stack([adapter_first, adapter_second]),
+        adapter_total.reshape(adapter.shape),
         gains[3],
         query_total,
         key_total,

time: 673 us -> 659 us (0.979)
  matrix products: 44.1 us -> 36.5 us
    dot_general x6 -> x3, matrix products: 31.8 us -> 24.3 us  [tn(): lax.dot_general(left, right, (((0,), (0,)), ((), ())), preferred_element_...]
    unnamed x47 -> x46, local copies, waits for them, and re-layouts: 19.6 us -> 22.9 us
  transfers between devices with their start and end apart: 8 -> 3, of which waited for: 2 -> 1; matrix products, arithmetic and copies ran while one was open for 8% -> 7% of each run, Pallas kernels for 49% -> 50%
where the time goes in v5:
time: 659 us; the launch traced here: 651 us
  Pallas kernels  550 us (83%)
  matrix products  36.5 us (6%)
  local copies, waits for them, and re-layouts  25.9 us (4%)
  other arithmetic  20.9 us (3%)
  starting transfers between devices  9.77 us (1%)
  waiting for transfers between devices  6.74 us (1%)
    pallas_call x1, Pallas kernels, reduce_all(): pl.pallas_call(functools.partial(reduce_kernel, items, small), out_shape=...  130 us
    pallas_call x1, Pallas kernels, attention_backward(): pl.pallas_call(functools.partial(attention_back_kernel, folds), out_shape...  105 us
    pallas_call x1, Pallas kernels, leave(): pl.pallas_call(functools.partial(leave_kernel, items), out_shape=(jax.Sha...  78.4 us
    pallas_call x1, Pallas kernels, enter(): pl.pallas_call(enter_kernel, out_shape=(jax.ShapeDtypeStruct((peers, rows...  78.2 us
    pallas_call x1, Pallas kernels, attention_forward(): pl.pallas_call(functools.partial(attention_kernel, fetches), out_shape=(j...  74.7 us
    pallas_call x1, Pallas kernels, middle_section(): pl.pallas_call(middle_kernel, grid_spec=pltpu.PrefetchScalarGridSpec(num_...  61.7 us
    dot_general x3, matrix products, tn(): lax.dot_general(left, right, (((0,), (0,)), ((), ())), preferred_element_...  24.3 us
    unnamed x46, local copies, waits for them, and re-layouts  22.9 us
  transfers between devices with their start and end apart: 3, of which 1 were waited for; matrix products, arithmetic and copies ran while one was open for 7% of the time, Pallas kernels for 50%

profile of v5, /device:TPU:0, one launch (start us, length us, event | category | flops | bytes accessed | tf_op | source)
XLA Modules:
  0.0 651.3 jit_solution(17899962308221785268)
XLA Ops:
  1.4 6.8 %bitcast_convert_fusion.mine = bf16[1280,1024]{1,0:T(8,128)(2,1)} fusion(bf16[2,512,1024]{2,1,0:T(8,128)(2,1)} %weight.1, bf16[1280,2,512]{2,1,0:T(2,128)(2,1)} %param.16), kind=kOutput, calls=%fused_computation.2 | convolution fusion | flops 2685665280 | bytes 7340032 | tf_op jit(solution)/shard_map/rcd,cde->re/dot_general | solution.py:2129
  8.1 3.7 fusion.9
  11.8 78.2 %enter.1 = (bf16[4,1280,384]{2,1,0:T(8,128)(2,1)}, bf16[1280,1024]{1,0:T(8,128)(2,1)}, bf16[1280,1024]{1,0:T(8,128)(2,1)}) custom-call(bf16[1280,1024]{1,0:T(8,128)(2,1)} %bitcast_convert_fusion.mine, f32[1,1024]{1,0:T(1,128)} %bitcast.61, bf16[1024,512]{1,0:T(8,128)(2,1)} %refs_5_.1, bf16[1024,512]{1,0:T(8,128)(2,1)} %refs_6_.1, bf16[1024,512]{1,0:T(8,128)(2,1)} %refs_7_.1, ...), custom_call_target="tpu_custom_call" | custom-call | flops 4026531840 | bytes 209715200 | tf_op jit(solution)/shard_map/enter/pallas_call | solution.py:1063
  90.0 4.5 sort_parts.1
  94.5 74.7 %attention_forward.1 = (bf16[5120,128]{1,0:T(8,128)(2,1)}, f32[5120,128]{1,0:T(8,128)}, bf16[512,1024]{1,0:T(8,128)(2,1)}, bf16[1024,1408]{1,0:T(8,128)(2,1)}, b...) custom-call(bf16[5120,384]{1,0:T(8,128)(2,1)} %get-tuple-element.62.refs_0_, bf16[512,1024]{1,0:T(8,128)(2,1)} %wo_own.1, ...), custom_call_target="tpu_custom_call" | custom-call | flops 10200547328 | bytes 7864320 | tf_op jit(solution)/shard_map/attention_forward/pallas_call | solution.py:592
  171.7 3.8 all-to-all-start
  176.1 3.7 convert_add_fusion.adapted.refs_1_
  179.8 6.2 fusion.8
  186.0 6.7 %all-to-all-done.heads = bf16[8,640,128]{2,1,0:T(8,128)(2,1)S(1)} async-done(((bf16[8,640,128]{2,1,0:T(8,128)(2,1)}), bf16[8,640,128]{2,1,0:T(8,128)(2,1)S(1)}, u32[]{:S(2)}, u32[]{:S(2)}) %all-to-all-start) | async-done | bytes 1310752 | tf_op jit(solution)/shard_map/all_to_all | solution.py:2141
  193.8 61.7 %middle_section.1 = (bf16[640,1024]{1,0:T(8,128)(2,1)}, f32[640,1024]{1,0:T(8,128)}, bf16[640,1024]{1,0:T(8,128)(2,1)}, bf16[640,1024]{1,0:T(8,128)(2,1)}, bf16[...) custom-call(s32[2]{0:T(128)} %pad_add_fusion.meta, ...), custom_call_target="tpu_custom_call" | custom-call | flops 24830279680 | bytes 43319296 | tf_op jit(solution)/shard_map/middle_section/pallas_call | solution.py:1251
  255.5 4.0 all-to-all-start.1
  261.6 14.6 %convolution_convert_fusion.refs_6_ = bf16[1024,5632]{1,0:T(8,128)(2,1)} fusion(bf16[640,1024]{1,0:T(8,128)(2,1)} %get-tuple-element.72, bf16[640,5632]{1,0:T(8,128)(2,1)} %get-tuple-element.73), kind=kOutput, calls=%fused_computation | convolution fusion | flops 7387742208 | bytes 20054016 | tf_op jit(solution)/shard_map/dot_general | solution.py:2095
  276.2 3.2 convolution_convert_fusion.2.refs_8_
  279.4 6.5 %convolution_convert_fusion.1.refs_7_ = bf16[2816,1024]{1,0:T(8,128)(2,1)} fusion(bf16[640,2816]{1,0:T(8,128)(2,1)S(1)} %copy-done.11, bf16[640,1024]{1,0:T(8,128)(2,1)S(1)} %copy-done.12), kind=kOutput, calls=%fused_computation.1 | convolution fusion | flops 3693871104 | bytes 10682368 | tf_op jit(solution)/shard_map/dot_general | solution.py:2095
  289.5 105.2 %attention_backward.1 = (bf16[5120,384]{1,0:T(8,128)(2,1)}, bf16[256,1408]{1,0:T(8,128)(2,1)}, bf16[352,1024]{1,0:T(8,128)(2,1)}, bf16[256,1408]{1,0:T(8,128)(2,1)}, bf16[128,1024]{1,0:T(8,128)(2,1)}) custom-call(bf16[5120,384]{1,0:T(8,128)(2,1)} %get-tuple-element.62.refs_0_, bf16[5120,128]{1,0:T(8,128)(2,1)} %pick.4.refs_1_, ...), custom_call_target="tpu_custom_call" | custom-call | flops 25501368320 | bytes 15728640 | tf_op jit(solution)/shard_map/attention_backward/pallas_call | solution.py:924
  394.6 4.4 pick.5
  399.0 78.4 %leave.1 = (bf16[1024,512]{1,0:T(8,128)(2,1)}, bf16[1024,512]{1,0:T(8,128)(2,1)}, bf16[1024,512]{1,0:T(8,128)(2,1)}, bf16[1280,1024]{1,0:T(8,128)(2,1)}, f32[8,1...) custom-call(bf16[4,1280,384]{2,1,0:T(8,128)(2,1)} %bitcast.51, ...), custom_call_target="tpu_custom_call" | custom-call | flops 8053063680 | bytes 209715200 | tf_op jit(solution)/shard_map/leave/pallas_call | solution.py:1818
  478.9 5.5 convert_bitcast_fusion
  485.8 130.5 %reduce_all.1 = (f32[1024,512]{1,0:T(8,128)}, f32[1024,512]{1,0:T(8,128)}, f32[1024,512]{1,0:T(8,128)}, f32[1024,1024]{1,0:T(8,128)}, f32[1024,1408]{1,0:T(8,128...) custom-call(bf16[1024,512]{1,0:T(8,128)(2,1)} %get-tuple-element.86.refs_0_, ...), custom_call_target="tpu_custom_call" | custom-call | flops 29884416 | bytes 224133120 | tf_op jit(solution)/shard_map/reduce_all/pallas_call | solution.py:2012
  617.8 7.9 %latent_grad.1 = f32[10240,128]{1,0:T(8,128)} custom-call(bf16[1280,1024]{1,0:T(8,128)(2,1)} %get-tuple-element.85.low, bf16[2,512,1024]{2,1,0:T(8,128)(2,1)} %weight.1), custom_call_target="tpu_custom_call" | custom-call | flops 2684354560 | bytes 9961472 | tf_op jit(solution)/shard_map/latent_grad/pallas_call | solution.py:2045
  627.3 3.1 maximum_convert_fusion
  641.7 2.9 copy.54
  644.6 2.9 copy.55
  648.6 2.5 copy.56
  (60 shorter events, 28.7 us)
Async XLA Ops:
  171.7 21.1 %all-to-all-start = ((bf16[8,640,128]{2,1,0:T(8,128)(2,1)}), bf16[8,640,128]{2,1,0:T(8,128)(2,1)S(1)}, u32[]{:S(2)}, u32[]{:S(2)}) async-start(bf16[8,640,128]{2,1,0:T(8,128)(2,1)} %bitcast.48), calls=%async_computation | async-start | bytes 2621440 | tf_op jit(solution)/shard_map/all_to_all | solution.py:2141
  192.8 1.1 copy-start.6
  255.5 4.0 copy-start.8
  255.5 4.0 copy-start.7
  255.5 30.4 %all-to-all-start.1 = ((bf16[8,640,128]{2,1,0:T(8,128)(2,1)}), bf16[8,640,128]{2,1,0:T(8,128)(2,1)S(1)}, u32[]{:S(2)}, u32[]{:S(2)}) async-start(bf16[8,640,128]{2,1,0:T(8,128)(2,1)} %get-tuple-element.70), calls=%async_computation.1 | async-start | bytes 2621440 | tf_op jit(solution)/shard_map/all_to_all | solution.py:2163
  259.5 366.2 %collective-permute-start = (bf16[640,1024]{1,0:T(8,128)(2,1)S(1)}, bf16[640,1024]{1,0:T(8,128)(2,1)}, u32[]{:S(2)}, u32[]{:S(2)}) collective-permute-start(bf16[640,1024]{1,0:T(8,128)(2,1)S(1)} %copy-done.7), channel_id=1, source_target_pairs={{0,1},{1,0},{2,3},{3,2},{4,5},{5,4},{6,7},{7,6},{8,9},{9,8},{10,11... | collective-permute-start | bytes 3932168 | tf_op jit(solution)/shard_map/ppermute | solution.py:2067
  261.6 14.6 %copy-start.9 = (bf16[640,1024]{1,0:T(8,128)(2,1)S(1)}, bf16[640,1024]{1,0:T(8,128)(2,1)}, u32[]{:S(2)}) copy-start(bf16[640,1024]{1,0:T(8,128)(2,1)} %get-tuple-element.76) | copy-start | bytes 3932164
  261.6 14.6 %copy-start.10 = (bf16[640,1024]{1,0:T(8,128)(2,1)S(1)}, bf16[640,1024]{1,0:T(8,128)(2,1)}, u32[]{:S(2)}) copy-start(bf16[640,1024]{1,0:T(8,128)(2,1)} %get-tuple-element.77) | copy-start | bytes 3932164
  276.2 3.2 copy-start.11
  276.2 3.2 copy-start.12
  285.9 1.1 copy-start
  627.3 3.7 copy-start.1
  630.9 3.1 copy-start.5
  630.9 4.4 copy-start.4
  630.9 5.7 copy-start.3
  634.0 7.1 %slice-start.4 = ((s8[5767168]{0:T(1024)(128)(4,1)}), s8[4194304]{0:T(1024)(128)(4,1)S(1)}, s32[]{:S(2)}) async-start(s8[5767168]{0:T(1024)(128)(4,1)} %bitcast.45), calls=%async_computation.6 | async-start | bytes 8388608
  635.3 9.3 %slice-start.2 = ((s8[5767168]{0:T(1024)(128)(4,1)}), s8[4194304]{0:T(1024)(128)(4,1)S(1)}, s32[]{:S(2)}) async-start(s8[5767168]{0:T(1024)(128)(4,1)} %bitcast.43), calls=%async_computation.4 | async-start | bytes 8388608
  636.7 3.1 copy-start.2
  636.7 5.0 slice-start.5
  639.8 4.8 slice-start.3
  641.7 5.8 slice-start
  644.6 4.0 slice-start.1

commit v6 on v5

--- a/solution.py
+++ b/solution.py
@@ -790,11 +790,11 @@
     parts, upstream, attended, logsum, cosine, sine = refs[:6]
     pair_grad, down_grad, output_grad = refs[6:9]
     refs = refs[9:]
-    split, hidden = folds[0].lanes, folds[1].rows
+    split, hidden = folds[0].lanes, folds[2].rows
     inner = folds[3].rows
     sides = [pair_grad.at[:, pl.ds(0, split)], pair_grad.at[:, pl.ds(2 * split, split)]]
+    sides += [pair_grad.at[:, pl.ds(split, split)], pair_grad.at[:, pl.ds(3 * split, split)]]
     sides += [down_grad.at[pl.ds(0, hidden)], down_grad.at[pl.ds(hidden, hidden)]]
-    sides += [pair_grad.at[:, pl.ds(split, split)], pair_grad.at[:, pl.ds(3 * split, split)]]
     sides += [output_grad.at[pl.ds(0, inner)], output_grad.at[pl.ds(inner, inner)]]
     out, sums, refs = refs[0], refs[1 : 1 + len(folds)], refs[1 + len(folds) :]
     qr, kr, vr, kt, dk, dv, dqt = refs[:7]
@@ -803,7 +803,7 @@
         size = len(fold.scratch())
         fold.bind(sides[2 * i : 2 * i + 2], sums[i], refs[:size])
         refs = refs[size:]
-    gate, down, up, output = folds
+    gate, up, down, output = folds
     barrier = pltpu.get_barrier_semaphore()
     for target in (gate.to_core, gate.to_x, gate.to_tensor):
         pl.semaphore_signal(barrier, inc=1, device_id=target, device_id_type=MESH)
@@ -812,11 +812,16 @@
         fold.start()
     call = functools.partial
     leaf_plan = {
-        2: [gate.fold_core, up.fold_core],
-        3: [down.fold_core, output.fold_core],
+        1: [gate.fold_core],
+        2: [down.fold_core],
+        3: [up.fold_core, output.fold_core],
+        7: [call(down.second, 0)],
     }
-    branch_plan = {3: [call(gate.second, 0), call(up.second, 0), call(output.second, 0)]}
-    trunk_plan = {5: [call(up.second, 1), call(output.second, 1)]}
+    branch_plan = {
+        2: [call(gate.second, 0), call(down.second, 1)],
+        3: [call(output.second, 0)],
+    }
+    trunk_plan = {5: [call(output.second, 1), call(up.second, 0)]}
     lane = lax.broadcasted_iota(jnp.int32, (SEG, WIDE), 1)
     first = lane < DH
     low = (lane % DH) < (DH // 2)
@@ -898,7 +903,7 @@
     lax.fori_loop(0, BRANCH, branch, 0)
     lax.fori_loop(0, TRUNK, trunk, 0)
 
-    down.second(0)
+    up.second(1)
 
     def settle(i, _):
         here = segment(i)
@@ -908,8 +913,10 @@
         return 0
 
     lax.fori_loop(0, SEGS, settle, 0)
-    for fold in (gate, up, output, down):
+    for fold in (gate, output, down):
         fold.third(0)
+    for piece in range(up.pieces):
+        up.third(piece)
     for fold in folds:
         fold.drain()
 
@@ -917,7 +924,7 @@
 def attention_backward(parts, upstream, attended, logsum, cosine, sine, grads, shapes):
     tokens = SEGS * SEG
     vmem = pl.BlockSpec(memory_space=pltpu.VMEM)
-    folds = [PairFold(shape, i < 2) for i, shape in enumerate(shapes)]
+    folds = [PairFold(shape, i < 2, 1 + i % 2) for i, shape in enumerate(shapes)]
     scratch = []
     for fold in folds:
         scratch += fold.scratch()
@@ -1308,7 +1315,8 @@
 
 
 class Reduction:
-    def __init__(self, shape, by_lane=False, kind="all", cuts=None, base=0):
+    def __init__(self, shape, by_lane=False, kind="all", cuts=None, base=0, x_early=False):
+        self.x_early = x_early
         self.base = base
         self.rows, self.lanes = shape
         self.by_lane = by_lane
@@ -1347,8 +1355,8 @@
                 others=pltpu.VMEM((3, rows // 4, lanes), BF16),
                 send=dma((3,)),
                 recv=dma((3,)),
-                all_send=dma((2, dp)),
-                all_recv=dma((dp,)),
+                all_send=dma((2, 2 * dp if self.x_early else dp)),
+                all_recv=dma((2 * dp if self.x_early else dp,)),
                 out_sem=dma((len(self.cuts),)),
             )
             for i, cut in enumerate(self.cuts):
@@ -1418,13 +1426,24 @@
             up,
         )
 
-    def z_all(self, j, step):
+    def z_all(self, j, step, which=0):
+        ref = self.others.at[0] if which else self.whole
+        place = j + self.dp * which
         return self.copy(
-            self.chunk(self.whole, j),
-            self.chunk(self.whole, j),
-            self.all_send.at[0 if step > 0 else 1, j],
-            self.all_recv.at[j],
+            self.chunk(ref, j),
+            self.chunk(ref, j),
+            self.all_send.at[0 if step > 0 else 1, place],
+            self.all_recv.at[place],
             {"dp": self.z + step},
+        )
+
+    def x_chunk(self):
+        return self.copy(
+            self.chunk(self.whole, self.z),
+            self.chunk(self.others.at[0], self.z),
+            self.send.at[0],
+            self.recv.at[0],
+            self.to_x,
         )
 
     def spread(self, which):
@@ -1489,25 +1508,25 @@
             self.to_x,
         ).wait_recv()
 
-    def all_hop(self, h):
+    def all_hop(self, h, which=0):
         z, last = self.z, self.dp - 1
         low, high = jnp.maximum(z - h, 0), jnp.minimum(z + h, last)
 
         @pl.when(z >= h)
         def _():
-            self.z_all(low, 1).wait_recv()
+            self.z_all(low, 1, which).wait_recv()
 
         @pl.when((z >= h) & (z < last))
         def _():
-            self.z_all(low, 1).start()
+            self.z_all(low, 1, which).start()
 
         @pl.when(z <= last - h)
         def _():
-            self.z_all(high, -1).wait_recv()
+            self.z_all(high, -1, which).wait_recv()
 
         @pl.when((z <= last - h) & (z > 0))
         def _():
-            self.z_all(high, -1).start()
+            self.z_all(high, -1, which).start()
 
     def stages(self):
         def start():
@@ -1553,18 +1572,34 @@
 
         def place():
             self.chunk(self.whole, self.z)[...] = self.part[...]
+            if self.x_early:
+                self.x_chunk().start()
             gather()
 
-        def gather():
+        def gather(which=0):
             z, last = self.z, self.dp - 1
 
             @pl.when(z < last)
             def _():
-                self.z_all(z, 1).start()
+                self.z_all(z, 1, which).start()
 
             @pl.when(z > 0)
             def _():
-                self.z_all(z, -1).start()
+                self.z_all(z, -1, which).start()
+
+        def gather_other():
+            self.x_chunk().wait_recv()
+            gather(1)
+
+        def share_both():
+            self.all_hop(self.dp - 1)
+            self.spread(1).start()
+            self.emit(0, self.whole)
+
+        def pass_both():
+            self.all_hop(self.dp - 1, 1)
+            self.spread(2).start()
+            self.emit(1, self.others.at[0])
 
         def share():
             self.all_hop(self.dp - 1)
@@ -1586,6 +1621,13 @@
         sums = [functools.partial(self.hop, h) for h in range(1, self.dp - 1)] + [settle]
         gathers = [functools.partial(self.all_hop, h) for h in range(1, self.dp - 1)]
         gathers += [share, pass_on, last]
+        if self.x_early:
+            hops = [
+                [functools.partial(self.all_hop, h, which) for which in range(2)]
+                for h in range(1, self.dp - 1)
+            ]
+            both = [call for pair in hops for call in pair]
+            return [place, gather_other] + both + [share_both, pass_both, last]
         return {
             "all": [start, fold_core, fold_x] + sums + gathers,
             "sum": [begin] + sums,
@@ -1612,15 +1654,19 @@
             return
         for j in range(self.dp):
 
-            @pl.when((z >= j) & (z < last))
-            def _():
-                self.z_all(j, 1).wait_send()
-
-            @pl.when((z <= j) & (z > 0))
-            def _():
-                self.z_all(j, -1).wait_send()
-
-        for which in range(3):
+            for which in range(2 if self.x_early else 1):
+
+                @pl.when((z >= j) & (z < last))
+                def _():
+                    self.z_all(j, 1, which).wait_send()
+
+                @pl.when((z <= j) & (z > 0))
+                def _():
+                    self.z_all(j, -1, which).wait_send()
+
+        if self.x_early:
+            self.x_chunk().wait_send()
+        for which in range(1 if self.x_early else 0, 3):
             self.spread(which).wait_send()
         for copy in self.writes(3):
             copy.wait()
@@ -2000,7 +2046,10 @@
     dp = lax.axis_size("dp")
     items = [Reduction(part.shape) for part in parts[:-1]]
     items.append(Reduction(parts[-1].shape, base=parts[-2].shape[0]))
-    items += [Reduction(shape, by_lane, "gather") for shape, by_lane in zip(shapes, by_lanes)]
+    items += [
+        Reduction(shape, by_lane, "gather", x_early=i == 0)
+        for i, (shape, by_lane) in enumerate(zip(shapes, by_lanes))
+    ]
     small = SmallSum(gains.shape)
     scratch, outs = small.scratch(dp), []
     for item in items:
@@ -2176,10 +2225,10 @@
         tn(hidden, mixed_low),
         tn(attended_all, attention_low),
     )
-    shapes = [gate_weight.shape, down_weight.shape, up_weight.shape, output_weight.shape]
+    shapes = [gate_weight.shape, up_weight.shape, down_weight.shape, output_weight.shape]
 
     table_cosine, table_sine = angle_tables(jnp.arange((TRUNK + 2) * SEG))
-    by_lanes = [False, True, False, False]
+    by_lanes = [False, False, True, False]
     sent, *sums = attention_backward(
         parts, pick(role, upstream), attended, logsum, table_cosine, table_sine, grads, shapes
     )
@@ -2211,8 +2260,8 @@
         value_total,
         adapter_total,
         gate_total,
+        up_total,
         down_total,
-        up_total,
         output_total,
         gains,
     ) = reduce_all(

time: 659 us -> 654 us (level)
  no operation moved by 1% of the time
where the time goes in v6:
time: 654 us; the launch traced here: 647 us
  Pallas kernels  546 us (83%)
  matrix products  36.5 us (6%)
  local copies, waits for them, and re-layouts  25.9 us (4%)
  other arithmetic  20.9 us (3%)
  starting transfers between devices  9.77 us (1%)
  waiting for transfers between devices  6.74 us (1%)
    pallas_call x1, Pallas kernels, reduce_all(): pl.pallas_call(functools.partial(reduce_kernel, items, small), out_shape=...  130 us
    pallas_call x1, Pallas kernels, attention_backward(): pl.pallas_call(functools.partial(attention_back_kernel, folds), out_shape...  101 us
    pallas_call x1, Pallas kernels, leave(): pl.pallas_call(functools.partial(leave_kernel, items), out_shape=(jax.Sha...  78.4 us
    pallas_call x1, Pallas kernels, enter(): pl.pallas_call(enter_kernel, out_shape=(jax.ShapeDtypeStruct((peers, rows...  78.2 us
    pallas_call x1, Pallas kernels, attention_forward(): pl.pallas_call(functools.partial(attention_kernel, fetches), out_shape=(j...  74.7 us
    pallas_call x1, Pallas kernels, middle_section(): pl.pallas_call(middle_kernel, grid_spec=pltpu.PrefetchScalarGridSpec(num_...  61.7 us
    dot_general x3, matrix products, tn(): lax.dot_general(left, right, (((0,), (0,)), ((), ())), preferred_element_...  24.3 us
    unnamed x46, local copies, waits for them, and re-layouts  22.9 us
  transfers between devices with their start and end apart: 3, of which 1 were waited for; matrix products, arithmetic and copies ran while one was open for 7% of the time, Pallas kernels for 50%

profile of v6, /device:TPU:0, one launch (start us, length us, event | category | flops | bytes accessed | tf_op | source)
XLA Modules:
  0.0 646.5 jit_solution(11869177026301184777)
XLA Ops:
  1.4 6.8 %bitcast_convert_fusion.mine = bf16[1280,1024]{1,0:T(8,128)(2,1)} fusion(bf16[2,512,1024]{2,1,0:T(8,128)(2,1)} %weight.1, bf16[1280,2,512]{2,1,0:T(2,128)(2,1)} %param.16), kind=kOutput, calls=%fused_computation.2 | convolution fusion | flops 2685665280 | bytes 7340032 | tf_op jit(solution)/shard_map/rcd,cde->re/dot_general | solution.py:2178
  8.1 3.7 fusion.9
  11.8 78.2 %enter.1 = (bf16[4,1280,384]{2,1,0:T(8,128)(2,1)}, bf16[1280,1024]{1,0:T(8,128)(2,1)}, bf16[1280,1024]{1,0:T(8,128)(2,1)}) custom-call(bf16[1280,1024]{1,0:T(8,128)(2,1)} %bitcast_convert_fusion.mine, f32[1,1024]{1,0:T(1,128)} %bitcast.61, bf16[1024,512]{1,0:T(8,128)(2,1)} %refs_5_.1, bf16[1024,512]{1,0:T(8,128)(2,1)} %refs_6_.1, bf16[1024,512]{1,0:T(8,128)(2,1)} %refs_7_.1, ...), custom_call_target="tpu_custom_call" | custom-call | flops 4026531840 | bytes 209715200 | tf_op jit(solution)/shard_map/enter/pallas_call | solution.py:1070
  90.0 4.5 sort_parts.1
  94.5 74.7 %attention_forward.1 = (bf16[5120,128]{1,0:T(8,128)(2,1)}, f32[5120,128]{1,0:T(8,128)}, bf16[512,1024]{1,0:T(8,128)(2,1)}, bf16[1024,1408]{1,0:T(8,128)(2,1)}, b...) custom-call(bf16[5120,384]{1,0:T(8,128)(2,1)} %get-tuple-element.62.refs_0_, bf16[512,1024]{1,0:T(8,128)(2,1)} %wo_own.1, ...), custom_call_target="tpu_custom_call" | custom-call | flops 10200547328 | bytes 7864320 | tf_op jit(solution)/shard_map/attention_forward/pallas_call | solution.py:592
  171.7 3.8 all-to-all-start
  176.1 3.7 convert_add_fusion.adapted.refs_1_
  179.8 6.2 fusion.8
  186.0 6.7 %all-to-all-done.heads = bf16[8,640,128]{2,1,0:T(8,128)(2,1)S(1)} async-done(((bf16[8,640,128]{2,1,0:T(8,128)(2,1)}), bf16[8,640,128]{2,1,0:T(8,128)(2,1)S(1)}, u32[]{:S(2)}, u32[]{:S(2)}) %all-to-all-start) | async-done | bytes 1310752 | tf_op jit(solution)/shard_map/all_to_all | solution.py:2190
  193.8 61.7 %middle_section.1 = (bf16[640,1024]{1,0:T(8,128)(2,1)}, f32[640,1024]{1,0:T(8,128)}, bf16[640,1024]{1,0:T(8,128)(2,1)}, bf16[640,1024]{1,0:T(8,128)(2,1)}, bf16[...) custom-call(s32[2]{0:T(128)} %pad_add_fusion.meta, ...), custom_call_target="tpu_custom_call" | custom-call | flops 24830279680 | bytes 43319296 | tf_op jit(solution)/shard_map/middle_section/pallas_call | solution.py:1258
  255.5 4.0 all-to-all-start.1
  261.6 14.6 %convolution_convert_fusion.refs_6_ = bf16[1024,5632]{1,0:T(8,128)(2,1)} fusion(bf16[640,1024]{1,0:T(8,128)(2,1)} %get-tuple-element.72, bf16[640,5632]{1,0:T(8,128)(2,1)} %get-tuple-element.73), kind=kOutput, calls=%fused_computation | convolution fusion | flops 7387742208 | bytes 20054016 | tf_op jit(solution)/shard_map/dot_general | solution.py:2144
  276.2 3.2 convolution_convert_fusion.2.refs_8_
  279.4 6.5 %convolution_convert_fusion.1.refs_7_ = bf16[2816,1024]{1,0:T(8,128)(2,1)} fusion(bf16[640,2816]{1,0:T(8,128)(2,1)S(1)} %copy-done.11, bf16[640,1024]{1,0:T(8,128)(2,1)S(1)} %copy-done.12), kind=kOutput, calls=%fused_computation.1 | convolution fusion | flops 3693871104 | bytes 10682368 | tf_op jit(solution)/shard_map/dot_general | solution.py:2144
  289.5 101.3 %attention_backward.1 = (bf16[5120,384]{1,0:T(8,128)(2,1)}, bf16[256,1408]{1,0:T(8,128)(2,1)}, bf16[256,1408]{1,0:T(8,128)(2,1)}, bf16[352,1024]{1,0:T(8,128)(2,1)}, bf16[128,1024]{1,0:T(8,128)(2,1)}) custom-call(bf16[5120,384]{1,0:T(8,128)(2,1)} %get-tuple-element.62.refs_0_, bf16[5120,128]{1,0:T(8,128)(2,1)} %pick.4.refs_1_, ...), custom_call_target="tpu_custom_call" | custom-call | flops 25501368320 | bytes 15728640 | tf_op jit(solution)/shard_map/attention_backward/pallas_call | solution.py:931
  390.8 4.4 pick.5
  395.2 78.4 %leave.1 = (bf16[1024,512]{1,0:T(8,128)(2,1)}, bf16[1024,512]{1,0:T(8,128)(2,1)}, bf16[1024,512]{1,0:T(8,128)(2,1)}, bf16[1280,1024]{1,0:T(8,128)(2,1)}, f32[8,1...) custom-call(bf16[4,1280,384]{2,1,0:T(8,128)(2,1)} %bitcast.51, ...), custom_call_target="tpu_custom_call" | custom-call | flops 8053063680 | bytes 209715200 | tf_op jit(solution)/shard_map/leave/pallas_call | solution.py:1864
  475.0 5.5 convert_bitcast_fusion
  481.9 129.6 %reduce_all.1 = (f32[1024,512]{1,0:T(8,128)}, f32[1024,512]{1,0:T(8,128)}, f32[1024,512]{1,0:T(8,128)}, f32[1024,1024]{1,0:T(8,128)}, f32[1024,1408]{1,0:T(8,128...) custom-call(bf16[1024,512]{1,0:T(8,128)(2,1)} %get-tuple-element.86.refs_0_, ...), custom_call_target="tpu_custom_call" | custom-call | flops 29884416 | bytes 224133120 | tf_op jit(solution)/shard_map/reduce_all/pallas_call | solution.py:2061
  613.1 7.9 %latent_grad.1 = f32[10240,128]{1,0:T(8,128)} custom-call(bf16[1280,1024]{1,0:T(8,128)(2,1)} %get-tuple-element.85.low, bf16[2,512,1024]{2,1,0:T(8,128)(2,1)} %weight.1), custom_call_target="tpu_custom_call" | custom-call | flops 2684354560 | bytes 9961472 | tf_op jit(solution)/shard_map/latent_grad/pallas_call | solution.py:2094
  622.5 3.1 maximum_convert_fusion
  636.9 2.9 copy.54
  639.9 2.9 copy.55
  643.8 2.5 copy.56
  (60 shorter events, 28.7 us)
Async XLA Ops:
  171.7 21.1 %all-to-all-start = ((bf16[8,640,128]{2,1,0:T(8,128)(2,1)}), bf16[8,640,128]{2,1,0:T(8,128)(2,1)S(1)}, u32[]{:S(2)}, u32[]{:S(2)}) async-start(bf16[8,640,128]{2,1,0:T(8,128)(2,1)} %bitcast.48), calls=%async_computation | async-start | bytes 2621440 | tf_op jit(solution)/shard_map/all_to_all | solution.py:2190
  192.8 1.1 copy-start.6
  255.5 4.0 copy-start.8
  255.5 4.0 copy-start.7
  255.5 30.4 %all-to-all-start.1 = ((bf16[8,640,128]{2,1,0:T(8,128)(2,1)}), bf16[8,640,128]{2,1,0:T(8,128)(2,1)S(1)}, u32[]{:S(2)}, u32[]{:S(2)}) async-start(bf16[8,640,128]{2,1,0:T(8,128)(2,1)} %get-tuple-element.70), calls=%async_computation.1 | async-start | bytes 2621440 | tf_op jit(solution)/shard_map/all_to_all | solution.py:2212
  259.5 361.4 %collective-permute-start = (bf16[640,1024]{1,0:T(8,128)(2,1)S(1)}, bf16[640,1024]{1,0:T(8,128)(2,1)}, u32[]{:S(2)}, u32[]{:S(2)}) collective-permute-start(bf16[640,1024]{1,0:T(8,128)(2,1)S(1)} %copy-done.7), channel_id=1, source_target_pairs={{0,1},{1,0},{2,3},{3,2},{4,5},{5,4},{6,7},{7,6},{8,9},{9,8},{10,11... | collective-permute-start | bytes 3932168 | tf_op jit(solution)/shard_map/ppermute | solution.py:2116
  261.6 14.6 %copy-start.9 = (bf16[640,1024]{1,0:T(8,128)(2,1)S(1)}, bf16[640,1024]{1,0:T(8,128)(2,1)}, u32[]{:S(2)}) copy-start(bf16[640,1024]{1,0:T(8,128)(2,1)} %get-tuple-element.76) | copy-start | bytes 3932164
  261.6 14.6 %copy-start.10 = (bf16[640,1024]{1,0:T(8,128)(2,1)S(1)}, bf16[640,1024]{1,0:T(8,128)(2,1)}, u32[]{:S(2)}) copy-start(bf16[640,1024]{1,0:T(8,128)(2,1)} %get-tuple-element.77) | copy-start | bytes 3932164
  276.2 3.2 copy-start.11
  276.2 3.2 copy-start.12
  285.9 1.1 copy-start
  622.5 3.7 copy-start.1
  626.1 3.1 copy-start.5
  626.1 4.4 copy-start.4
  626.1 5.7 copy-start.3
  629.2 7.1 %slice-start.4 = ((s8[5767168]{0:T(1024)(128)(4,1)}), s8[4194304]{0:T(1024)(128)(4,1)S(1)}, s32[]{:S(2)}) async-start(s8[5767168]{0:T(1024)(128)(4,1)} %bitcast.45), calls=%async_computation.6 | async-start | bytes 8388608
  630.6 9.3 %slice-start.2 = ((s8[5767168]{0:T(1024)(128)(4,1)}), s8[4194304]{0:T(1024)(128)(4,1)S(1)}, s32[]{:S(2)}) async-start(s8[5767168]{0:T(1024)(128)(4,1)} %bitcast.43), calls=%async_computation.4 | async-start | bytes 8388608
  631.9 3.1 copy-start.2
  631.9 5.0 slice-start.5
  635.0 4.8 slice-start.3
  636.9 5.8 slice-start
  639.9 4.0 slice-start.1
